TPU v7x, 32 devices: a whole 2x2x4 slice. The times are simulated.
32 devices in a mesh: dp: 8 (over z, y), row: 2 (over core), col: 2 (over x).
Axes of the slice: x: 2, y: 2, z: 4, core: 2. Of those that a mesh axis runs over, the one named last changes fastest.
Arguments:
- hidden: bfloat16 [16384, 768], P('dp', 'row'), may hold values from -6 to 6
- gate_proj: bfloat16 [768, 1536], P('row', 'col'), may hold values from -0.21875 to 0.21875
- value_proj: bfloat16 [768, 1536], P('row', 'col'), may hold values from -0.21875 to 0.21875
- step_proj: bfloat16 [768, 24], P('row', 'col'), may hold values from -0.21875 to 0.21875
- state_proj: bfloat16 [768, 256], P('row'), may hold values from -0.21875 to 0.21875
- value_filter: float32 [4, 1536], P(None, ('col', 'row')), may hold values from -3 to 3
- value_shift: float32 [1536], P(('col', 'row')), may hold values from -0.5 to 0.5
- shared_kernel: float32 [4, 256], replicated, may hold values from -3 to 3
- shared_offset: float32 [256], replicated, may hold values from -0.5 to 0.5
- decay_log: float32 [24], P(('col', 'row')), may hold values from 0 to 2.77
- step_bias: float32 [24], P(('col', 'row')), may hold values from -6.9 to -2.3
- skip_gain: float32 [24], P(('col', 'row')), may hold values from 0.5 to 1.5
- input_gain: float32 [768], P('row'), may hold values from 0.5 to 1.5
- gated_gain: bfloat16 [1536], P(('col', 'row')), may hold values from 0.5 to 1.5
- output_proj: bfloat16 [1536, 768], P('col', 'row'), may hold values from -0.15625 to 0.15625
- cotangent: bfloat16 [16384, 768], P('dp', 'row'), may hold values from -6 to 6
Outputs:
- result: bfloat16 [16384, 768], P('dp', 'row')
- hidden_grad: float32 [16384, 768], P('dp', 'row')
- gate_grad: float32 [768, 1536], P('row', 'col')
- value_grad: float32 [768, 1536], P('row', 'col')
- step_grad: float32 [768, 24], P('row', 'col')
- state_grad: float32 [768, 256], P('row')
- filter_grad: float32 [4, 1536], P(None, ('col', 'row'))
- shift_grad: float32 [1536], P(('col', 'row'))
- kernel_grad: float32 [4, 256], replicated
- offset_grad: float32 [256], replicated
- decay_grad: float32 [24], P(('col', 'row'))
- bias_grad: float32 [24], P(('col', 'row'))
- skip_grad: float32 [24], P(('col', 'row'))
- norm_grad: float32 [768], P('row')
- gated_grad: float32 [1536], P(('col', 'row'))
- output_grad: float32 [1536, 768], P('col', 'row')
All inputs are finite; a program needn't handle non-finite values.
Results may differ from a plain program's by a relative error of at most 0.012.
Values may be sent and summed in bfloat16 or wider, within the bound.
A program may use at most 320 MiB of HBM per device.

v0:
```python
import functools

import jax
import jax.numpy as jnp
from jax import lax
from jax.sharding import PartitionSpec as P

D = 768
GROUP = 256
LEN = 2048


EPSILON = 1e-05
HIGHEST = lax.Precision.HIGHEST


def from_everyone(shard, axis):
    size = lax.axis_size(axis)
    return lax.all_to_all(
        jnp.broadcast_to(shard[None], (size, *shard.shape)), axis, 0, 0, tiled=True
    )


def over_copies(shard, axis):
    everything = from_everyone(shard, axis)
    return jnp.sum(everything.astype(jnp.float32), axis=0)


def causal_filter(signal, kernel, offset, seq_count):
    channels = signal.shape[-1]
    taps = kernel.shape[0]
    seq_view = signal.reshape(seq_count, -1, channels)
    length = seq_view.shape[1]
    padded = jnp.pad(seq_view, ((0, 0), (taps - 1, 0), (0, 0)))
    total = jnp.zeros_like(seq_view) + offset
    for position in range(taps):
        total = total + padded[:, position : position + length] * kernel[position]
    return jax.nn.silu(total).reshape(signal.shape)


def state_scan(values, inputs_b, reads_c, steps, logdecay, block_len):
    seq_count, length, heads, channels = values.shape
    width = inputs_b.shape[-1]
    blocks = length // block_len

    def split(array):
        shaped = array.reshape((seq_count, blocks, block_len) + array.shape[2:])
        return jnp.moveaxis(shaped, 1, 0)

    positions = jnp.arange(block_len)
    lower = (positions[:, None] >= positions[None, :])[None, :, :, None]

    def advance(carried, pieces):
        vals, b_in, c_in, step_in, log_in = pieces
        cumul = jnp.cumsum(log_in, axis=1)
        gaps = cumul[:, :, None, :] - cumul[:, None, :, :]
        decays = jnp.where(lower, jnp.exp(jnp.where(lower, gaps, 0.0)), 0.0)
        scores = jnp.einsum("sqn,skn->sqk", c_in, b_in, precision=HIGHEST)
        weights = scores[..., None] * decays * step_in[:, None, :, :]
        inside = jnp.einsum("sqkh,skhp->sqhp", weights, vals, precision=HIGHEST)
        carried_out = jnp.einsum("sqn,shpn->sqhp", c_in, carried, precision=HIGHEST)
        outputs = inside + carried_out * jnp.exp(cumul)[..., None]
        final = cumul[:, -1, :]
        tails = jnp.exp(final[:, None, :] - cumul) * step_in
        fresh = jnp.einsum("skh,skhp,skn->shpn", tails, vals, b_in, precision=HIGHEST)
        carried = carried * jnp.exp(final)[:, :, None, None] + fresh
        return (carried, outputs)

    start = jnp.zeros((seq_count, heads, channels, width), jnp.float32)
    _, outputs = lax.scan(
        advance,
        start,
        (split(values), split(inputs_b), split(reads_c), split(steps), split(logdecay)),
    )
    return jnp.moveaxis(outputs, 0, 1).reshape(seq_count, length, heads, channels)


def mixer_core(
    pre_value,
    pre_shared,
    pre_step,
    pre_gate,
    value_filter,
    value_shift,
    shared_kernel,
    shared_offset,
    decay_log,
    step_bias,
    skip_gain,
    seq_count,
    block_len,
):
    heads = pre_step.shape[1]
    channels = pre_value.shape[1] // heads
    width = pre_shared.shape[1] // 2
    token_count = pre_value.shape[0]
    filtered = causal_filter(pre_value, value_filter, value_shift, seq_count)
    shared = causal_filter(pre_shared, shared_kernel, shared_offset, seq_count)
    steps = jax.nn.softplus(pre_step + step_bias)
    logdecay = -jnp.exp(decay_log) * steps
    values = filtered.reshape(seq_count, -1, heads, channels)
    inputs_b = shared[:, :width].reshape(seq_count, -1, width)
    reads_c = shared[:, width:].reshape(seq_count, -1, width)
    outputs = state_scan(
        values,
        inputs_b,
        reads_c,
        steps.reshape(seq_count, -1, heads),
        logdecay.reshape(seq_count, -1, heads),
        block_len,
    )
    outputs = outputs + skip_gain[:, None] * values
    return outputs.reshape(token_count, heads * channels) * jax.nn.silu(pre_gate)


def body(
    hidden,
    gate_proj,
    value_proj,
    step_proj,
    state_proj,
    value_filter,
    value_shift,
    shared_kernel,
    shared_offset,
    decay_log,
    step_bias,
    skip_gain,
    input_gain,
    gated_gain,
    output_proj,
    cotangent,
):
    token_count = hidden.shape[0]
    seq_count = token_count // LEN
    row_count = lax.axis_size("row")
    inner_width = gated_gain.shape[0] * row_count * lax.axis_size("col")
    hidden32 = hidden.astype(jnp.float32)
    normed = (hidden32 * input_gain).astype(jnp.bfloat16)
    square_part = jnp.sum(hidden32 * hidden32, axis=1)
    gate_part = jnp.dot(normed, gate_proj, preferred_element_type=jnp.float32)
    value_part = jnp.dot(normed, value_proj, preferred_element_type=jnp.float32)
    step_part = jnp.dot(normed, step_proj, preferred_element_type=jnp.float32)
    shared_part = jnp.dot(normed, state_proj, preferred_element_type=jnp.float32)
    q_gate, q_value, q_step = (
        lax.psum_scatter(gate_part, "row", scatter_dimension=1, tiled=True),
        lax.psum_scatter(value_part, "row", scatter_dimension=1, tiled=True),
        lax.psum_scatter(step_part, "row", scatter_dimension=1, tiled=True),
    )
    q_shared, square_sum = lax.psum((shared_part, square_part), "row")
    recip = lax.rsqrt(square_sum / D + EPSILON)[:, None]
    local_mixer = functools.partial(mixer_core, seq_count=seq_count, block_len=GROUP)
    mixed32, pullback = jax.vjp(
        local_mixer,
        recip * q_value,
        recip * q_shared,
        recip * q_step,
        recip * q_gate,
        value_filter,
        value_shift,
        shared_kernel,
        shared_offset,
        decay_log,
        step_bias,
        skip_gain,
    )
    mixed = mixed32.astype(jnp.bfloat16)
    mixed_rows, gain_rows = (
        lax.all_gather(mixed, "row", axis=1, tiled=True),
        lax.all_gather(gated_gain.reshape(1, -1), "row", axis=1, tiled=True),
    )
    mixed_block = mixed_rows.astype(jnp.float32)
    square_block = jnp.sum(mixed_block * mixed_block, axis=1)
    weighted = (mixed_block * gain_rows.astype(jnp.float32)).astype(jnp.bfloat16)
    proj_part = jnp.dot(weighted, output_proj, preferred_element_type=jnp.float32)
    proj, square_inner = lax.psum((proj_part, square_block), "col")
    scale = lax.rsqrt(square_inner / inner_width + EPSILON)[:, None]
    result = (hidden32 + scale * proj).astype(jnp.bfloat16)
    cot = cotangent.astype(jnp.float32)
    scale_dot = lax.psum(jnp.sum(cot * proj, axis=1), "row")[:, None]
    scaled_cot = (scale * cot).astype(jnp.bfloat16)
    g_output = jnp.dot(weighted.T, scaled_cot, preferred_element_type=jnp.float32)
    weighted_part = jnp.dot(scaled_cot, output_proj.T, preferred_element_type=jnp.float32)
    d_weighted = lax.psum_scatter(weighted_part, "row", scatter_dimension=1, tiled=True)
    mixed_own = mixed.astype(jnp.float32)
    g_gated = jnp.sum(d_weighted * mixed_own, axis=0)
    d_mixed = (
        d_weighted * gated_gain.astype(jnp.float32) - scale_dot * scale**3 * mixed_own / inner_width
    )
    pulled = pullback(d_mixed)
    d_value, d_shared_part, d_step, d_gate = (pulled[0], pulled[1], pulled[2], pulled[3])
    head_recip = (
        jnp.sum(d_gate * q_gate, axis=1)
        + jnp.sum(d_value * q_value, axis=1)
        + jnp.sum(d_step * q_step, axis=1)
    )
    d_shared, recip_sum, g_kernel, g_offset = lax.psum(
        (d_shared_part, head_recip, pulled[6], pulled[7]), ("row", "col")
    )
    d_recip = (recip_sum + jnp.sum(d_shared * q_shared, axis=1))[:, None]
    p_gate = (recip * d_gate).astype(jnp.bfloat16)
    p_value = (recip * d_value).astype(jnp.bfloat16)
    p_step = (recip * d_step).astype(jnp.bfloat16)
    p_shared = (recip * d_shared).astype(jnp.bfloat16)
    gate_rows, value_rows, step_rows = (
        lax.all_gather(p_gate, "row", axis=1, tiled=True),
        lax.all_gather(p_value, "row", axis=1, tiled=True),
        lax.all_gather(p_step, "row", axis=1, tiled=True),
    )
    g_gate = jnp.dot(normed.T, gate_rows, preferred_element_type=jnp.float32)
    g_value = jnp.dot(normed.T, value_rows, preferred_element_type=jnp.float32)
    g_step = jnp.dot(normed.T, step_rows, preferred_element_type=jnp.float32)
    g_state = jnp.dot(normed.T, p_shared, preferred_element_type=jnp.float32)
    normed_part = jnp.dot(gate_rows, gate_proj.T, preferred_element_type=jnp.float32)
    normed_part = normed_part + jnp.dot(
        value_rows, value_proj.T, preferred_element_type=jnp.float32
    )
    normed_part = normed_part + jnp.dot(step_rows, step_proj.T, preferred_element_type=jnp.float32)
    d_normed = over_copies(normed_part.astype(jnp.bfloat16), "col").astype(jnp.float32)
    d_normed = d_normed + jnp.dot(p_shared, state_proj.T, preferred_element_type=jnp.float32)
    hidden_grad = cot + d_normed * input_gain - d_recip * recip**3 * hidden32 / D
    g_norm = jnp.sum(d_normed * hidden32, axis=0)
    reduced = lax.psum(
        (
            g_gate,
            g_value,
            g_step,
            g_state,
            pulled[4],
            pulled[5],
            g_kernel,
            g_offset,
            pulled[8],
            pulled[9],
            pulled[10],
            g_norm,
            g_gated,
            g_output,
        ),
        "dp",
    )
    return (result, hidden_grad) + tuple(reduced)


def solution(mesh):
    in_specs = (
        P("dp", "row"),
        P("row", "col"),
        P("row", "col"),
        P("row", "col"),
        P("row", None),
        P(None, ("col", "row")),
        P(("col", "row")),
        P(),
        P(),
        P(("col", "row")),
        P(("col", "row")),
        P(("col", "row")),
        P("row"),
        P(("col", "row")),
        P("col", "row"),
        P("dp", "row"),
    )
    out_specs = (
        P("dp", "row"),
        P("dp", "row"),
        P("row", "col"),
        P("row", "col"),
        P("row", "col"),
        P("row", None),
        P(None, ("col", "row")),
        P(("col", "row")),
        P(),
        P(),
        P(("col", "row")),
        P(("col", "row")),
        P(("col", "row")),
        P("row"),
        P(("col", "row")),
        P("col", "row"),
    )
    return jax.shard_map(body, mesh=mesh, in_specs=in_specs, out_specs=out_specs, check_vma=False)
```

profile of v0, /device:TPU:0, one launch (start us, length us, event | category | flops | bytes accessed | tf_op | source)
XLA Modules:
  0.0 1108.9 jit_solution(1876727664826304818)
XLA Ops:
  41.1 11.3 %reduce-scatter.6.cloned.1.call-done = f32[2048,384]{1,0:T(8,128)} async-done(((f32[2048,768]{1,0:T(8,128)}), f32[2048,384]{1,0:T(8,128)}) %reduce-scatter.6.cloned.1.call-update) | async-done | bytes 3145744 | tf_op jit(solution)/shard_map/reduce_scatter | solution.py:147
  70.9 247.3 %while.73 = (s32[]{:T(128)}, f32[1,6,64,128]{3,2,1,0:T(8,128)S(1)}, f32[8,1,256,6,64]{2,0,4,3,1:T(8,128)}, f32[8,1,256,256,6]{3,2,4,1,0:T(8,128)}, f32[8,1,256,2...) while((s32[]{:T(128)}, f32[1,6,64,128]{3,2,1,0:T(8,128)S(1)}, ...), condition=%wide.region_8.9_spmd.clone.clone, body=%wide.region_5.8_spmd.clone.clone.sunk | while | flops 709413888 | bytes 13977169 | solution.py:70
  84.2 9.8 dynamic_update_slice.236
  115.0 9.8 dynamic_update_slice.236
  145.9 9.8 dynamic_update_slice.236
  176.7 9.8 dynamic_update_slice.236
  207.6 9.8 dynamic_update_slice.236
  238.6 9.8 dynamic_update_slice.236
  269.6 9.8 dynamic_update_slice.236
  334.1 11.5 %all-gather.7.cloned.1.call-done = bf16[2048,768]{1,0:T(8,128)(2,1)} async-done(((bf16[2048,384]{1,0:T(8,128)(2,1)}), bf16[2048,768]{1,0:T(8,128)(2,1)}) %all-gather.7.cloned.1.call-update) | async-done | bytes 3145744 | tf_op jit(solution)/shard_map/all_gather | solution.py:169
  364.6 73.5 %all-reduce.33.cloned.1.call-done = f32[2048,384]{1,0:T(8,128)} async-done(((f32[2048,384]{1,0:T(8,128)}), f32[2048,384]{1,0:T(8,128)}) %all-reduce.33.cloned.1.call-update) | async-done | bytes 3145744 | tf_op jit(solution)/shard_map/psum | solution.py:176
  475.8 353.1 %while.74 = (s32[]{:T(128)}, f32[1,6,64,128]{3,2,1,0:T(8,128)S(1)}, f32[8,1,256,6,64]{2,0,4,3,1:T(8,128)}, f32[8,1,256,128]{3,2,1,0:T(8,128)}, f32[8,1,256,128]{...) while((s32[]{:T(128)}, f32[1,6,64,128]{3,2,1,0:T(8,128)S(1)}, ...), condition=%wide.region_26.27_spmd.clone.clone, body=%wide.region_16.26_spmd.clone.clone.sunk | while | flops 1415001600 | bytes 18002120 | solution.py:70
  499.6 9.8 dynamic_update_slice.245
  543.7 9.8 dynamic_update_slice.245
  587.8 9.8 dynamic_update_slice.245
  720.2 9.8 dynamic_update_slice.245
  764.3 9.8 dynamic_update_slice.245
  808.4 9.8 dynamic_update_slice.245
  873.7 37.3 %all-reduce.35.cloned.1.call-done = f32[2048,256]{1,0:T(8,128)} async-done(((f32[2048,256]{1,0:T(8,128)}), f32[2048,256]{1,0:T(8,128)}) %all-reduce.35.cloned.1.call-update) | async-done | bytes 2097168 | tf_op jit(solution)/shard_map/psum | solution.py:197
  914.3 11.0 all-gather.11.cloned.1.call-done
  929.6 10.5 all-gather.9.cloned.1.call-done
  960.7 43.3 %all-reduce.25 = (f32[2048]{0:T(1024)S(1)}, f32[4,256]{1,0:T(4,128)S(1)}, f32[256]{0:T(256)S(1)}) all-reduce(f32[2048]{0:T(1024)S(1)} %add_add_fusion, f32[4,256]{1,0:T(4,128)S(1)} %pad_add_fusion.7, f32[256]{0:T(256)S(1)} %get-tuple-element.1537), channel_id=1, replica_groups=mesh['dp'=8,'row'=2,'col'=2] {'row','col'}, use_global_device_ids=true, to_apply=%region_32.33 | all-reduce | flops 3328 | bytes 26624 | tf_op jit(solution)/shard_map/psum | solution.py:197
  1012.9 38.8 %all-reduce.23 = (f32[384,12]{0,1:T(8,128)}, f32[4,384]{1,0:T(4,128)}, f32[384]{0:T(512)}, f32[4,256]{1,0:T(4,128)}, f32[256]{0:T(256)}, /*index=5*/f32[6]{0:T(1...) all-reduce(f32[384,12]{0,1:T(8,128)S(1)} %fusion.177, ...), channel_id=1, replica_groups=mesh['dp'=8,'row'=2,'col'=2] {'dp'}, use_global_device_ids=true, to_apply=%region_36.37 | all-reduce | flops 8594 | bytes 68752 | tf_op jit(solution)/shard_map/psum | solution.py:223
  1051.7 44.6 %all-reduce.37.cloned.1.call-done = (f32[384,768]{1,0:T(8,128)}, f32[384,768]{1,0:T(8,128)}, f32[384,256]{1,0:T(8,128)}, f32[768,384]{1,0:T(8,128)}) async-done(((f32[384,768]{1,0:T(8,128)}, f32[384,768]{1,0:T(8,128)}, f32[384,256]{1,0:T(8,128)}, f32[768,384]{1,0:T(8,128)}), (f32[384,768]{1,0:T(8,128)}, f32[384,768]{1,0:T(8,128)}, f32[384,256]{1,0:T(8,128)}, ...) | async-done | bytes 3932176 | tf_op jit(solution)/shard_map/psum | solution.py:223
  (748 shorter events, 681.0 us)
Async XLA Ops:
  7.2 338.4 %copy-start = (bf16[768,384]{1,0:T(8,128)(2,1)S(1)}, bf16[768,384]{1,0:T(8,128)(2,1)}, u32[]{:S(2)}) copy-start(bf16[768,384]{1,0:T(8,128)(2,1)} %param.34) | copy-start | bytes 1769476
  7.2 27.8 %all-reduce.31.cloned.1.call-start = ((), (), s32[]{:S(2)}) async-start(), calls=%async_computation.5 | async-start | bytes 4194304 | tf_op jit(solution)/shard_map/psum | solution.py:150
  10.9 41.5 %reduce-scatter.6.cloned.1.call-start = ((), (), s32[]{:S(2)}) async-start(), calls=%async_computation.4 | async-start | bytes 9437184 | tf_op jit(solution)/shard_map/reduce_scatter | solution.py:147
  15.4 6.6 copy-start.17
  15.4 311.2 %reduce-scatter.8.cloned.1.call-start = ((), (), s32[]{:S(2)}) async-start(), calls=%async_computation.6 | async-start | bytes 9437184 | tf_op jit(solution)/shard_map/reduce_scatter | solution.py:146
  19.9 11.4 %collective-permute-start = (f32[2048,2]{0,1:T(2,128)S(1)}, f32[2048,2]{0,1:T(2,128)S(1)}, u32[]{:S(2)}, u32[]{:S(2)}) collective-permute-start(f32[2048,2]{0,1:T(2,128)S(1)} %slice.117), channel_id=1, source_target_pairs={{0,2},{1,3},{4,6},{5,7},{8,10},{9,11},{12,14},{13,15},{16,18},{17,... | collective-permute-start | bytes 49160
  26.4 10.7 copy-start.38
  26.4 319.1 %all-gather.7.cloned.1.call-start = ((), (), s32[]{:S(2)}) async-start(), calls=%async_computation.7 | async-start | bytes 4718592 | tf_op jit(solution)/shard_map/all_gather | solution.py:169
  29.7 10.0 copy-start.24
  29.7 10.0 copy-start.35
  41.1 13.7 %copy-start.37 = (f32[384]{0:T(512)S(1)}, f32[384]{0:T(512)}, u32[]{:S(2)}) copy-start(f32[384]{0:T(512)} %param.26) | copy-start | bytes 4612
  332.1 106.0 %all-reduce.33.cloned.1.call-start = ((), (), s32[]{:S(2)}) async-start(), calls=%async_computation.8 | async-start | bytes 6291456 | tf_op jit(solution)/shard_map/psum | solution.py:176
  334.0 16.9 %copy-start.29 = (f32[768]{0:T(1024)}, f32[768]{0:T(1024)S(1)}, u32[]{:S(2)}) copy-start(f32[768]{0:T(1024)S(1)} %reshape.985) | copy-start | bytes 9220
  350.9 103.2 %reduce-scatter.10.cloned.1.call-start = ((), (), s32[]{:S(2)}) async-start(), calls=%async_computation.9 | async-start | bytes 9437184 | tf_op jit(solution)/shard_map/reduce_scatter | solution.py:184
  364.5 546.5 %all-reduce.35.cloned.1.call-start = ((), (), s32[]{:S(2)}) async-start(), calls=%async_computation.12 | async-start | bytes 4194304 | tf_op jit(solution)/shard_map/psum | solution.py:197
  847.1 6.2 copy-start.8
  847.1 6.2 copy-start.10
  847.1 6.7 copy-start.13
  858.2 67.1 %all-gather.11.cloned.1.call-start = ((), (), s32[]{:S(2)}) async-start(), calls=%async_computation.11 | async-start | bytes 4718592 | tf_op jit(solution)/shard_map/all_gather | solution.py:207
  858.3 6.9 copy-start.9
  867.3 72.8 %all-gather.9.cloned.1.call-start = ((), (), s32[]{:S(2)}) async-start(), calls=%async_computation.10 | async-start | bytes 4718592 | tf_op jit(solution)/shard_map/all_gather | solution.py:206
  868.1 228.2 %all-reduce.37.cloned.1.call-start = ((), (), s32[]{:S(2)}) async-start(), calls=%async_computation.13 | async-start | bytes 7864320 | tf_op jit(solution)/shard_map/psum | solution.py:223
  955.1 48.9 %copy-start.43 = (f32[6]{0:T(128)S(1)}, f32[6]{0:T(128)}, u32[]{:S(2)}) copy-start(f32[6]{0:T(128)} %param.29) | copy-start | bytes 76
  955.1 51.9 %all-to-all-start = ((bf16[2,2048,384]{2,1,0:T(8,128)(2,1)}), bf16[2,2048,384]{2,1,0:T(8,128)(2,1)}, u32[]{:S(2)}, u32[]{:S(2)}) async-start(bf16[2,2048,384]{2,1,0:T(8,128)(2,1)} %broadcast_in_dim.280), calls=%async_computation.3 | async-start | bytes 6291456 | tf_op jit(solution)/shard_map/all_to_all | solution.py:19
  (32 other events, 115.0 us)
Sparse Core Ops, SparseCore 0:
  11.0 24.0 all-reduce.30
  37.4 14.9 reduce-scatter.5
  54.7 15.0 reduce-scatter.7
  332.2 13.2 all-gather.6
  351.1 87.0 all-reduce.32
  440.3 13.8 reduce-scatter.9
  858.4 52.6 all-reduce.34
  913.2 12.0 all-gather.10
  926.9 13.1 all-gather.8
  945.0 151.2 all-reduce.36
where the time goes:
time: 1120 us; the launch traced here: 1110 us
  local copies, waits for them, and re-layouts  297 us (27%)
  matrix products  264 us (24%)
  waiting for transfers between devices  213 us (19%)
  other arithmetic  209 us (19%)
  blocking collectives  99.6 us (9%)
  between operations  16.1 us (1%)
    dynamic_update_slice x96, local copies, waits for them, and re-layouts, state_scan(): lax.scan(advance, start, (split(values), split(inputs_b), split(reads_c),...  192 us
    dot_general x24, matrix products, advance(): inside = jnp.einsum('sqkh,skhp->sqhp', weights, vals, precision=HIGHEST)  81.3 us
    another operation x46, other arithmetic  76.3 us
    psum x1, waiting for transfers between devices, body(): proj, square_inner = lax.psum((proj_part, square_block), 'col')  73.5 us
    dynamic_update_slice x32, other arithmetic, state_scan(): lax.scan(advance, start, (split(values), split(inputs_b), split(reads_c),...  45.9 us
    dot_general x24, matrix products, advance(): jnp.einsum('skh,skhp,skn->shpn', tails, vals, b_in, precision=HIGHEST)  44.9 us
    psum x1, waiting for transfers between devices, body(): lax.psum((g_gate, g_value, g_step, g_state, pulled[4], pulled[5], g_kerne...  44.6 us
    dot_general x24, matrix products, advance(): scores = jnp.einsum('sqn,skn->sqk', c_in, b_in, precision=HIGHEST)  44 us
  transfers between devices with their start and end apart: 12, of which 9 were waited for; matrix products, arithmetic and copies ran while one was open for 31% of the time, Pallas kernels for 0%

commit v1 on v0

v1 whole, which is shorter than its diff:
```python
import functools

import jax
import jax.numpy as jnp
from jax import lax
from jax.experimental import pallas as pl
from jax.experimental.pallas import tpu as pltpu
from jax.sharding import PartitionSpec as P

LEN = 2048
EPSILON = 1e-05
SUB = 128
STEP = 256
F32 = jnp.float32
BF16 = jnp.bfloat16
SWAP = [(0, 1), (1, 0)]


def dot(a, b):
    return jnp.dot(a, b, preferred_element_type=F32)


def dot_nt(a, b):
    return lax.dot_general(a, b, (((1,), (1,)), ((), ())), preferred_element_type=F32)


def dot_tn(a, b):
    return lax.dot_general(a, b, (((0,), (0,)), ((), ())), preferred_element_type=F32)


def sigmoid(x):
    return 0.5 * jnp.tanh(0.5 * x) + 0.5


def softplus(x):
    return jnp.maximum(x, 0.0) + jnp.log1p(jnp.exp(-jnp.abs(x)))


def fold8(x):
    return jnp.sum(x.reshape(x.shape[0] // 8, 8, x.shape[1]), axis=0)


def row_scan(x, mat):
    hi = x.astype(BF16).astype(F32)
    rest = x - hi
    mid = rest.astype(BF16).astype(F32)
    low = rest - mid
    parts = jnp.concatenate([hi, mid, low, jnp.zeros_like(x)], axis=0).astype(BF16)
    out = dot(parts, mat)
    return out[0:8] + out[8:16] + out[16:24]


def head_sums(sel, z):
    hi = z.astype(BF16)
    low = (z - hi.astype(F32)).astype(BF16)
    return (dot_nt(sel, hi) + dot_nt(sel, low))[0:8]


def iota(shape, dim):
    return lax.broadcasted_iota(jnp.int32, shape, dim)


def spread(cols, first, rows):
    lane = iota((rows, 128), 1)
    return jnp.where(
        lane < 64,
        jnp.broadcast_to(cols[:, first : first + 1], (rows, 128)),
        jnp.broadcast_to(cols[:, first + 1 : first + 2], (rows, 128)),
    )


def pair_stack(x):
    lane = iota(x.shape, 1)
    zero = jnp.zeros_like(x)
    return jnp.concatenate([jnp.where(lane < 64, x, zero), jnp.where(lane < 64, zero, x)], axis=0)


def forward_kernel(
    steps_per_seq,
    width,
    hid_own,
    hid_rec,
    gains,
    w_own,
    w_rec,
    vtap,
    stap,
    head_par,
    mixed_out,
    pre_gate_out,
    pre_value_out,
    conv_value_out,
    pre_shared_out,
    conv_shared_out,
    y_out,
    state_out,
    rows_out,
    state,
    vbuf,
    sbuf,
):
    chan = mixed_out.shape[1]
    pairs = chan // 128

    @pl.when(pl.program_id(0) % steps_per_seq == 0)
    def _():
        state[...] = jnp.zeros_like(state)
        vbuf[0:8, :] = jnp.zeros((8, vbuf.shape[1]), F32)
        sbuf[0:8, :] = jnp.zeros((8, sbuf.shape[1]), F32)

    h0 = hid_own[...].astype(F32)
    h1 = hid_rec[...].astype(F32)
    square = jnp.sum(h0 * h0, axis=1, keepdims=True) + jnp.sum(h1 * h1, axis=1, keepdims=True)
    recip = lax.rsqrt(square / width + EPSILON)
    n0 = (h0 * gains[0:1, :]).astype(BF16)
    n1 = (h1 * gains[1:2, :]).astype(BF16)
    q = dot(n0, w_own[...]) + dot(n1, w_rec[...])
    pre = q * recip
    gate = pre[:, 0:chan]
    pre_gate_out[...] = gate
    pre_value = pre[:, chan : 2 * chan]
    pre_value_out[...] = pre_value
    pre_shared = pre[:, 2 * chan : 2 * chan + 256]
    pre_shared_out[...] = pre_shared
    vbuf[8 : 8 + STEP, :] = pre_value
    sbuf[8 : 8 + STEP, :] = pre_shared
    conv = jnp.broadcast_to(vtap[4:5, :], (STEP, chan))
    conv_s = jnp.broadcast_to(stap[4:5, :], (STEP, 256))
    for k in range(4):
        conv = conv + vbuf[5 + k : 5 + k + STEP, :] * vtap[k : k + 1, :]
        conv_s = conv_s + sbuf[5 + k : 5 + k + STEP, :] * stap[k : k + 1, :]
    vbuf[0:8, :] = vbuf[STEP : STEP + 8, :]
    sbuf[0:8, :] = sbuf[STEP : STEP + 8, :]
    conv_value_out[...] = conv
    conv_shared_out[...] = conv_s
    x = conv * sigmoid(conv)
    act = conv_s * sigmoid(conv_s)

    head_rows = jnp.transpose(pre[:, 2 * chan + 256 : 2 * chan + 384])[0:8]
    v = head_rows + head_par[0:8, 0:1]
    steps = softplus(v)
    logd = head_par[8:16, 0:1] * steps
    rows_out[0:8, :] = v
    rows_out[16:24, :] = jnp.transpose(jnp.broadcast_to(recip, (STEP, 128)))[0:8]

    upper = (iota((SUB, SUB), 0) <= iota((SUB, SUB), 1)).astype(F32).astype(BF16)
    causal = iota((SUB, SUB), 0) >= iota((SUB, SUB), 1)
    sg = gate * sigmoid(gate)
    for sub in range(STEP // SUB):
        lo, hi = sub * SUB, (sub + 1) * SUB
        cum_r = row_scan(logd[:, lo:hi], upper)
        rows_out[8:16, lo:hi] = cum_r
        cols = jnp.transpose(jnp.concatenate([cum_r, steps[:, lo:hi]], axis=0))
        b_in = act[lo:hi, 0:128]
        b_bf = b_in.astype(BF16)
        c_bf = act[lo:hi, 128:256].astype(BF16)
        b_t = jnp.transpose(b_in).astype(BF16)
        scores = dot_nt(c_bf, b_bf)
        for p in range(pairs):
            pl0, pl1 = p * 128, (p + 1) * 128
            c0 = jnp.broadcast_to(cols[:, 2 * p : 2 * p + 1], (SUB, 128))
            c1 = jnp.broadcast_to(cols[:, 2 * p + 1 : 2 * p + 2], (SUB, 128))
            weights = []
            for col, h in ((c0, 2 * p), (c1, 2 * p + 1)):
                gap = jnp.where(causal, col - cum_r[h : h + 1, :], -1e30)
                weights.append((scores * jnp.exp(gap)).astype(BF16))
            lane = iota((SUB, 128), 1)
            cum_e = jnp.where(lane < 64, c0, c1)
            step_e = spread(cols, 8 + 2 * p, SUB)
            xs = x[lo:hi, pl0:pl1]
            xh = step_e * xs
            inside = dot(jnp.concatenate(weights, axis=1), pair_stack(xh.astype(BF16)))
            held = state[:, pl0:pl1]
            held_bf = held.astype(BF16)
            state_out[lo:hi, pl0:pl1] = held_bf
            carried = dot(c_bf, held_bf)
            y = inside + carried * jnp.exp(cum_e)
            y_out[lo:hi, pl0:pl1] = y
            last = cum_e[SUB - 1 : SUB, :]
            tail = (xh * jnp.exp(last - cum_e)).astype(BF16)
            state[:, pl0:pl1] = held * jnp.exp(last) + dot(b_t, tail)
            y = y + vtap[5:6, pl0:pl1] * xs
            mixed_out[lo:hi, pl0:pl1] = (y * sg[lo:hi, pl0:pl1]).astype(BF16)


def backward_kernel(
    steps_per_seq,
    cot_own,
    cot_rec,
    wo_own,
    wo_rec,
    trow,
    rows_in,
    mixed,
    pre_gate,
    pre_value,
    conv_value,
    pre_shared,
    conv_shared,
    y_in,
    state_in,
    w_own,
    w_rec,
    vtap,
    stap,
    head_par,
    sel_ref,
    p_out,
    dn_own,
    dn_rec,
    rsum_out,
    acc_v,
    acc_s,
    acc_h,
    grad,
    vbuf,
    sbuf,
    dxbuf,
    dbbuf,
):
    chan = mixed.shape[1]
    pairs = chan // 128

    @pl.when(pl.program_id(0) == 0)
    def _():
        acc_v[...] = jnp.zeros_like(acc_v)
        acc_s[...] = jnp.zeros_like(acc_s)
        acc_h[...] = jnp.zeros_like(acc_h)

    @pl.when(pl.program_id(0) % steps_per_seq == 0)
    def _():
        grad[...] = jnp.zeros_like(grad)
        vbuf[STEP : STEP + 8, :] = jnp.zeros((8, vbuf.shape[1]), F32)
        sbuf[STEP : STEP + 8, :] = jnp.zeros((8, sbuf.shape[1]), F32)

    tcol = jnp.transpose(jnp.concatenate([trow[...], rows_in[16:24, :]], axis=0))
    scale = tcol[:, 0:1]
    coef = tcol[:, 1:2]
    recip = tcol[:, 8:9]
    s0 = (cot_own[...].astype(F32) * scale).astype(BF16)
    s1 = (cot_rec[...].astype(F32) * scale).astype(BF16)
    d_weighted = dot_nt(s0, wo_own[...]) + dot_nt(s1, wo_rec[...])
    mix = mixed[...].astype(F32)
    acc_v[48:56, :] += fold8(d_weighted * mix)
    d_mixed = d_weighted * vtap[6:7, :] - coef * mix
    gate = pre_gate[...]
    sig = sigmoid(gate)
    silu = gate * sig
    conv = conv_value[...]
    sig_v = sigmoid(conv)
    x = conv * sig_v
    y_scan = y_in[...]
    y = y_scan + vtap[5:6, :] * x
    dy = d_mixed * silu
    d_gate = d_mixed * y * (sig + silu * (1.0 - sig))
    acc_v[40:48, :] += fold8(dy * x)
    conv_s = conv_shared[...]
    sig_s = sigmoid(conv_s)
    act = conv_s * sig_s

    sel = sel_ref[...]
    sel_f = sel.astype(F32)[0:8]
    v = rows_in[0:8, :]
    steps = softplus(v)
    logd = head_par[8:16, 0:1] * steps
    lower = (iota((SUB, SUB), 0) >= iota((SUB, SUB), 1)).astype(F32).astype(BF16)
    strict = (iota((SUB, SUB), 0) < iota((SUB, SUB), 1)).astype(F32).astype(BF16)
    causal_t = iota((SUB, SUB), 0) <= iota((SUB, SUB), 1)
    for sub in reversed(range(STEP // SUB)):
        lo, hi = sub * SUB, (sub + 1) * SUB
        cum_r = rows_in[8:16, lo:hi]
        cols = jnp.transpose(jnp.concatenate([cum_r, steps[:, lo:hi]], axis=0))
        b_bf = act[lo:hi, 0:128].astype(BF16)
        c_in = act[lo:hi, 128:256]
        c_bf = c_in.astype(BF16)
        c_t = jnp.transpose(c_in).astype(BF16)
        scores_t = dot_nt(b_bf, c_bf)
        d_scores = jnp.zeros((SUB, SUB), F32)
        db = jnp.zeros((SUB, 128), F32)
        dc = jnp.zeros((SUB, 128), F32)
        z_sum = jnp.zeros((8, SUB), F32)
        e_sum = jnp.zeros((8, SUB), F32)
        f_sum = jnp.zeros((8, SUB), F32)
        gh = jnp.zeros((8, 1), F32)
        for p in range(pairs):
            pl0, pl1 = p * 128, (p + 1) * 128
            c0 = jnp.broadcast_to(cols[:, 2 * p : 2 * p + 1], (SUB, 128))
            c1 = jnp.broadcast_to(cols[:, 2 * p + 1 : 2 * p + 2], (SUB, 128))
            decays = []
            for col, h in ((c0, 2 * p), (c1, 2 * p + 1)):
                gap = jnp.where(causal_t, cum_r[h : h + 1, :] - col, -1e30)
                decays.append(jnp.exp(gap))
            weights = [(scores_t * d).astype(BF16) for d in decays]
            lane = iota((SUB, 128), 1)
            cum_e = jnp.where(lane < 64, c0, c1)
            step_e = spread(cols, 8 + 2 * p, SUB)
            xs = x[lo:hi, pl0:pl1]
            xh = step_e * xs
            xh_bf = xh.astype(BF16)
            dys = dy[lo:hi, pl0:pl1]
            dys_bf = dys.astype(BF16)
            stack = pair_stack(dys_bf)
            inner = dot(jnp.concatenate(weights, axis=1), stack)
            d_pair = dot_nt(xh_bf, stack)
            d_scores = d_scores + decays[0] * d_pair[:, 0:128] + decays[1] * d_pair[:, 128:256]
            last = cum_e[SUB - 1 : SUB, :]
            tail_e = jnp.exp(last - cum_e)
            g = grad[:, pl0:pl1]
            g_bf = g.astype(BF16)
            outer = dot(b_bf, g_bf) * tail_e
            u = inner + outer
            dxbuf[lo:hi, pl0:pl1] = step_e * u + vtap[5:6, pl0:pl1] * dys
            db = db + dot_nt((xh * tail_e).astype(BF16), g_bf)
            dya = (dys * jnp.exp(cum_e)).astype(BF16)
            held = state_in[lo:hi, pl0:pl1]
            dc = dc + dot_nt(dya, held)
            sel_p = sel[:, pl0:pl1]
            z_sum = z_sum + head_sums(
                sel_p, dys_bf.astype(F32) * y_in[lo:hi, pl0:pl1] - xh_bf.astype(F32) * inner
            )
            e_sum = e_sum + head_sums(sel_p, xh * outer)
            f_sum = f_sum + head_sums(sel_p, xs * u)
            decay_row = jnp.exp(last)
            gh_row = decay_row * jnp.sum(g * held.astype(F32), axis=0, keepdims=True)
            gh = gh + jnp.sum(sel_f[:, pl0:pl1] * gh_row, axis=1, keepdims=True)
            grad[:, pl0:pl1] = g * decay_row + dot(c_t, dya)
        ds_bf = d_scores.astype(BF16)
        dbbuf[lo:hi, 0:128] = db + dot(ds_bf, c_bf)
        dbbuf[lo:hi, 128:256] = dc + dot(jnp.transpose(d_scores).astype(BF16), b_bf)
        d_log = row_scan(z_sum, lower) + row_scan(e_sum, strict) + gh
        d_step = (f_sum + d_log * head_par[8:16, 0:1]) * sigmoid(v[:, lo:hi])
        acc_h[0:8, :] += d_log * logd[:, lo:hi]
        acc_h[8:16, :] += d_step
        pre_step = v[:, lo:hi] - head_par[0:8, 0:1]
        rsum_out[:, lo:hi] = jnp.broadcast_to(
            jnp.sum(d_step * pre_step, axis=0, keepdims=True), (8, SUB)
        )
        d_cols = jnp.transpose(jnp.concatenate([d_step, jnp.zeros((120, SUB), F32)], axis=0))
        p_out[lo:hi, 2 * chan + 256 : 2 * chan + 384] = (recip[lo:hi] * d_cols).astype(BF16)

    d_conv = dxbuf[...] * (sig_v + x * (1.0 - sig_v))
    d_conv_s = dbbuf[...] * (sig_s + act * (1.0 - sig_s))
    vbuf[0:STEP, :] = d_conv
    sbuf[0:STEP, :] = d_conv_s
    acc_v[32:40, :] += fold8(d_conv)
    acc_s[32:40, :] += fold8(d_conv_s)
    pv = pre_value[...]
    ps = pre_shared[...]
    d_value = jnp.zeros((STEP, chan), F32)
    d_shared = jnp.zeros((STEP, 256), F32)
    for k in range(4):
        moved = vbuf[3 - k : 3 - k + STEP, :]
        d_value = d_value + vtap[k : k + 1, :] * moved
        acc_v[8 * k : 8 * k + 8, :] += fold8(pv * moved)
        moved = sbuf[3 - k : 3 - k + STEP, :]
        d_shared = d_shared + stap[k : k + 1, :] * moved
        acc_s[8 * k : 8 * k + 8, :] += fold8(ps * moved)
    vbuf[STEP : STEP + 8, :] = vbuf[0:8, :]
    sbuf[STEP : STEP + 8, :] = sbuf[0:8, :]
    p_out[:, 0:chan] = (recip * d_gate).astype(BF16)
    p_out[:, chan : 2 * chan] = (recip * d_value).astype(BF16)
    p_out[:, 2 * chan : 2 * chan + 256] = (recip * d_shared).astype(BF16)
    ones = jnp.ones((16, chan), BF16)
    rsum_out[...] += head_sums(ones, d_gate * gate + d_value * pv)
    rsum_out[...] += head_sums(ones[:, 0:256], d_shared * ps)
    pb = p_out[...]
    dn_own[...] = dot_nt(pb, w_own[...]).astype(BF16)
    dn_rec[...] = dot_nt(pb, w_rec[...]).astype(BF16)


def swap(x, axis):
    return lax.ppermute(x, axis, SWAP)


def body(
    hidden,
    gate_proj,
    value_proj,
    step_proj,
    state_proj,
    value_filter,
    value_shift,
    shared_kernel,
    shared_offset,
    decay_log,
    step_bias,
    skip_gain,
    input_gain,
    gated_gain,
    output_proj,
    cotangent,
):
    tokens, half = hidden.shape
    width = 2 * half
    chan = gated_gain.shape[0]
    inner_width = 4 * chan
    heads = decay_log.shape[0]
    r = lax.axis_index("row")
    seq_len = min(LEN, tokens)
    steps_per_seq = seq_len // STEP
    grid = tokens // STEP

    def cut(x, start, size, axis):
        return lax.dynamic_slice_in_dim(x, start * size, size, axis)

    def packed(side):
        return jnp.concatenate(
            [
                cut(gate_proj, side, chan, 1),
                cut(value_proj, side, chan, 1),
                state_proj,
                jnp.pad(cut(step_proj, side, heads, 1), ((0, 0), (0, 128 - heads))),
            ],
            axis=1,
        )

    w_own = packed(r)
    w_rec = swap(packed(1 - r), "row")
    hid_rec = swap(hidden, "row")
    cot_rec = swap(cotangent, "row")
    wo_own = cut(output_proj, r, chan, 0)
    wo_part = cut(output_proj, 1 - r, chan, 0)
    wo_rec = swap(wo_part, "row")
    gain_f = gated_gain.astype(F32)
    two = swap(jnp.stack([input_gain, gain_f]), "row")
    gains = jnp.concatenate([input_gain[None], two[0:1], jnp.zeros((6, half), F32)], axis=0)
    gated_rec = two[1]

    skip_lane = jnp.repeat(skip_gain, chan // heads)
    vtap = jnp.concatenate(
        [value_filter, value_shift[None], skip_lane[None], gain_f[None], jnp.zeros((1, chan), F32)], axis=0
    )
    stap = jnp.concatenate([shared_kernel, shared_offset[None], jnp.zeros((3, 256), F32)], axis=0)
    pad_h = (0, 8 - heads)
    head_par = jnp.concatenate([jnp.pad(step_bias, pad_h), jnp.pad(-jnp.exp(decay_log), pad_h)])
    head_par = jnp.broadcast_to(head_par[:, None], (16, 128))

    wide = w_own.shape[1]

    def blk(cols):
        return pl.BlockSpec((STEP, cols), lambda i: (i, 0))

    def whole(shape):
        return pl.BlockSpec(shape, lambda i: (0, 0))

    def arr(cols, dtype=F32):
        return jax.ShapeDtypeStruct((tokens, cols), dtype)

    mixed, pre_gate, pre_value, conv_value, pre_shared, conv_shared, y_scan, states, rows = pl.pallas_call(
        functools.partial(forward_kernel, steps_per_seq, width),
        grid=(grid,),
        in_specs=[
            blk(half),
            blk(half),
            whole((8, half)),
            whole((half, wide)),
            whole((half, wide)),
            whole((8, chan)),
            whole((8, 256)),
            whole((16, 128)),
        ],
        out_specs=[
            blk(chan),
            blk(chan),
            blk(chan),
            blk(chan),
            blk(256),
            blk(256),
            blk(chan),
            blk(chan),
            pl.BlockSpec((24, STEP), lambda i: (0, i)),
        ],
        out_shape=[
            arr(chan, BF16),
            arr(chan),
            arr(chan),
            arr(chan),
            arr(256),
            arr(256),
            arr(chan),
            arr(chan, BF16),
            jax.ShapeDtypeStruct((24, tokens), F32),
        ],
        scratch_shapes=[
            pltpu.VMEM((128, chan), F32),
            pltpu.VMEM((STEP + 8, chan), F32),
            pltpu.VMEM((STEP + 8, 256), F32),
        ],
        name="forward_core",
    )(hidden, hid_rec, gains, w_own, w_rec, vtap, stap, head_par)

    mixed_rec = swap(mixed, "row")
    own32 = mixed.astype(F32)
    rec32 = mixed_rec.astype(F32)
    weighted = (own32 * gain_f).astype(BF16)
    weighted_rec = (rec32 * gated_rec).astype(BF16)
    proj_part = dot(weighted, wo_own) + dot(weighted_rec, wo_part)
    hidden32 = hidden.astype(F32)
    cot32 = cotangent.astype(F32)
    sums = jnp.stack([jnp.sum(own32 * own32, axis=1), jnp.sum(cot32 * proj_part, axis=1)])
    sums = sums + swap(sums, "row")
    sums = sums + swap(sums, "col")
    proj_bf = proj_part.astype(BF16)
    proj = proj_bf.astype(F32) + swap(proj_bf, "col").astype(F32)
    scale = lax.rsqrt(sums[0] / inner_width + EPSILON)
    result = (hidden32 + scale[:, None] * proj).astype(BF16)
    scaled_cot = (scale[:, None] * cot32).astype(BF16)
    g_out_own = dot_tn(weighted, scaled_cot)
    g_out_rec = dot_tn(weighted_rec, scaled_cot)
    trow = jnp.concatenate(
        [scale[None], (sums[1] * scale**3 / inner_width)[None], jnp.zeros((6, tokens), F32)], axis=0
    )

    lane_head = jnp.arange(chan) // (chan // heads)
    sel = (jnp.arange(16)[:, None] == lane_head[None, :]).astype(BF16)
    last = grid - 1

    def rblk(cols):
        return pl.BlockSpec((STEP, cols), lambda i: (last - i, 0))

    def rrow(count):
        return pl.BlockSpec((count, STEP), lambda i: (0, last - i))

    p_all, dn_own, dn_rec, rsum, acc_v, acc_s, acc_h = pl.pallas_call(
        functools.partial(backward_kernel, steps_per_seq),
        grid=(grid,),
        in_specs=[
            rblk(half),
            rblk(half),
            whole((chan, half)),
            whole((chan, half)),
            rrow(8),
            rrow(24),
            rblk(chan),
            rblk(chan),
            rblk(chan),
            rblk(chan),
            rblk(256),
            rblk(256),
            rblk(chan),
            rblk(chan),
            whole((half, wide)),
            whole((half, wide)),
            whole((8, chan)),
            whole((8, 256)),
            whole((16, 128)),
            whole((16, chan)),
        ],
        out_specs=[
            rblk(wide),
            rblk(half),
            rblk(half),
            rrow(8),
            whole((56, chan)),
            whole((40, 256)),
            whole((16, 128)),
        ],
        out_shape=[
            arr(wide, BF16),
            arr(half, BF16),
            arr(half, BF16),
            jax.ShapeDtypeStruct((8, tokens), F32),
            jax.ShapeDtypeStruct((56, chan), F32),
            jax.ShapeDtypeStruct((40, 256), F32),
            jax.ShapeDtypeStruct((16, 128), F32),
        ],
        scratch_shapes=[
            pltpu.VMEM((128, chan), F32),
            pltpu.VMEM((STEP + 8, chan), F32),
            pltpu.VMEM((STEP + 8, 256), F32),
            pltpu.VMEM((STEP, chan), F32),
            pltpu.VMEM((STEP, 256), F32),
        ],
        name="backward_core",
    )(
        cotangent,
        cot_rec,
        wo_own,
        wo_rec,
        trow,
        rows,
        mixed,
        pre_gate,
        pre_value,
        conv_value,
        pre_shared,
        conv_shared,
        y_scan,
        states,
        w_own,
        w_rec,
        vtap,
        stap,
        head_par,
        sel,
    )

    rs = rsum[0]
    rs = rs + swap(rs, "row")
    rs = rs + swap(rs, "col")
    dn_sum = (dn_own.astype(F32) + swap(dn_rec, "row").astype(F32)).astype(BF16)
    d_normed = dn_sum.astype(F32) + swap(dn_sum, "col").astype(F32)
    recip = rows[16]
    hidden_grad = (
        cot32 + d_normed * input_gain - (rs * recip * recip / width)[:, None] * hidden32
    )
    g_norm = jnp.sum(d_normed * hidden32, axis=0)

    normed = (hidden32 * input_gain).astype(BF16)
    normed_rec = (hid_rec.astype(F32) * gains[1]).astype(BF16)
    g_own = dot_tn(normed, p_all)
    g_other = swap(dot_tn(normed_rec, p_all), "row")

    def arrange(mine, theirs, axis):
        first = jnp.where(r == 0, mine, theirs)
        second = jnp.where(r == 0, theirs, mine)
        return jnp.concatenate([first, second], axis=axis)

    g_gate = arrange(g_own[:, 0:chan], g_other[:, 0:chan], 1)
    g_value = arrange(g_own[:, chan : 2 * chan], g_other[:, chan : 2 * chan], 1)
    g_state = g_own[:, 2 * chan : 2 * chan + 256] + g_other[:, 2 * chan : 2 * chan + 256]
    s0 = 2 * chan + 256
    g_step = arrange(g_own[:, s0 : s0 + heads], g_other[:, s0 : s0 + heads], 1)
    g_output = arrange(g_out_own, g_out_rec, 0)

    vsum = jnp.sum(acc_v.reshape(7, 8, chan), axis=1)
    ssum = jnp.sum(acc_s.reshape(5, 8, 256), axis=1)
    hsum = jnp.sum(acc_h.reshape(2, 8, 128), axis=2)[:, 0:heads]
    g_skip = jnp.sum(vsum[5].reshape(heads, chan // heads), axis=1)
    shared_all = jnp.concatenate([g_state, jnp.pad(ssum, ((0, 3), (0, 0)))], axis=0)
    shared_all = shared_all + swap(shared_all, "col")
    g_state = shared_all[0:half]
    s_part = shared_all[half : half + 5]
    s_part = s_part + swap(s_part, "row")
    reduced = lax.psum(
        (
            g_gate,
            g_value,
            g_step,
            g_state,
            vsum[0:4],
            vsum[4],
            s_part[0:4],
            s_part[4],
            hsum[0],
            hsum[1],
            g_skip,
            g_norm,
            vsum[6],
            g_output,
        ),
        "dp",
    )
    return (result, hidden_grad) + tuple(reduced)


def solution(mesh):
    in_specs = (
        P("dp", "row"),
        P("row", "col"),
        P("row", "col"),
        P("row", "col"),
        P("row", None),
        P(None, ("col", "row")),
        P(("col", "row")),
        P(),
        P(),
        P(("col", "row")),
        P(("col", "row")),
        P(("col", "row")),
        P("row"),
        P(("col", "row")),
        P("col", "row"),
        P("dp", "row"),
    )
    out_specs = (
        P("dp", "row"),
        P("dp", "row"),
        P("row", "col"),
        P("row", "col"),
        P("row", "col"),
        P("row", None),
        P(None, ("col", "row")),
        P(("col", "row")),
        P(),
        P(),
        P(("col", "row")),
        P(("col", "row")),
        P(("col", "row")),
        P("row"),
        P(("col", "row")),
        P("col", "row"),
    )
    return jax.shard_map(body, mesh=mesh, in_specs=in_specs, out_specs=out_specs, check_vma=False)
```

time: 1120 us -> 286 us (0.26)
  local copies, waits for them, and re-layouts: 297 us -> 26.1 us
  matrix products: 264 us -> 15.7 us
  other arithmetic: 209 us -> 29.2 us
  waiting for transfers between devices: 213 us -> 89.4 us
  blocking collectives: 99.6 us -> 39.9 us
  Pallas kernels: 0 us -> 59.4 us
    dot_general x111 -> x6, matrix products: 264 us -> 15.7 us  [the longest x4 12 us: dot_tn(): lax.dot_general(a, b, (((0,), (0,)), ((), ())), preferred_element_type=F32)]
    dynamic_update_slice x96 -> x0, local copies, waits for them, and re-layouts: 192 us -> none  [state_scan(): lax.scan(advance, start, (split(values), split(inputs_b), split(reads_c),...]
    psum x4 -> x1, waiting for transfers between devices: 159 us -> 28.5 us  [body(): lax.psum((g_gate, g_value, g_step, g_state, vsum[0:4], vsum[4], s_part[0:...]
    another operation x46 -> x2, other arithmetic: 76.3 us -> 0.03 us  [the longest x1 0.02 us: body(): jnp.stack([jnp.sum(own32 * own32, axis=1), jnp.sum(cot32 * proj_part, axi...]
    ppermute x0 -> x16, waiting for transfers between devices: none -> 60.8 us  [swap(): return lax.ppermute(x, axis, SWAP)]
    pallas_call x0 -> x2, Pallas kernels: none -> 59.4 us  [the longest x1 37.9 us: body(): pl.pallas_call(functools.partial(backward_kernel, steps_per_seq), grid=(g...]
    psum x5 -> x1, blocking collectives: 92.2 us -> 39.9 us  [body(): lax.psum((g_gate, g_value, g_step, g_state, vsum[0:4], vsum[4], s_part[0:...]
    reduce_sum x35 -> x6, other arithmetic: 58.4 us -> 10.6 us  [the longest x1 5.22 us: body(): g_norm = jnp.sum(d_normed * hidden32, axis=0)]
  transfers between devices with their start and end apart: 12 -> 17, of which waited for: 9 -> 6; matrix products, arithmetic and copies ran while one was open for 31% -> 19% of each run, Pallas kernels for 0% -> 0%
where the time goes in v1:
time: 286 us; the launch traced here: 285 us
  waiting for transfers between devices  89.4 us (31%)
  Pallas kernels  59.4 us (21%)
  blocking collectives  39.9 us (14%)
  other arithmetic  29.2 us (10%)
  local copies, waits for them, and re-layouts  26.1 us (9%)
  matrix products  15.7 us (5%)
  between operations  14.5 us (5%)
  starting transfers between devices  11.2 us (4%)
    ppermute x16, waiting for transfers between devices, swap(): return lax.ppermute(x, axis, SWAP)  60.8 us
    psum x1, blocking collectives, body(): lax.psum((g_gate, g_value, g_step, g_state, vsum[0:4], vsum[4], s_part[0:...  39.9 us
    pallas_call x1, Pallas kernels, body(): pl.pallas_call(functools.partial(backward_kernel, steps_per_seq), grid=(g...  37.9 us
    psum x1, waiting for transfers between devices, body(): lax.psum((g_gate, g_value, g_step, g_state, vsum[0:4], vsum[4], s_part[0:...  28.5 us
    pallas_call x1, Pallas kernels, body(): pl.pallas_call(functools.partial(forward_kernel, steps_per_seq, width), g...  21.5 us
    dot_general x4, matrix products, dot_tn(): lax.dot_general(a, b, (((0,), (0,)), ((), ())), preferred_element_type=F32)  12 us
    ppermute x16, starting transfers between devices, swap(): return lax.ppermute(x, axis, SWAP)  11.1 us
    unnamed x80, local copies, waits for them, and re-layouts  9.98 us
  transfers between devices with their start and end apart: 17, of which 6 were waited for; matrix products, arithmetic and copies ran while one was open for 19% of the time, Pallas kernels for 0%

profile of v1, /device:TPU:0, one launch (start us, length us, event | category | flops | bytes accessed | tf_op | source)
XLA Modules:
  0.0 285.5 jit_solution(9565443075961573976)
XLA Ops:
  17.2 21.5 %forward_core.1 = (bf16[2048,384]{1,0:T(8,128)(2,1)}, f32[2048,384]{1,0:T(8,128)}, f32[2048,384]{1,0:T(8,128)}, f32[2048,384]{1,0:T(8,128)}, f32[2048,256]{1,0:T...) custom-call(bf16[2048,384]{1,0:T(8,128)(2,1)} %hid_own.1, ...), custom_call_target="tpu_custom_call" | custom-call | tf_op jit(solution)/shard_map/forward_core/pallas_call | solution.py:449
  39.6 1.8 fusion
  45.0 2.6 fusion.2
  48.9 2.7 collective-permute-start.5
  55.3 37.9 %backward_core.1 = (bf16[2048,1152]{1,0:T(8,128)(2,1)}, bf16[2048,384]{1,0:T(8,128)(2,1)}, bf16[2048,384]{1,0:T(8,128)(2,1)}, f32[8,2048]{1,0:T(8,128)}, f32[56,...) custom-call(bf16[2048,384]{1,0:T(8,128)(2,1)} %cot_own.1, bf16[2048,384]{1,0:T(8,128)(2,1)} %copy-done.8, ...), custom_call_target="tpu_custom_call" | custom-call | tf_op jit(solution)/shard_map/backward_core/pallas_call | solution.py:524
  93.2 5.9 %fusion.10 = f32[384,1152]{1,0:T(8,128)} fusion(bf16[2048,1152]{1,0:T(8,128)(2,1)} %get-tuple-element.44, bf16[2048,384]{1,0:T(8,128)(2,1)S(1)} %copy-done.10, f32[384]{0:T(512)S(1)} %get-tuple-element.67), kind=kOutput, calls=%fused_computation.24 | convolution fusion | flops 1814298624 | bytes 8062464 | tf_op jit(solution)/shard_map/dot_general | solution.py:28
  99.7 2.7 fusion.15
  105.4 2.3 fusion.11
  107.7 1.4 slice_add_fusion
  109.1 2.1 collective-permute-start.14
  111.2 1.4 slice_select_fusion.1
  114.8 5.8 %collective-permute-done.14 = f32[392,256]{1,0:T(8,128)S(1)} collective-permute-done((f32[392,256]{1,0:T(8,128)S(1)}, f32[392,256]{1,0:T(8,128)S(1)}, u32[]{:S(2)}, u32[]{:S(2)}) %collective-permute-start.14) | collective-permute-done | bytes 401440 | tf_op jit(solution)/shard_map/ppermute | solution.py:372
  121.5 1.8 collective-permute-start.6
  123.3 3.4 %add_convert_fusion = bf16[2048,384]{1,0:T(8,128)(2,1)} fusion(bf16[2048,384]{1,0:T(8,128)(2,1)} %collective-permute-done.9, bf16[2048,384]{1,0:T(8,128)(2,1)} %get-tuple-element.41), kind=kLoop, calls=%fused_computation.19 | loop fusion | flops 3145728 | bytes 4718592 | tf_op jit(solution)/shard_map/convert_element_type | solution.py:601
  127.0 1.4 slice.80
  134.8 1.7 collective-permute-start.12
  139.8 51.7 %collective-permute-done.12 = f32[2048]{0:T(1024)} collective-permute-done((f32[2048]{0:T(1024)}, f32[2048]{0:T(1024)}, u32[]{:S(2)}, u32[]{:S(2)}) %collective-permute-start.12) | collective-permute-done | bytes 8224 | tf_op jit(solution)/shard_map/ppermute | solution.py:372
  192.8 1.8 slice_select_fusion.5
  194.7 1.6 copy.41
  196.3 1.6 copy.42
  199.4 5.2 %fusion.7 = (f32[384]{0:T(512)S(1)}, f32[2048,384]{1,0:T(8,128)}, bf16[2048,384]{1,0:T(8,128)(2,1)}) fusion(bf16[2048,384]{1,0:T(8,128)(2,1)S(1)} %copy-done.4, bf16[2048,384]{1,0:T(8,128)(2,1)} %collective-permute-done.10, bf16[2048,384]{1,0:T(8,128)(2,1)} %add_convert_fusion, f32[2048]{0:T(1024)} %fusion.27, f32[384]{0:T(512)} %param.28, ...), kind=kLoop, calls=%fused_computation.16 | loop fusion | flops 13368960 | bytes 14175232 | tf_op jit(solution)/shard_map/reduce_sum | solution.py:607
  204.7 39.9 %all-reduce.5 = (f32[384,12]{0,1:T(8,128)}, f32[4,384]{1,0:T(4,128)}, f32[384]{0:T(512)}, f32[4,256]{1,0:T(4,128)}, f32[256]{0:T(256)}, /*index=5*/f32[6]{0:T(12...) all-reduce(f32[384,12]{0,1:T(8,128)S(1)} %copy-done.18, ...), channel_id=1, replica_groups=mesh['dp'=8,'row'=2,'col'=2] {'dp'}, use_global_device_ids=true, to_apply=%region_4.5 | all-reduce | flops 8594 | bytes 68752 | tf_op jit(solution)/shard_map/psum | solution.py:635
  244.6 28.5 %all-reduce.9.cloned.1.call-done = (f32[384,768]{1,0:T(8,128)}, f32[384,768]{1,0:T(8,128)}, f32[384,256]{1,0:T(8,128)}, f32[768,384]{1,0:T(8,128)}) async-done(((f32[384,768]{1,0:T(8,128)}, f32[384,768]{1,0:T(8,128)}, f32[384,256]{1,0:T(8,128)}, f32[768,384]{1,0:T(8,128)}), (f32[384,768]{1,0:T(8,128)}, f32[384,768]{1,0:T(8,128)}, f32[384,256]{1,0:T(8,128)}, ...) | async-done | bytes 3932176 | tf_op jit(solution)/shard_map/psum | solution.py:635
  273.2 2.5 copy.51
  (164 shorter events, 41.5 us)
Async XLA Ops:
  7.2 266.0 %all-reduce.9.cloned.1.call-start = ((), (), s32[]{:S(2)}) async-start(), calls=%async_computation | async-start | bytes 7864320 | tf_op jit(solution)/shard_map/psum | solution.py:635
  8.6 6.4 %collective-permute-start.1 = (f32[2,384]{1,0:T(2,128)S(1)}, f32[2,384]{1,0:T(2,128)S(1)}, u32[]{:S(2)}, u32[]{:S(2)}) collective-permute-start(f32[2,384]{1,0:T(2,128)S(1)} %pad_maximum_fusion.7), channel_id=1, source_target_pairs={{0,2},{2,0},{1,3},{3,1},{4,6},{6,4},{5,7},{7,5},{8,10},{10,8},{9,1... | collective-permute-start | bytes 9224 | tf_op jit(solution)/shard_map/ppermute | solution.py:372
  9.2 6.6 %collective-permute-start = (bf16[2048,384]{1,0:T(8,128)(2,1)}, bf16[2048,384]{1,0:T(8,128)(2,1)S(1)}, u32[]{:S(2)}, u32[]{:S(2)}) collective-permute-start(bf16[2048,384]{1,0:T(8,128)(2,1)} %hid_own.1), channel_id=1, source_target_pairs={{0,2},{2,0},{1,3},{3,1},{4,6},{6,4},{5,7},{7,5},{8,10},{10,8},{9,1... | collective-permute-start | bytes 4718600 | tf_op jit(solution)/shard_map/ppermute | solution.py:372
  13.0 2.8 collective-permute-start.2
  17.2 21.7 %copy-start.14 = (bf16[768,384]{1,0:T(8,128)(2,1)S(1)}, bf16[768,384]{1,0:T(8,128)(2,1)}, u32[]{:S(2)}) copy-start(bf16[768,384]{1,0:T(8,128)(2,1)} %param.30) | copy-start | bytes 1769476
  17.2 22.3 %copy-start = (bf16[2048,384]{1,0:T(8,128)(2,1)S(1)}, bf16[2048,384]{1,0:T(8,128)(2,1)}, u32[]{:S(2)}) copy-start(bf16[2048,384]{1,0:T(8,128)(2,1)} %cot_own.1) | copy-start | bytes 4718596
  17.2 22.3 %copy-start.26 = (bf16[384]{0:T(512)(128)(2,1)S(1)}, bf16[384]{0:T(512)(128)(2,1)}, u32[]{:S(2)}) copy-start(bf16[384]{0:T(512)(128)(2,1)} %param.29) | copy-start | bytes 2308
  38.8 3.7 %collective-permute-start.3 = (bf16[2048,384]{1,0:T(8,128)(2,1)}, bf16[2048,384]{1,0:T(8,128)(2,1)S(1)}, u32[]{:S(2)}, u32[]{:S(2)}) collective-permute-start(bf16[2048,384]{1,0:T(8,128)(2,1)} %get-tuple-element.32.mixed), channel_id=1, source_target_pairs={{0,2},{2,0},{1,3},{3,1},{4,6},{6,4},{5,7},{7,5},{8,10},{10,8},{9,1... | collective-permute-start | bytes 4718600 | tf_op jit(solution)/shard_map/ppermute | solution.py:372
  39.0 5.8 %copy-start.6 = (bf16[384,384]{1,0:T(8,128)(2,1)}, bf16[384,384]{1,0:T(8,128)(2,1)S(1)}, u32[]{:S(2)}) copy-start(bf16[384,384]{1,0:T(8,128)(2,1)S(1)} %get-tuple-element.99.wo_own) | copy-start | bytes 884740
  39.0 15.1 %collective-permute-start.8 = (bf16[384,384]{1,0:T(8,128)(2,1)S(1)}, bf16[384,384]{1,0:T(8,128)(2,1)S(1)}, u32[]{:S(2)}, u32[]{:S(2)}) collective-permute-start(bf16[384,384]{1,0:T(8,128)(2,1)S(1)} %get-tuple-element.98), channel_id=1, source_target_pairs={{0,2},{2,0},{1,3},{3,1},{4,6},{6,4},{5,7},{7,5},{8,10},{10,8},{9,1... | collective-permute-start | bytes 884744 | tf_op jit(solution)/shard_map/ppermute | solution.py:372
  39.5 14.6 %collective-permute-start.7 = (bf16[2048,384]{1,0:T(8,128)(2,1)S(1)}, bf16[2048,384]{1,0:T(8,128)(2,1)S(1)}, u32[]{:S(2)}, u32[]{:S(2)}) collective-permute-start(bf16[2048,384]{1,0:T(8,128)(2,1)S(1)} %copy-done), channel_id=1, source_target_pairs={{0,2},{2,0},{1,3},{3,1},{4,6},{6,4},{5,7},{7,5},{8,10},{10,8},{9,1... | collective-permute-start | bytes 4718600 | tf_op jit(solution)/shard_map/ppermute | solution.py:372
  47.6 1.2 collective-permute-start.4
  48.9 4.4 %collective-permute-start.5 = (f32[2,2048]{1,0:T(2,128)S(1)}, f32[2,2048]{1,0:T(2,128)S(1)}, u32[]{:S(2)}, u32[]{:S(2)}) collective-permute-start(f32[2,2048]{1,0:T(2,128)S(1)} %fusion.35), channel_id=1, source_target_pairs={{0,1},{1,0},{2,3},{3,2},{4,5},{5,4},{6,7},{7,6},{8,9},{9,8},{10,11... | collective-permute-start | bytes 49160 | tf_op jit(solution)/shard_map/ppermute | solution.py:372
  55.3 37.9 %copy-start.10 = (bf16[2048,384]{1,0:T(8,128)(2,1)S(1)}, bf16[2048,384]{1,0:T(8,128)(2,1)}, u32[]{:S(2)}) copy-start(bf16[2048,384]{1,0:T(8,128)(2,1)} %copy-done.9) | copy-start | bytes 4718596
  93.2 6.5 %copy-start.20 = (f32[40,256]{1,0:T(8,128)S(1)}, f32[40,256]{1,0:T(8,128)}, u32[]{:S(2)}) copy-start(f32[40,256]{1,0:T(8,128)} %get-tuple-element.45) | copy-start | bytes 122884
  93.2 6.5 %copy-start.1 = (bf16[2048,384]{1,0:T(8,128)(2,1)S(1)}, bf16[2048,384]{1,0:T(8,128)(2,1)}, u32[]{:S(2)}) copy-start(bf16[2048,384]{1,0:T(8,128)(2,1)} %cot_own.1) | copy-start | bytes 4718596
  99.1 8.6 %collective-permute-start.13 = (f32[384,1152]{1,0:T(8,128)}, f32[384,1152]{1,0:T(8,128)}, u32[]{:S(2)}, u32[]{:S(2)}) collective-permute-start(f32[384,1152]{1,0:T(8,128)} %fusion.10), channel_id=1, source_target_pairs={{0,2},{2,0},{1,3},{3,1},{4,6},{6,4},{5,7},{7,5},{8,10},{10,8},{9,1... | collective-permute-start | bytes 5308424 | tf_op jit(solution)/shard_map/ppermute | solution.py:372
  99.1 24.2 %collective-permute-start.9 = (bf16[2048,384]{1,0:T(8,128)(2,1)}, bf16[2048,384]{1,0:T(8,128)(2,1)}, u32[]{:S(2)}, u32[]{:S(2)}) collective-permute-start(bf16[2048,384]{1,0:T(8,128)(2,1)} %get-tuple-element.42), channel_id=1, source_target_pairs={{0,2},{2,0},{1,3},{3,1},{4,6},{6,4},{5,7},{7,5},{8,10},{10,8},{9,1... | collective-permute-start | bytes 4718600 | tf_op jit(solution)/shard_map/ppermute | solution.py:372
  109.1 11.5 %collective-permute-start.14 = (f32[392,256]{1,0:T(8,128)S(1)}, f32[392,256]{1,0:T(8,128)S(1)}, u32[]{:S(2)}, u32[]{:S(2)}) collective-permute-start(f32[392,256]{1,0:T(8,128)S(1)} %select_maximum_fusion), channel_id=1, source_target_pairs={{0,1},{1,0},{2,3},{3,2},{4,5},{5,4},{6,7},{7,6},{8,9},{9,8},{10,11... | collective-permute-start | bytes 1204232 | tf_op jit(solution)/shard_map/ppermute | solution.py:372
  121.5 77.9 %collective-permute-start.6 = (bf16[2048,384]{1,0:T(8,128)(2,1)}, bf16[2048,384]{1,0:T(8,128)(2,1)}, u32[]{:S(2)}, u32[]{:S(2)}) collective-permute-start(bf16[2048,384]{1,0:T(8,128)(2,1)} %get-tuple-element.86), channel_id=1, source_target_pairs={{0,1},{1,0},{2,3},{3,2},{4,5},{5,4},{6,7},{7,6},{8,9},{9,8},{10,11... | collective-permute-start | bytes 4718600 | tf_op jit(solution)/shard_map/ppermute | solution.py:372
  126.8 72.6 %collective-permute-start.10 = (bf16[2048,384]{1,0:T(8,128)(2,1)}, bf16[2048,384]{1,0:T(8,128)(2,1)}, u32[]{:S(2)}, u32[]{:S(2)}) collective-permute-start(bf16[2048,384]{1,0:T(8,128)(2,1)} %add_convert_fusion), channel_id=1, source_target_pairs={{0,1},{1,0},{2,3},{3,2},{4,5},{5,4},{6,7},{7,6},{8,9},{9,8},{10,11... | collective-permute-start | bytes 4718600 | tf_op jit(solution)/shard_map/ppermute | solution.py:372
  132.0 2.2 collective-permute-start.11
  134.8 56.7 %collective-permute-start.12 = (f32[2048]{0:T(1024)}, f32[2048]{0:T(1024)}, u32[]{:S(2)}, u32[]{:S(2)}) collective-permute-start(f32[2048]{0:T(1024)} %add.125), channel_id=1, source_target_pairs={{0,1},{1,0},{2,3},{3,2},{4,5},{5,4},{6,7},{7,6},{8,9},{9,8},{10,11... | collective-permute-start | bytes 24584 | tf_op jit(solution)/shard_map/ppermute | solution.py:372
  197.9 1.3 collective-permute-start.15
  (31 other events, 91.0 us)
Sparse Core Ops, SparseCore 0:
  121.6 151.4 all-reduce.8

commit v2 on v1

--- a/solution.py
+++ b/solution.py
@@ -14,6 +14,7 @@
 F32 = jnp.float32
 BF16 = jnp.bfloat16
 SWAP = [(0, 1), (1, 0)]
+DN_PARTS = 4
 
 
 def dot(a, b):
@@ -95,6 +96,7 @@
     y_out,
     state_out,
     rows_out,
+    nt_out,
     state,
     vbuf,
     sbuf,
@@ -114,6 +116,9 @@
     recip = lax.rsqrt(square / width + EPSILON)
     n0 = (h0 * gains[0:1, :]).astype(BF16)
     n1 = (h1 * gains[1:2, :]).astype(BF16)
+    half = n0.shape[1]
+    nt_out[0:half, :] = jnp.transpose(n0)
+    nt_out[half : 2 * half, :] = jnp.transpose(n1)
     q = dot(n0, w_own[...]) + dot(n1, w_rec[...])
     pre = q * recip
     gate = pre[:, 0:chan]
@@ -368,6 +373,274 @@
     dn_rec[...] = dot_nt(pb, w_rec[...]).astype(BF16)
 
 
+def unit_rows(dp):
+    return 16 * dp
+
+
+def big_rows(dp, rows):
+    return pl.cdiv(rows, unit_rows(dp)) * unit_rows(dp)
+
+
+def sum_kernel(
+    dp,
+    g_cat,
+    g_out,
+    small_row,
+    small_own,
+    rs_in,
+    hid,
+    dn_own,
+    dn_rec,
+    out,
+    dn_sum,
+    dn_col,
+    rs_out,
+    acc,
+    stage,
+    land,
+    row_send,
+    row_land,
+    col_send,
+    col_land,
+    dn_land,
+    rs_land,
+    norm,
+    send_sem,
+    recv_sem,
+    pair_send,
+    pair_recv,
+    dn_send_sem,
+    dn_recv_sem,
+):
+    half = g_cat.shape[0] // 2
+    chan = g_out.shape[1]
+    wide = g_cat.shape[1]
+    size = big_rows(dp, 2 * half)
+    tail = out.shape[0] - 3 * size
+    bits = dp.bit_length() - 1
+    me = lax.axis_index("dp")
+    r = lax.axis_index("row")
+    c = lax.axis_index("col")
+
+    def bit_of(k):
+        return lax.rem(me // (1 << k), 2)
+
+    def partner(k):
+        return {"dp": me + (1 - 2 * bit_of(k)) * (1 << k)}
+
+    barrier = pltpu.get_barrier_semaphore()
+    for target in [partner(k) for k in range(bits)] + [{"row": 1 - r}, {"col": 1 - c}]:
+        pl.semaphore_signal(barrier, inc=1, device_id=target, device_id_type=pl.DeviceIdType.MESH)
+    pl.semaphore_wait(barrier, bits + 2)
+
+    other = pl.multiple_of((1 - r) * half, 128)
+    mine = pl.multiple_of(r * half, 128)
+    to_row, to_col = {"row": 1 - r}, {"col": 1 - c}
+
+    def pair_copy(src, dst, send, recv, target):
+        return pltpu.make_async_remote_copy(
+            src_ref=src,
+            dst_ref=dst,
+            send_sem=send,
+            recv_sem=recv,
+            device_id=target,
+            device_id_type=pl.DeviceIdType.MESH,
+        )
+
+    tokens = hid.shape[0]
+    cut = tokens // DN_PARTS
+
+    def dn_copy(i, side):
+        rows = pl.ds(i * cut, cut)
+        if side == 0:
+            src, dst, target = dn_rec, dn_land, to_row
+        else:
+            src, dst, target = dn_sum, dn_col, to_col
+        return pair_copy(src.at[rows, :], dst.at[rows, :], dn_send_sem.at[side, i], dn_recv_sem.at[side, i], target)
+
+    dn_rows = [dn_copy(i, 0) for i in range(DN_PARTS)]
+    dn_cols = [dn_copy(i, 1) for i in range(DN_PARTS)]
+    rs_row = pair_copy(rs_in, rs_land.at[0], pair_send.at[2], pair_recv.at[2], to_row)
+    rs_col = pair_copy(rs_out, rs_land.at[1], pair_send.at[3], pair_recv.at[3], to_col)
+    for copy in dn_rows:
+        copy.start()
+    rs_row.start()
+    row_send[0:half, :] = g_cat[half : 2 * half, :].astype(BF16)
+    row_send[half : half + 16, 0:256] = small_row[...].astype(BF16)
+    row_send[half : half + 16, 256:wide] = jnp.zeros((16, wide - 256), BF16)
+    row_copy = pair_copy(row_send, row_land, pair_send.at[0], pair_recv.at[0], to_row)
+    row_copy.start()
+
+    chunks = [
+        (0, size, tuple(range(bits))),
+        (size, size, tuple(range(1, bits)) + (0,)),
+        (2 * size, size, tuple(range(bits))),
+        (3 * size, tail, tuple(range(bits))),
+    ]
+    lows = {}
+
+    def copy_of(i, level, src, rows, dst, dst_rows, k):
+        return pltpu.make_async_remote_copy(
+            src_ref=src.at[rows, :],
+            dst_ref=dst.at[dst_rows, :],
+            send_sem=send_sem.at[i, level],
+            recv_sem=recv_sem.at[i, level],
+            device_id=partner(k),
+            device_id_type=pl.DeviceIdType.MESH,
+        )
+
+    flying = {}
+
+    def span(start, rows):
+        return pl.ds(pl.multiple_of(start, 16), rows)
+
+    def start_level(i, level):
+        base, rows, order = chunks[i]
+        if level < bits:
+            k = order[level]
+            low = lows.get(i, base)
+            part = rows >> (level + 1)
+            keep = low + bit_of(k) * part
+            give = low + (1 - bit_of(k)) * part
+            stage[span(give, part), :] = acc[span(give, part), :].astype(BF16)
+            where = base + rows - (rows >> level)
+            copy = copy_of(i, level, stage, span(give, part), land, span(where, part), k)
+            lows[i] = keep
+            flying[i] = (copy, keep, where, part)
+        else:
+            back = 2 * bits - 1 - level
+            k = order[back]
+            part = rows >> (back + 1)
+            low = lows[i]
+            copy = copy_of(i, level, out, span(low, part), out, span(low, part), k)
+            lows[i] = low - bit_of(k) * part
+            flying[i] = (copy, low, None, part)
+        copy.start()
+
+    def end_level(i, level):
+        copy, low, where, part = flying[i]
+        copy.wait()
+        if level < bits:
+            total = acc[span(low, part), :] + land[span(where, part), :].astype(F32)
+            acc[span(low, part), :] = total
+            if level == bits - 1:
+                out[span(low, part), :] = total.astype(BF16)
+
+    acc[span(r * chan, chan), :] = g_out[0:chan, :]
+    acc[span((1 - r) * chan, chan), :] = g_out[chan : 2 * chan, :]
+    if size > 2 * chan:
+        acc[2 * chan : size, :] = jnp.zeros((size - 2 * chan, chan), F32)
+    start_level(0, 0)
+    norm[...] = jnp.zeros_like(norm)
+    for i in range(DN_PARTS):
+        rows = slice(i * cut, (i + 1) * cut)
+        dn_rows[i].wait()
+        part = (dn_own[rows, :].astype(F32) + dn_land[rows, :].astype(F32)).astype(BF16)
+        dn_sum[rows, :] = part
+        dn_cols[i].start()
+        norm[...] += fold8(part.astype(F32) * hid[rows, :].astype(F32))
+    row_copy.wait()
+    for i in (1, 2):
+        lo = (i - 1) * chan
+        acc[span(i * size + mine, half), :] = g_cat[0:half, lo : lo + chan]
+        acc[span(i * size + other, half), :] = row_land[0:half, lo : lo + chan].astype(F32)
+        if size > 2 * half:
+            acc[i * size + 2 * half : (i + 1) * size, :] = jnp.zeros((size - 2 * half, chan), F32)
+        if i == 1:
+            start_level(1, 0)
+    misc = 3 * size
+    lo = 2 * chan
+    state = g_cat[0:half, lo : lo + 256] + row_land[0:half, lo : lo + 256].astype(F32)
+    norm_row = jnp.sum(norm[...], axis=0, keepdims=True)
+    norm_rows = jnp.concatenate(
+        [norm_row[:, 0:256], norm_row[:, 256:half], jnp.zeros((1, 512 - half), F32)], axis=1
+    )
+    extra = small_row[...] + row_land[half : half + 16, 0:256].astype(F32)
+    extra = jnp.concatenate([extra[0:8], norm_rows[:, 0:256], norm_rows[:, 256:512], jnp.zeros((6, 256), F32)])
+    acc[misc : misc + half, 0:256] = state
+    acc[misc + half : misc + half + 16, 0:256] = extra
+    col_send[0:half, :] = state.astype(BF16)
+    col_send[half : half + 16, :] = extra.astype(BF16)
+    col_copy = pair_copy(col_send, col_land, pair_send.at[1], pair_recv.at[1], to_col)
+    col_copy.start()
+    start_level(2, 0)
+    lo = 2 * chan + 256
+    acc[misc : misc + half, 256:384] = jnp.concatenate(
+        [g_cat[0:half, lo : lo + 64], row_land[0:half, lo : lo + 64].astype(F32)], axis=1
+    )
+    acc[misc + half : misc + half + 16, 256:384] = jnp.zeros((16, 128), F32)
+    acc[misc + half + 16 : misc + half + 32, :] = small_own[...]
+    if tail > half + 32:
+        acc[misc + half + 32 : misc + tail, :] = jnp.zeros((tail - half - 32, chan), F32)
+    rs_row.wait()
+    rs_out[...] = rs_in[...] + rs_land[0]
+    rs_col.start()
+    for i in (0, 1):
+        end_level(i, 0)
+        start_level(i, 1)
+    col_copy.wait()
+    acc[misc : misc + half + 16, 0:256] = (
+        col_send[...].astype(F32) + col_land[...].astype(F32)
+    )
+    start_level(3, 0)
+    end_level(2, 0)
+    start_level(2, 1)
+    for level in range(1, 2 * bits):
+        for i in (0, 1):
+            end_level(i, level)
+            if level + 1 < 2 * bits:
+                start_level(i, level + 1)
+        end_level(3, level - 1)
+        start_level(3, level)
+        end_level(2, level)
+        if level + 1 < 2 * bits:
+            start_level(2, level + 1)
+    end_level(3, 2 * bits - 1)
+    rs_col.wait()
+    for copy in dn_cols:
+        copy.wait()
+    rs_out[...] = rs_out[...] + rs_land[1]
+
+
+def sum_over_dp(dp, g_cat, g_out, small_row, small_own, rs, hid, dn_own, dn_rec):
+    half = g_cat.shape[0] // 2
+    wide = g_cat.shape[1]
+    chan = g_out.shape[1]
+    rows = 3 * big_rows(dp, 2 * half) + big_rows(dp, half + 32)
+    bits = dp.bit_length() - 1
+    tokens = hid.shape[0]
+    vmem = pl.BlockSpec(memory_space=pltpu.VMEM)
+    hbm = pl.BlockSpec(memory_space=pl.ANY)
+    act = jax.ShapeDtypeStruct((tokens, half), BF16)
+    return pl.pallas_call(
+        functools.partial(sum_kernel, dp),
+        in_specs=[vmem] * 7 + [hbm],
+        out_specs=[vmem, vmem, hbm, vmem],
+        out_shape=[jax.ShapeDtypeStruct((rows, chan), BF16), act, act, jax.ShapeDtypeStruct(rs.shape, F32)],
+        scratch_shapes=[
+            pltpu.VMEM((rows, chan), F32),
+            pltpu.VMEM((rows, chan), BF16),
+            pltpu.VMEM((rows, chan), BF16),
+            pltpu.VMEM((half + 16, wide), BF16),
+            pltpu.VMEM((half + 16, wide), BF16),
+            pltpu.VMEM((half + 16, 256), BF16),
+            pltpu.VMEM((half + 16, 256), BF16),
+            pltpu.VMEM((tokens, half), BF16),
+            pltpu.VMEM((2,) + rs.shape, F32),
+            pltpu.VMEM((8, half), F32),
+            pltpu.SemaphoreType.DMA((4, 2 * bits)),
+            pltpu.SemaphoreType.DMA((4, 2 * bits)),
+            pltpu.SemaphoreType.DMA((4,)),
+            pltpu.SemaphoreType.DMA((4,)),
+            pltpu.SemaphoreType.DMA((2, DN_PARTS)),
+            pltpu.SemaphoreType.DMA((2, DN_PARTS)),
+        ],
+        compiler_params=pltpu.CompilerParams(collective_id=0, has_side_effects=True),
+        cost_estimate=pl.CostEstimate(flops=1_000_000, bytes_accessed=150_000_000, transcendentals=0),
+        name="sum_over_dp",
+    )(g_cat, g_out, small_row, small_own, rs, hid, dn_own, dn_rec)
+
+
 def swap(x, axis):
     return lax.ppermute(x, axis, SWAP)
 
@@ -396,6 +669,7 @@
     inner_width = 4 * chan
     heads = decay_log.shape[0]
     r = lax.axis_index("row")
+    dp = lax.axis_size("dp")
     seq_len = min(LEN, tokens)
     steps_per_seq = seq_len // STEP
     grid = tokens // STEP
@@ -446,7 +720,7 @@
     def arr(cols, dtype=F32):
         return jax.ShapeDtypeStruct((tokens, cols), dtype)
 
-    mixed, pre_gate, pre_value, conv_value, pre_shared, conv_shared, y_scan, states, rows = pl.pallas_call(
+    mixed, pre_gate, pre_value, conv_value, pre_shared, conv_shared, y_scan, states, rows, normed_t = pl.pallas_call(
         functools.partial(forward_kernel, steps_per_seq, width),
         grid=(grid,),
         in_specs=[
@@ -469,6 +743,7 @@
             blk(chan),
             blk(chan),
             pl.BlockSpec((24, STEP), lambda i: (0, i)),
+            pl.BlockSpec((width, STEP), lambda i: (0, i)),
         ],
         out_shape=[
             arr(chan, BF16),
@@ -480,12 +755,14 @@
             arr(chan),
             arr(chan, BF16),
             jax.ShapeDtypeStruct((24, tokens), F32),
+            jax.ShapeDtypeStruct((width, tokens), BF16),
         ],
         scratch_shapes=[
             pltpu.VMEM((128, chan), F32),
             pltpu.VMEM((STEP + 8, chan), F32),
             pltpu.VMEM((STEP + 8, 256), F32),
         ],
+        cost_estimate=pl.CostEstimate(flops=12_000_000_000, bytes_accessed=40_000_000, transcendentals=8_000_000),
         name="forward_core",
     )(hidden, hid_rec, gains, w_own, w_rec, vtap, stap, head_par)
 
@@ -571,6 +848,7 @@
             pltpu.VMEM((STEP, chan), F32),
             pltpu.VMEM((STEP, 256), F32),
         ],
+        cost_estimate=pl.CostEstimate(flops=24_000_000_000, bytes_accessed=60_000_000, transcendentals=8_000_000),
         name="backward_core",
     )(
         cotangent,
@@ -595,63 +873,55 @@
         sel,
     )
 
-    rs = rsum[0]
-    rs = rs + swap(rs, "row")
-    rs = rs + swap(rs, "col")
-    dn_sum = (dn_own.astype(F32) + swap(dn_rec, "row").astype(F32)).astype(BF16)
-    d_normed = dn_sum.astype(F32) + swap(dn_sum, "col").astype(F32)
+    g_cat = dot(normed_t, p_all)
+    vsum = jnp.sum(acc_v.reshape(7, 8, chan), axis=1)
+    ssum = jnp.sum(acc_s.reshape(5, 8, 256), axis=1)
+    hsum = jnp.sum(acc_h.reshape(2, 8, 128), axis=2)
+    small_row = jnp.pad(ssum, ((0, 11), (0, 0)))
+    small_own = jnp.concatenate(
+        [vsum, jnp.pad(hsum.reshape(1, 16), ((0, 0), (0, chan - 16))), jnp.zeros((8, chan), F32)], axis=0
+    )
+    g_out = jnp.concatenate([g_out_own, g_out_rec], axis=0)
+    out, dn_sum, dn_col, rs = sum_over_dp(
+        dp, g_cat, g_out, small_row, small_own, rsum, hidden, dn_own, dn_rec
+    )
+    size, misc = big_rows(dp, 2 * half), 3 * big_rows(dp, 2 * half)
+
+    def side_by_side(start):
+        return jnp.concatenate([out[start : start + half], out[start + half : start + 2 * half]], axis=1).astype(F32)
+
+    g_output = out[0 : 2 * chan].astype(F32)
+    g_gate = side_by_side(size)
+    g_value = side_by_side(2 * size)
+    g_state = out[misc : misc + half, 0:256].astype(F32)
+    s_own = out[misc : misc + half, 256 : 256 + heads].astype(F32)
+    s_rec = out[misc : misc + half, 320 : 320 + heads].astype(F32)
+    g_step = jnp.where(r == 0, jnp.concatenate([s_own, s_rec], axis=1), jnp.concatenate([s_rec, s_own], axis=1))
+    small = out[misc + half : misc + half + 32].astype(F32)
+    g_norm = small[8:10, 0:256].reshape(512)[0:half]
+    d_normed = dn_sum.astype(F32) + dn_col.astype(F32)
     recip = rows[16]
     hidden_grad = (
-        cot32 + d_normed * input_gain - (rs * recip * recip / width)[:, None] * hidden32
-    )
-    g_norm = jnp.sum(d_normed * hidden32, axis=0)
-
-    normed = (hidden32 * input_gain).astype(BF16)
-    normed_rec = (hid_rec.astype(F32) * gains[1]).astype(BF16)
-    g_own = dot_tn(normed, p_all)
-    g_other = swap(dot_tn(normed_rec, p_all), "row")
-
-    def arrange(mine, theirs, axis):
-        first = jnp.where(r == 0, mine, theirs)
-        second = jnp.where(r == 0, theirs, mine)
-        return jnp.concatenate([first, second], axis=axis)
-
-    g_gate = arrange(g_own[:, 0:chan], g_other[:, 0:chan], 1)
-    g_value = arrange(g_own[:, chan : 2 * chan], g_other[:, chan : 2 * chan], 1)
-    g_state = g_own[:, 2 * chan : 2 * chan + 256] + g_other[:, 2 * chan : 2 * chan + 256]
-    s0 = 2 * chan + 256
-    g_step = arrange(g_own[:, s0 : s0 + heads], g_other[:, s0 : s0 + heads], 1)
-    g_output = arrange(g_out_own, g_out_rec, 0)
-
-    vsum = jnp.sum(acc_v.reshape(7, 8, chan), axis=1)
-    ssum = jnp.sum(acc_s.reshape(5, 8, 256), axis=1)
-    hsum = jnp.sum(acc_h.reshape(2, 8, 128), axis=2)[:, 0:heads]
-    g_skip = jnp.sum(vsum[5].reshape(heads, chan // heads), axis=1)
-    shared_all = jnp.concatenate([g_state, jnp.pad(ssum, ((0, 3), (0, 0)))], axis=0)
-    shared_all = shared_all + swap(shared_all, "col")
-    g_state = shared_all[0:half]
-    s_part = shared_all[half : half + 5]
-    s_part = s_part + swap(s_part, "row")
-    reduced = lax.psum(
-        (
-            g_gate,
-            g_value,
-            g_step,
-            g_state,
-            vsum[0:4],
-            vsum[4],
-            s_part[0:4],
-            s_part[4],
-            hsum[0],
-            hsum[1],
-            g_skip,
-            g_norm,
-            vsum[6],
-            g_output,
-        ),
-        "dp",
-    )
-    return (result, hidden_grad) + tuple(reduced)
+        cot32 + d_normed * input_gain - (rs[0] * recip * recip / width)[:, None] * hidden32
+    )
+    return (
+        result,
+        hidden_grad,
+        g_gate,
+        g_value,
+        g_step,
+        g_state,
+        small[16:20],
+        small[20],
+        small[0:4, 0:256],
+        small[4, 0:256],
+        small[23, 0:heads],
+        small[23, 8 : 8 + heads],
+        jnp.sum(small[21].reshape(heads, chan // heads), axis=1),
+        g_norm,
+        small[22],
+        g_output,
+    )
 
 
 def solution(mesh):

time: 286 us -> 219 us (0.77)
  Pallas kernels: 59.4 us -> 153 us
  waiting for transfers between devices: 89.4 us -> 2.22 us
  blocking collectives: 39.9 us -> 0 us
  between operations: 14.5 us -> 0.94 us
  local copies, waits for them, and re-layouts: 26.1 us -> 18.3 us
  starting transfers between devices: 11.2 us -> 4.8 us
  other arithmetic: 29.2 us -> 24.7 us
    pallas_call x0 -> x1, Pallas kernels: none -> 93.4 us  [sum_over_dp(): pl.pallas_call(functools.partial(sum_kernel, dp), in_specs=[vmem] * 7 + [...]
    ppermute x16 -> x9, waiting for transfers between devices: 60.8 us -> 2.22 us  [swap(): return lax.ppermute(x, axis, SWAP)]
    psum x1 -> x0, blocking collectives: 39.9 us -> none  [body(): lax.psum((g_gate, g_value, g_step, g_state, vsum[0:4], vsum[4], s_part[0:...]
    psum x1 -> x0, waiting for transfers between devices: 28.5 us -> none  [body(): lax.psum((g_gate, g_value, g_step, g_state, vsum[0:4], vsum[4], s_part[0:...]
    unnamed x80 -> x54, local copies, waits for them, and re-layouts: 9.98 us -> 2.54 us
    ppermute x16 -> x9, starting transfers between devices: 11.1 us -> 4.8 us  [swap(): return lax.ppermute(x, axis, SWAP)]
    dot_general x4 -> x2, matrix products: 12 us -> 6.13 us  [dot_tn(): lax.dot_general(a, b, (((0,), (0,)), ((), ())), preferred_element_type=F32)]
    reduce_sum x3 -> x2, other arithmetic: 7.87 us -> 2.12 us  [the longest x1 1.31 us: body(): jnp.sum(small[21].reshape(heads, chan // heads), axis=1)]
  transfers between devices with their start and end apart: 17 -> 9, of which waited for: 6 -> 3; matrix products, arithmetic and copies ran while one was open for 19% -> 23% of each run, Pallas kernels for 0% -> 60%
where the time goes in v2:
time: 219 us
  Pallas kernels  153 us (70%)
  other arithmetic  24.7 us (11%)
  local copies, waits for them, and re-layouts  18.3 us (8%)
  matrix products  14.8 us (7%)
  starting transfers between devices  4.8 us (2%)
  waiting for transfers between devices  2.22 us (1%)
    pallas_call x1, Pallas kernels, sum_over_dp(): pl.pallas_call(functools.partial(sum_kernel, dp), in_specs=[vmem] * 7 + [...  93.4 us
    pallas_call x1, Pallas kernels, body(): pl.pallas_call(functools.partial(backward_kernel, steps_per_seq), grid=(g...  37.9 us
    pallas_call x1, Pallas kernels, body(): pl.pallas_call(functools.partial(forward_kernel, steps_per_seq, width), g...  21.5 us
    dot_general x3, matrix products, dot(): return jnp.dot(a, b, preferred_element_type=F32)  8.71 us
    dot_general x2, matrix products, dot_tn(): lax.dot_general(a, b, (((0,), (0,)), ((), ())), preferred_element_type=F32)  6.13 us
    ppermute x9, starting transfers between devices, swap(): return lax.ppermute(x, axis, SWAP)  4.8 us
  transfers between devices with their start and end apart: 9, of which 3 were waited for; matrix products, arithmetic and copies ran while one was open for 23% of the time, Pallas kernels for 60%

profile of v2, /device:TPU:0, one launch (start us, length us, event | category | flops | bytes accessed | tf_op | source)
XLA Modules:
  0.0 218.5 jit_solution(1787427442496053472)
XLA Ops:
  3.9 1.4 constant_dynamic-slice_fusion.3
  5.3 1.1 fusion.15
  10.4 21.5 %forward_core.1 = (bf16[2048,384]{1,0:T(8,128)(2,1)}, f32[2048,384]{1,0:T(8,128)}, f32[2048,384]{1,0:T(8,128)}, f32[2048,384]{1,0:T(8,128)}, f32[2048,256]{1,0:T...) custom-call(bf16[2048,384]{1,0:T(8,128)(2,1)} %hid.1, ...), custom_call_target="tpu_custom_call" | custom-call | flops 12000000000 | bytes 40000000 | tf_op jit(solution)/shard_map/forward_core/pallas_call | solution.py:723
  32.8 1.8 fusion.2
  35.6 1.1 fusion.9
  37.6 1.6 fusion.4
  40.5 2.7 %collective-permute-start.5 = (f32[2,2048]{1,0:T(2,128)S(1)}, f32[2,2048]{1,0:T(2,128)S(1)}, u32[]{:S(2)}, u32[]{:S(2)}) collective-permute-start(f32[2,2048]{1,0:T(2,128)S(1)} %fusion.30), channel_id=1, source_target_pairs={{0,1},{1,0},{2,3},{3,2},{4,5},{5,4},{6,7},{7,6},{8,9},{9,8},{10,11... | collective-permute-start | bytes 49160 | tf_op jit(solution)/shard_map/ppermute | solution.py:645
  45.7 3.4 %fusion.10 = f32[384,384]{1,0:T(8,128)} fusion(bf16[2048,384]{1,0:T(8,128)(2,1)} %get-tuple-element.37.mixed, f32[384]{0:T(512)S(1)} %convert_element_type.77, bf16[2048,384]{1,0:T(8,128)(2,1)S(1)} %copy-done.1, f32[2048]{0:T(1024)S(1)} %bitcast.30), kind=kOutput, calls=%fused_computation.20 | convolution fusion | flops 608698368 | bytes 3745280 | tf_op jit(solution)/shard_map/dot_general | solution.py:29
  49.1 37.9 %backward_core.1 = (bf16[2048,1152]{1,0:T(8,128)(2,1)}, bf16[2048,384]{1,0:T(8,128)(2,1)}, bf16[2048,384]{1,0:T(8,128)(2,1)}, f32[8,2048]{1,0:T(8,128)}, f32[56,...) custom-call(bf16[2048,384]{1,0:T(8,128)(2,1)} %cot_own.1, bf16[2048,384]{1,0:T(8,128)(2,1)} %collective-permute-done.7.cot_rec, ...), custom_call_target="tpu_custom_call" | custom-call | flops 24000000000 | bytes 60000000 | tf_op jit(solution)/shard_map/backward_core/pallas_call | solution.py:801
  90.2 2.7 %fusion.8 = f32[384,384]{1,0:T(8,128)S(1)} fusion(bf16[2048,384]{1,0:T(8,128)(2,1)} %copy-done.6, f32[384]{0:T(512)S(1)} %get-tuple-element.101, bf16[2048,384]{1,0:T(8,128)(2,1)S(1)} %copy-done.2, f32[2048]{0:T(1024)S(1)} %bitcast.31), kind=kOutput, calls=%fused_computation.18 | convolution fusion | flops 608698368 | bytes 3745280 | tf_op jit(solution)/shard_map/dot_general | solution.py:29
  92.9 1.1 pad_maximum_fusion.g_out
  94.3 6.0 %fusion.33.g_cat = f32[768,1152]{1,0:T(8,128)} fusion(bf16[768,2048]{1,0:T(8,128)(2,1)S(1)} %copy-done.24, bf16[2048,1152]{1,0:T(8,128)(2,1)S(1)} %copy-done.23), kind=kOutput, calls=%fused_computation.85 | convolution fusion | flops 3623878656 | bytes 11403264 | tf_op jit(solution)/shard_map/dot_general | solution.py:21
  100.9 93.4 %sum_over_dp.1 = (bf16[2816,384]{1,0:T(8,128)(2,1)}, bf16[2048,384]{1,0:T(8,128)(2,1)}, bf16[2048,384]{1,0:T(8,128)(2,1)}, f32[8,2048]{1,0:T(8,128)}) custom-call(f32[768,1152]{1,0:T(8,128)} %fusion.33.g_cat, f32[768,384]{1,0:T(8,128)} %pad_maximum_fusion.g_out, f32[16,256]{1,0:T(8,128)} %pad.26.small_row, f32[16,384]{1,0:T(8,128)} %fusion.18.small_own, ...), custom_call_target="tpu_custom_call" | custom-call | flops 1000000 | bytes 150000000 | tf_op jit(solution)/shard_map/sum_over_dp/pallas_call | solution.py:615
  198.5 1.4 slice.79
  200.5 1.3 reshape_squeeze.3
  201.9 1.3 reduce_sum.59
  204.0 1.4 maximum_select_fusion
  205.4 1.3 fusion.32
  206.8 1.1 maximum_convert_fusion.1
  207.9 1.1 maximum_convert_fusion
  209.0 1.6 slice_bitcast_fusion.1
  210.6 1.7 slice_convert_fusion.1
  212.3 2.2 slice_convert_fusion
  214.4 4.1 %fusion.1 = (f32[2048,384]{1,0:T(8,128)}, bf16[2048,384]{1,0:T(8,128)(2,1)}) fusion(bf16[2048,384]{1,0:T(8,128)(2,1)S(1)} %copy-done, bf16[2048,384]{1,0:T(8,128)(2,1)S(1)} %copy-done.2, bf16[2048,384]{1,0:T(8,128)(2,1)S(1)} %copy-done.5, bf16[2048,384]{1,0:T(8,128)(2,1)S(1)} %copy-done.4, f32[2048]{0:T(1024)S(1)} %fusion.22, f32[384]{0:T(512)S(1)} %copy-done.13, ...), kind=kLoop, calls=%fused_computation.8 | loop fusion | flops 11796480 | bytes 14173696 | tf_op jit(solution)/shard_map/sub | solution.py:905
  (116 shorter events, 23.4 us)
Async XLA Ops:
  0.6 4.7 %copy-start.10 = (bf16[384,256]{1,0:T(8,128)(2,1)S(1)}, bf16[384,256]{1,0:T(8,128)(2,1)}, u32[]{:S(2)}) copy-start(bf16[384,256]{1,0:T(8,128)(2,1)} %param.20) | copy-start | bytes 589828
  2.1 6.4 %collective-permute-start.1 = (f32[2,384]{1,0:T(2,128)S(1)}, f32[2,384]{1,0:T(2,128)S(1)}, u32[]{:S(2)}, u32[]{:S(2)}) collective-permute-start(f32[2,384]{1,0:T(2,128)S(1)} %pad_maximum_fusion.4), channel_id=1, source_target_pairs={{0,2},{2,0},{1,3},{3,1},{4,6},{6,4},{5,7},{7,5},{8,10},{10,8},{9,1... | collective-permute-start | bytes 9224 | tf_op jit(solution)/shard_map/ppermute | solution.py:645
  2.6 6.6 %collective-permute-start = (bf16[2048,384]{1,0:T(8,128)(2,1)}, bf16[2048,384]{1,0:T(8,128)(2,1)S(1)}, u32[]{:S(2)}, u32[]{:S(2)}) collective-permute-start(bf16[2048,384]{1,0:T(8,128)(2,1)} %hid.1), channel_id=1, source_target_pairs={{0,2},{2,0},{1,3},{3,1},{4,6},{6,4},{5,7},{7,5},{8,10},{10,8},{9,1... | collective-permute-start | bytes 4718600 | tf_op jit(solution)/shard_map/ppermute | solution.py:645
  5.3 2.6 %copy-start.14 = (f32[4,384]{1,0:T(4,128)S(1)}, f32[4,384]{1,0:T(4,128)}, u32[]{:S(2)}) copy-start(f32[4,384]{1,0:T(4,128)} %param.21) | copy-start | bytes 18436
  6.4 2.8 %collective-permute-start.2 = (bf16[384,1152]{1,0:T(8,128)(2,1)S(1)}, bf16[384,1152]{1,0:T(8,128)(2,1)}, u32[]{:S(2)}, u32[]{:S(2)}) collective-permute-start(bf16[384,1152]{1,0:T(8,128)(2,1)S(1)} %get-tuple-element.95), channel_id=1, source_target_pairs={{0,2},{2,0},{1,3},{3,1},{4,6},{6,4},{5,7},{7,5},{8,10},{10,8},{9,1... | collective-permute-start | bytes 2654216 | tf_op jit(solution)/shard_map/ppermute | solution.py:645
  10.4 21.8 %copy-start.8 = (bf16[768,384]{1,0:T(8,128)(2,1)S(1)}, bf16[768,384]{1,0:T(8,128)(2,1)}, u32[]{:S(2)}) copy-start(bf16[768,384]{1,0:T(8,128)(2,1)} %param.30) | copy-start | bytes 1769476
  10.4 22.3 %copy-start.1 = (bf16[2048,384]{1,0:T(8,128)(2,1)S(1)}, bf16[2048,384]{1,0:T(8,128)(2,1)}, u32[]{:S(2)}) copy-start(bf16[2048,384]{1,0:T(8,128)(2,1)} %cot_own.1) | copy-start | bytes 4718596
  10.4 22.4 %copy-start.16 = (bf16[384]{0:T(512)(128)(2,1)S(1)}, bf16[384]{0:T(512)(128)(2,1)}, u32[]{:S(2)}) copy-start(bf16[384]{0:T(512)(128)(2,1)} %param.29) | copy-start | bytes 2308
  31.9 3.7 %collective-permute-start.3 = (bf16[2048,384]{1,0:T(8,128)(2,1)}, bf16[2048,384]{1,0:T(8,128)(2,1)S(1)}, u32[]{:S(2)}, u32[]{:S(2)}) collective-permute-start(bf16[2048,384]{1,0:T(8,128)(2,1)} %get-tuple-element.37.mixed), channel_id=1, source_target_pairs={{0,2},{2,0},{1,3},{3,1},{4,6},{6,4},{5,7},{7,5},{8,10},{10,8},{9,1... | collective-permute-start | bytes 4718600 | tf_op jit(solution)/shard_map/ppermute | solution.py:645
  32.2 4.6 %copy-start.7 = (bf16[384,384]{1,0:T(8,128)(2,1)}, bf16[384,384]{1,0:T(8,128)(2,1)S(1)}, u32[]{:S(2)}) copy-start(bf16[384,384]{1,0:T(8,128)(2,1)S(1)} %get-tuple-element.90.wo_own) | copy-start | bytes 884740
  32.2 16.9 %collective-permute-start.8 = (bf16[384,384]{1,0:T(8,128)(2,1)S(1)}, bf16[384,384]{1,0:T(8,128)(2,1)}, u32[]{:S(2)}, u32[]{:S(2)}) collective-permute-start(bf16[384,384]{1,0:T(8,128)(2,1)S(1)} %get-tuple-element.89), channel_id=1, source_target_pairs={{0,2},{2,0},{1,3},{3,1},{4,6},{6,4},{5,7},{7,5},{8,10},{10,8},{9,1... | collective-permute-start | bytes 884744 | tf_op jit(solution)/shard_map/ppermute | solution.py:645
  32.6 16.4 %collective-permute-start.7 = (bf16[2048,384]{1,0:T(8,128)(2,1)S(1)}, bf16[2048,384]{1,0:T(8,128)(2,1)}, u32[]{:S(2)}, u32[]{:S(2)}) collective-permute-start(bf16[2048,384]{1,0:T(8,128)(2,1)S(1)} %copy-done.1), channel_id=1, source_target_pairs={{0,2},{2,0},{1,3},{3,1},{4,6},{6,4},{5,7},{7,5},{8,10},{10,8},{9,1... | collective-permute-start | bytes 4718600 | tf_op jit(solution)/shard_map/ppermute | solution.py:645
  39.2 1.2 collective-permute-start.4
  40.5 4.4 %collective-permute-start.5 = (f32[2,2048]{1,0:T(2,128)S(1)}, f32[2,2048]{1,0:T(2,128)S(1)}, u32[]{:S(2)}, u32[]{:S(2)}) collective-permute-start(f32[2,2048]{1,0:T(2,128)S(1)} %fusion.30), channel_id=1, source_target_pairs={{0,1},{1,0},{2,3},{3,2},{4,5},{5,4},{6,7},{7,6},{8,9},{9,8},{10,11... | collective-permute-start | bytes 49160 | tf_op jit(solution)/shard_map/ppermute | solution.py:645
  44.7 169.7 %collective-permute-start.6 = (bf16[2048,384]{1,0:T(8,128)(2,1)S(1)}, bf16[2048,384]{1,0:T(8,128)(2,1)}, u32[]{:S(2)}, u32[]{:S(2)}) collective-permute-start(bf16[2048,384]{1,0:T(8,128)(2,1)S(1)} %get-tuple-element.80), channel_id=1, source_target_pairs={{0,1},{1,0},{2,3},{3,2},{4,5},{5,4},{6,7},{7,6},{8,9},{9,8},{10,11... | collective-permute-start | bytes 4718600 | tf_op jit(solution)/shard_map/ppermute | solution.py:645
  49.1 41.0 %copy-start.2 = (bf16[2048,384]{1,0:T(8,128)(2,1)S(1)}, bf16[2048,384]{1,0:T(8,128)(2,1)}, u32[]{:S(2)}) copy-start(bf16[2048,384]{1,0:T(8,128)(2,1)} %cot_own.1) | copy-start | bytes 4718596
  90.1 2.8 %copy-start.9 = (f32[384,384]{1,0:T(8,128)S(1)}, f32[384,384]{1,0:T(8,128)}, u32[]{:S(2)}) copy-start(f32[384,384]{1,0:T(8,128)} %fusion.10) | copy-start | bytes 1769476
  90.1 3.9 %copy-start.23 = (bf16[2048,1152]{1,0:T(8,128)(2,1)S(1)}, bf16[2048,1152]{1,0:T(8,128)(2,1)}, u32[]{:S(2)}) copy-start(bf16[2048,1152]{1,0:T(8,128)(2,1)} %get-tuple-element.47) | copy-start | bytes 14155780
  90.1 4.1 %copy-start.24 = (bf16[768,2048]{1,0:T(8,128)(2,1)S(1)}, bf16[768,2048]{1,0:T(8,128)(2,1)}, u32[]{:S(2)}) copy-start(bf16[768,2048]{1,0:T(8,128)(2,1)} %get-tuple-element.38) | copy-start | bytes 9437188
  206.8 3.8 %copy-start.12 = (f32[1,2048]{1,0:T(1,128)S(1)}, f32[1,2048]{1,0:T(1,128)}, u32[]{:S(2)}) copy-start(f32[1,2048]{1,0:T(1,128)} %slice.79) | copy-start | bytes 24580
  206.8 7.6 %copy-start.5 = (bf16[2048,384]{1,0:T(8,128)(2,1)S(1)}, bf16[2048,384]{1,0:T(8,128)(2,1)}, u32[]{:S(2)}) copy-start(bf16[2048,384]{1,0:T(8,128)(2,1)} %get-tuple-element.55) | copy-start | bytes 4718596
  207.9 6.5 %copy-start = (bf16[2048,384]{1,0:T(8,128)(2,1)S(1)}, bf16[2048,384]{1,0:T(8,128)(2,1)}, u32[]{:S(2)}) copy-start(bf16[2048,384]{1,0:T(8,128)(2,1)} %hid.1) | copy-start | bytes 4718596
  207.9 6.5 %copy-start.4 = (bf16[2048,384]{1,0:T(8,128)(2,1)S(1)}, bf16[2048,384]{1,0:T(8,128)(2,1)}, u32[]{:S(2)}) copy-start(bf16[2048,384]{1,0:T(8,128)(2,1)} %get-tuple-element.54) | copy-start | bytes 4718596
  207.9 6.6 %copy-start.13 = (f32[384]{0:T(512)S(1)}, f32[384]{0:T(512)}, u32[]{:S(2)}) copy-start(f32[384]{0:T(512)} %param.28) | copy-start | bytes 4612
  (10 other events, 18.3 us)

commit v3 on v2

--- a/solution.py
+++ b/solution.py
@@ -87,7 +87,11 @@
     vtap,
     stap,
     head_par,
+    wo_own,
+    wo_rec,
     mixed_out,
+    po_own,
+    po_rec,
     pre_gate_out,
     pre_value_out,
     conv_value_out,
@@ -186,6 +190,11 @@
             state[:, pl0:pl1] = held * jnp.exp(last) + dot(b_t, tail)
             y = y + vtap[5:6, pl0:pl1] * xs
             mixed_out[lo:hi, pl0:pl1] = (y * sg[lo:hi, pl0:pl1]).astype(BF16)
+    mix = mixed_out[...].astype(F32)
+    weighted = (mix * vtap[6:7, :]).astype(BF16)
+    po_own[...] = dot(weighted, wo_own[...]).astype(BF16)
+    po_rec[...] = dot(weighted, wo_rec[...]).astype(BF16)
+    rows_out[24:32, :] = head_sums(jnp.ones((16, chan), BF16), mix * mix)
 
 
 def backward_kernel(
@@ -210,6 +219,8 @@
     stap,
     head_par,
     sel_ref,
+    hid_own,
+    hid_rec,
     p_out,
     dn_own,
     dn_rec,
@@ -217,6 +228,9 @@
     acc_v,
     acc_s,
     acc_h,
+    acc_n,
+    go_own,
+    go_rec,
     grad,
     vbuf,
     sbuf,
@@ -231,6 +245,9 @@
         acc_v[...] = jnp.zeros_like(acc_v)
         acc_s[...] = jnp.zeros_like(acc_s)
         acc_h[...] = jnp.zeros_like(acc_h)
+        acc_n[...] = jnp.zeros_like(acc_n)
+        go_own[...] = jnp.zeros_like(go_own)
+        go_rec[...] = jnp.zeros_like(go_rec)
 
     @pl.when(pl.program_id(0) % steps_per_seq == 0)
     def _():
@@ -240,13 +257,16 @@
 
     tcol = jnp.transpose(jnp.concatenate([trow[...], rows_in[16:24, :]], axis=0))
     scale = tcol[:, 0:1]
-    coef = tcol[:, 1:2]
-    recip = tcol[:, 8:9]
+    coef = tcol[:, 8:9]
+    recip = tcol[:, 16:17]
     s0 = (cot_own[...].astype(F32) * scale).astype(BF16)
     s1 = (cot_rec[...].astype(F32) * scale).astype(BF16)
     d_weighted = dot_nt(s0, wo_own[...]) + dot_nt(s1, wo_rec[...])
     mix = mixed[...].astype(F32)
     acc_v[48:56, :] += fold8(d_weighted * mix)
+    weighted_t = jnp.transpose((mix * vtap[6:7, :]).astype(BF16))
+    go_own[...] += dot(weighted_t, s0)
+    go_rec[...] += dot(weighted_t, s1)
     d_mixed = d_weighted * vtap[6:7, :] - coef * mix
     gate = pre_gate[...]
     sig = sigmoid(gate)
@@ -369,8 +389,10 @@
     rsum_out[...] += head_sums(ones, d_gate * gate + d_value * pv)
     rsum_out[...] += head_sums(ones[:, 0:256], d_shared * ps)
     pb = p_out[...]
-    dn_own[...] = dot_nt(pb, w_own[...]).astype(BF16)
-    dn_rec[...] = dot_nt(pb, w_rec[...]).astype(BF16)
+    for n, (hid, weight, dn) in enumerate(((hid_own, w_own, dn_own), (hid_rec, w_rec, dn_rec))):
+        part = dot_nt(pb, weight[...])
+        dn[...] = part.astype(BF16)
+        acc_n[8 * n : 8 * n + 8, :] += fold8(part * hid[...].astype(F32))
 
 
 def unit_rows(dp):
@@ -379,16 +401,108 @@
 
 def big_rows(dp, rows):
     return pl.cdiv(rows, unit_rows(dp)) * unit_rows(dp)
+
+
+def remote(src, dst, send, recv, target):
+    return pltpu.make_async_remote_copy(
+        src_ref=src,
+        dst_ref=dst,
+        send_sem=send,
+        recv_sem=recv,
+        device_id=target,
+        device_id_type=pl.DeviceIdType.MESH,
+    )
+
+
+def greet(targets):
+    barrier = pltpu.get_barrier_semaphore()
+    for target in targets:
+        pl.semaphore_signal(barrier, inc=1, device_id=target, device_id_type=pl.DeviceIdType.MESH)
+    pl.semaphore_wait(barrier, len(targets))
+
+
+def mid_kernel(
+    inner_width,
+    rows_in,
+    cot,
+    po_own,
+    po_rec,
+    proj_out,
+    trow,
+    po_land,
+    sums,
+    sums_land,
+    po_send_sem,
+    po_recv_sem,
+    send_sem,
+    recv_sem,
+):
+    r = lax.axis_index("row")
+    c = lax.axis_index("col")
+    targets = [{"row": 1 - r}, {"col": 1 - c}, {"row": 1 - r, "col": 1 - c}]
+    greet(targets)
+    tokens, half = cot.shape
+    cut = tokens // DN_PARTS
+    copies = []
+    for i in range(DN_PARTS):
+        rows = pl.ds(i * cut, cut)
+        copy = remote(po_rec.at[rows, :], po_land.at[rows, :], po_send_sem.at[i], po_recv_sem.at[i], targets[0])
+        copy.start()
+        copies.append(copy)
+    ones = jnp.ones((16, half), BF16)
+    sums[0:8, :] = rows_in[24:32, :]
+    for i in range(DN_PARTS):
+        rows = slice(i * cut, (i + 1) * cut)
+        copies[i].wait()
+        part = po_own[rows, :].astype(F32) + po_land[rows, :].astype(F32)
+        proj_out[rows, :] = part.astype(BF16)
+        sums[8:16, rows] = head_sums(ones, part * cot[rows, :].astype(F32))
+    ends = []
+    for i, target in enumerate(targets):
+        copy = remote(sums, sums_land.at[i], send_sem.at[i], recv_sem.at[i], target)
+        copy.start()
+        ends.append(copy)
+    for copy in ends:
+        copy.wait()
+    total = (sums[...] + sums_land[0]) + (sums_land[1] + sums_land[2])
+    scale = lax.rsqrt(total[0:8] / inner_width + EPSILON)
+    trow[0:8, :] = scale
+    trow[8:16, :] = total[8:16] * (scale * scale * scale) / inner_width
+
+
+def mid_exchange(inner_width, rows, cot, po_own, po_rec):
+    tokens, half = cot.shape
+    vmem = pl.BlockSpec(memory_space=pltpu.VMEM)
+    return pl.pallas_call(
+        functools.partial(mid_kernel, inner_width),
+        in_specs=[vmem, vmem, vmem, pl.BlockSpec(memory_space=pl.ANY)],
+        out_specs=[vmem, vmem],
+        out_shape=[jax.ShapeDtypeStruct((tokens, half), BF16), jax.ShapeDtypeStruct((16, tokens), F32)],
+        scratch_shapes=[
+            pltpu.VMEM((tokens, half), BF16),
+            pltpu.VMEM((16, tokens), F32),
+            pltpu.VMEM((3, 16, tokens), F32),
+            pltpu.SemaphoreType.DMA((DN_PARTS,)),
+            pltpu.SemaphoreType.DMA((DN_PARTS,)),
+            pltpu.SemaphoreType.DMA((3,)),
+            pltpu.SemaphoreType.DMA((3,)),
+        ],
+        compiler_params=pltpu.CompilerParams(collective_id=1, has_side_effects=True),
+        cost_estimate=pl.CostEstimate(flops=1_000_000, bytes_accessed=20_000_000, transcendentals=0),
+        name="mid_exchange",
+    )(rows, cot, po_own, po_rec)
 
 
 def sum_kernel(
     dp,
     g_cat,
-    g_out,
-    small_row,
-    small_own,
+    go_own,
+    go_rec,
+    acc_v,
+    acc_s,
+    acc_h,
+    acc_n,
     rs_in,
-    hid,
     dn_own,
     dn_rec,
     out,
@@ -404,7 +518,6 @@
     col_land,
     dn_land,
     rs_land,
-    norm,
     send_sem,
     recv_sem,
     pair_send,
@@ -413,14 +526,16 @@
     dn_recv_sem,
 ):
     half = g_cat.shape[0] // 2
-    chan = g_out.shape[1]
+    chan = go_own.shape[0]
     wide = g_cat.shape[1]
     size = big_rows(dp, 2 * half)
-    tail = out.shape[0] - 3 * size
+    misc = 3 * size
+    tail = out.shape[0] - misc
     bits = dp.bit_length() - 1
     me = lax.axis_index("dp")
     r = lax.axis_index("row")
     c = lax.axis_index("col")
+    to_row, to_col = {"row": 1 - r}, {"col": 1 - c}
 
     def bit_of(k):
         return lax.rem(me // (1 << k), 2)
@@ -428,26 +543,26 @@
     def partner(k):
         return {"dp": me + (1 - 2 * bit_of(k)) * (1 << k)}
 
-    barrier = pltpu.get_barrier_semaphore()
-    for target in [partner(k) for k in range(bits)] + [{"row": 1 - r}, {"col": 1 - c}]:
-        pl.semaphore_signal(barrier, inc=1, device_id=target, device_id_type=pl.DeviceIdType.MESH)
-    pl.semaphore_wait(barrier, bits + 2)
-
-    other = pl.multiple_of((1 - r) * half, 128)
-    mine = pl.multiple_of(r * half, 128)
-    to_row, to_col = {"row": 1 - r}, {"col": 1 - c}
-
-    def pair_copy(src, dst, send, recv, target):
-        return pltpu.make_async_remote_copy(
-            src_ref=src,
-            dst_ref=dst,
-            send_sem=send,
-            recv_sem=recv,
-            device_id=target,
-            device_id_type=pl.DeviceIdType.MESH,
-        )
-
-    tokens = hid.shape[0]
+    def sum8(ref, n):
+        return jnp.sum(ref[8 * n : 8 * n + 8, :], axis=0, keepdims=True)
+
+    greet([partner(k) for k in range(bits)] + [to_row, to_col])
+
+    row_send[0:half, 0:wide] = g_cat[half : 2 * half, :].astype(BF16)
+    row_send[0:half, wide : wide + half] = go_rec[...].astype(BF16)
+    small = jnp.concatenate([sum8(acc_s, n) for n in range(5)] + [jnp.zeros((3, 256), F32)], axis=0)
+    norm_own, norm_rec = [
+        jnp.concatenate([sum8(acc_n, n), jnp.zeros((1, 512 - half), F32)], axis=1) for n in (0, 1)
+    ]
+    pad6 = jnp.zeros((6, 256), F32)
+    row_send[half : half + 16, 0:256] = jnp.concatenate(
+        [small, norm_rec[:, 0:256], norm_rec[:, 256:512], pad6], axis=0
+    ).astype(BF16)
+    row_send[half : half + 16, 256 : wide + half] = jnp.zeros((16, wide + half - 256), BF16)
+    row_copy = remote(row_send, row_land, pair_send.at[0], pair_recv.at[0], to_row)
+    row_copy.start()
+
+    tokens = dn_own.shape[0]
     cut = tokens // DN_PARTS
 
     def dn_copy(i, side):
@@ -456,46 +571,37 @@
             src, dst, target = dn_rec, dn_land, to_row
         else:
             src, dst, target = dn_sum, dn_col, to_col
-        return pair_copy(src.at[rows, :], dst.at[rows, :], dn_send_sem.at[side, i], dn_recv_sem.at[side, i], target)
+        return remote(src.at[rows, :], dst.at[rows, :], dn_send_sem.at[side, i], dn_recv_sem.at[side, i], target)
 
     dn_rows = [dn_copy(i, 0) for i in range(DN_PARTS)]
     dn_cols = [dn_copy(i, 1) for i in range(DN_PARTS)]
-    rs_row = pair_copy(rs_in, rs_land.at[0], pair_send.at[2], pair_recv.at[2], to_row)
-    rs_col = pair_copy(rs_out, rs_land.at[1], pair_send.at[3], pair_recv.at[3], to_col)
+    rs_row = remote(rs_in, rs_land.at[0], pair_send.at[2], pair_recv.at[2], to_row)
+    rs_col = remote(rs_out, rs_land.at[1], pair_send.at[3], pair_recv.at[3], to_col)
+    rs_row.start()
     for copy in dn_rows:
         copy.start()
-    rs_row.start()
-    row_send[0:half, :] = g_cat[half : 2 * half, :].astype(BF16)
-    row_send[half : half + 16, 0:256] = small_row[...].astype(BF16)
-    row_send[half : half + 16, 256:wide] = jnp.zeros((16, wide - 256), BF16)
-    row_copy = pair_copy(row_send, row_land, pair_send.at[0], pair_recv.at[0], to_row)
-    row_copy.start()
-
-    chunks = [
-        (0, size, tuple(range(bits))),
-        (size, size, tuple(range(1, bits)) + (0,)),
-        (2 * size, size, tuple(range(bits))),
-        (3 * size, tail, tuple(range(bits))),
+
+    orders = [
+        tuple(range(bits)),
+        tuple(range(1, bits)) + (0,),
+        tuple(range(bits)),
+        tuple(range(bits)),
     ]
+    bounds = [(0, size), (size, size), (2 * size, size), (misc, tail)]
     lows = {}
-
-    def copy_of(i, level, src, rows, dst, dst_rows, k):
-        return pltpu.make_async_remote_copy(
-            src_ref=src.at[rows, :],
-            dst_ref=dst.at[dst_rows, :],
-            send_sem=send_sem.at[i, level],
-            recv_sem=recv_sem.at[i, level],
-            device_id=partner(k),
-            device_id_type=pl.DeviceIdType.MESH,
-        )
-
     flying = {}
 
     def span(start, rows):
         return pl.ds(pl.multiple_of(start, 16), rows)
 
+    def copy_of(i, level, src, rows, dst, dst_rows, k):
+        return remote(
+            src.at[rows, :], dst.at[dst_rows, :], send_sem.at[i, level], recv_sem.at[i, level], partner(k)
+        )
+
     def start_level(i, level):
-        base, rows, order = chunks[i]
+        base, rows = bounds[i]
+        order = orders[i]
         if level < bits:
             k = order[level]
             low = lows.get(i, base)
@@ -525,76 +631,67 @@
             acc[span(low, part), :] = total
             if level == bits - 1:
                 out[span(low, part), :] = total.astype(BF16)
-
-    acc[span(r * chan, chan), :] = g_out[0:chan, :]
-    acc[span((1 - r) * chan, chan), :] = g_out[chan : 2 * chan, :]
-    if size > 2 * chan:
-        acc[2 * chan : size, :] = jnp.zeros((size - 2 * chan, chan), F32)
-    start_level(0, 0)
-    norm[...] = jnp.zeros_like(norm)
+        if level + 1 < 2 * bits:
+            start_level(i, level + 1)
+
+    mine = pl.multiple_of(r * half, 128)
+    other = pl.multiple_of((1 - r) * half, 128)
+
+    def fill(i, own, lo):
+        acc[span(i * size + mine, half), :] = own
+        acc[span(i * size + other, half), :] = row_land[0:half, lo : lo + chan].astype(F32)
+        if size > 2 * half:
+            acc[i * size + 2 * half : (i + 1) * size, :] = jnp.zeros((size - 2 * half, chan), F32)
+
+    for i in range(3):
+        acc_own = go_own[...] if i == 0 else g_cat[0:half, (i - 1) * chan : i * chan]
+        if i == 0:
+            row_copy.wait()
+        fill(i, acc_own, wide if i == 0 else (i - 1) * chan)
+        start_level(i, 0)
+        if i == 0:
+            lo = 2 * chan
+            state = g_cat[0:half, lo : lo + 256] + row_land[0:half, lo : lo + 256].astype(F32)
+            extra = jnp.concatenate([small, norm_own[:, 0:256], norm_own[:, 256:512], pad6], axis=0)
+            extra = extra + row_land[half : half + 16, 0:256].astype(F32)
+            col_send[0:half, :] = state.astype(BF16)
+            col_send[half : half + 16, :] = extra.astype(BF16)
+            col_copy = remote(col_send, col_land, pair_send.at[1], pair_recv.at[1], to_col)
+            col_copy.start()
+            rs_row.wait()
+            rs_out[...] = rs_in[...] + rs_land[0]
+            rs_col.start()
     for i in range(DN_PARTS):
         rows = slice(i * cut, (i + 1) * cut)
         dn_rows[i].wait()
-        part = (dn_own[rows, :].astype(F32) + dn_land[rows, :].astype(F32)).astype(BF16)
-        dn_sum[rows, :] = part
+        dn_sum[rows, :] = (dn_own[rows, :].astype(F32) + dn_land[rows, :].astype(F32)).astype(BF16)
         dn_cols[i].start()
-        norm[...] += fold8(part.astype(F32) * hid[rows, :].astype(F32))
-    row_copy.wait()
-    for i in (1, 2):
-        lo = (i - 1) * chan
-        acc[span(i * size + mine, half), :] = g_cat[0:half, lo : lo + chan]
-        acc[span(i * size + other, half), :] = row_land[0:half, lo : lo + chan].astype(F32)
-        if size > 2 * half:
-            acc[i * size + 2 * half : (i + 1) * size, :] = jnp.zeros((size - 2 * half, chan), F32)
-        if i == 1:
-            start_level(1, 0)
-    misc = 3 * size
-    lo = 2 * chan
-    state = g_cat[0:half, lo : lo + 256] + row_land[0:half, lo : lo + 256].astype(F32)
-    norm_row = jnp.sum(norm[...], axis=0, keepdims=True)
-    norm_rows = jnp.concatenate(
-        [norm_row[:, 0:256], norm_row[:, 256:half], jnp.zeros((1, 512 - half), F32)], axis=1
-    )
-    extra = small_row[...] + row_land[half : half + 16, 0:256].astype(F32)
-    extra = jnp.concatenate([extra[0:8], norm_rows[:, 0:256], norm_rows[:, 256:512], jnp.zeros((6, 256), F32)])
-    acc[misc : misc + half, 0:256] = state
-    acc[misc + half : misc + half + 16, 0:256] = extra
-    col_send[0:half, :] = state.astype(BF16)
-    col_send[half : half + 16, :] = extra.astype(BF16)
-    col_copy = pair_copy(col_send, col_land, pair_send.at[1], pair_recv.at[1], to_col)
-    col_copy.start()
-    start_level(2, 0)
+
     lo = 2 * chan + 256
     acc[misc : misc + half, 256:384] = jnp.concatenate(
         [g_cat[0:half, lo : lo + 64], row_land[0:half, lo : lo + 64].astype(F32)], axis=1
     )
     acc[misc + half : misc + half + 16, 256:384] = jnp.zeros((16, 128), F32)
-    acc[misc + half + 16 : misc + half + 32, :] = small_own[...]
-    if tail > half + 32:
-        acc[misc + half + 32 : misc + tail, :] = jnp.zeros((tail - half - 32, chan), F32)
-    rs_row.wait()
-    rs_out[...] = rs_in[...] + rs_land[0]
-    rs_col.start()
-    for i in (0, 1):
-        end_level(i, 0)
-        start_level(i, 1)
+    first = misc + half + 16
+    acc[first : first + 8, :] = jnp.concatenate(
+        [sum8(acc_v, n) for n in range(7)] + [jnp.zeros((1, chan), F32)], axis=0
+    )
+    acc[first + 8 : first + 24, :] = jnp.broadcast_to(
+        jnp.sum(acc_h[...], axis=1, keepdims=True), (16, chan)
+    )
+    if misc + tail > first + 24:
+        acc[first + 24 : misc + tail, :] = jnp.zeros((misc + tail - first - 24, chan), F32)
+    end_level(0, 0)
     col_copy.wait()
-    acc[misc : misc + half + 16, 0:256] = (
-        col_send[...].astype(F32) + col_land[...].astype(F32)
-    )
+    acc[misc : misc + half + 16, 0:256] = col_send[...].astype(F32) + col_land[...].astype(F32)
     start_level(3, 0)
+    end_level(1, 0)
     end_level(2, 0)
-    start_level(2, 1)
     for level in range(1, 2 * bits):
         for i in (0, 1):
             end_level(i, level)
-            if level + 1 < 2 * bits:
-                start_level(i, level + 1)
         end_level(3, level - 1)
-        start_level(3, level)
         end_level(2, level)
-        if level + 1 < 2 * bits:
-            start_level(2, level + 1)
     end_level(3, 2 * bits - 1)
     rs_col.wait()
     for copy in dn_cols:
@@ -602,32 +699,31 @@
     rs_out[...] = rs_out[...] + rs_land[1]
 
 
-def sum_over_dp(dp, g_cat, g_out, small_row, small_own, rs, hid, dn_own, dn_rec):
+def sum_over_dp(dp, g_cat, go_own, go_rec, acc_v, acc_s, acc_h, acc_n, rs, dn_own, dn_rec):
     half = g_cat.shape[0] // 2
     wide = g_cat.shape[1]
-    chan = g_out.shape[1]
-    rows = 3 * big_rows(dp, 2 * half) + big_rows(dp, half + 32)
+    chan = go_own.shape[0]
+    rows = 3 * big_rows(dp, 2 * half) + big_rows(dp, half + 40)
     bits = dp.bit_length() - 1
-    tokens = hid.shape[0]
+    tokens = dn_own.shape[0]
     vmem = pl.BlockSpec(memory_space=pltpu.VMEM)
     hbm = pl.BlockSpec(memory_space=pl.ANY)
     act = jax.ShapeDtypeStruct((tokens, half), BF16)
     return pl.pallas_call(
         functools.partial(sum_kernel, dp),
-        in_specs=[vmem] * 7 + [hbm],
+        in_specs=[vmem] * 9 + [hbm],
         out_specs=[vmem, vmem, hbm, vmem],
         out_shape=[jax.ShapeDtypeStruct((rows, chan), BF16), act, act, jax.ShapeDtypeStruct(rs.shape, F32)],
         scratch_shapes=[
             pltpu.VMEM((rows, chan), F32),
             pltpu.VMEM((rows, chan), BF16),
             pltpu.VMEM((rows, chan), BF16),
-            pltpu.VMEM((half + 16, wide), BF16),
-            pltpu.VMEM((half + 16, wide), BF16),
+            pltpu.VMEM((half + 16, wide + half), BF16),
+            pltpu.VMEM((half + 16, wide + half), BF16),
             pltpu.VMEM((half + 16, 256), BF16),
             pltpu.VMEM((half + 16, 256), BF16),
             pltpu.VMEM((tokens, half), BF16),
             pltpu.VMEM((2,) + rs.shape, F32),
-            pltpu.VMEM((8, half), F32),
             pltpu.SemaphoreType.DMA((4, 2 * bits)),
             pltpu.SemaphoreType.DMA((4, 2 * bits)),
             pltpu.SemaphoreType.DMA((4,)),
@@ -638,7 +734,111 @@
         compiler_params=pltpu.CompilerParams(collective_id=0, has_side_effects=True),
         cost_estimate=pl.CostEstimate(flops=1_000_000, bytes_accessed=150_000_000, transcendentals=0),
         name="sum_over_dp",
-    )(g_cat, g_out, small_row, small_own, rs, hid, dn_own, dn_rec)
+    )(g_cat, go_own, go_rec, acc_v, acc_s, acc_h, acc_n, rs, dn_own, dn_rec)
+
+
+def finish_kernel(
+    width,
+    size,
+    out,
+    hid,
+    cot,
+    dn_sum,
+    dn_col,
+    proj_own,
+    proj_col,
+    trow,
+    rows_in,
+    rs,
+    gains,
+    result,
+    hidden_grad,
+    g_gate,
+    g_value,
+    g_step,
+    g_state,
+    small_a,
+    small_b,
+    small_h,
+    g_output,
+):
+    half = hid.shape[1]
+    step_rows = hid.shape[0]
+    hid32 = hid[...].astype(F32)
+    recip = rows_in[16:24, :]
+    cols = jnp.transpose(jnp.concatenate([trow[0:8, :], rs[...] * recip * recip / width], axis=0))
+    proj = proj_own[...].astype(F32) + proj_col[...].astype(F32)
+    result[...] = (hid32 + cols[:, 0:1] * proj).astype(BF16)
+    d_normed = dn_sum[...].astype(F32) + dn_col[...].astype(F32)
+    hidden_grad[...] = cot[...].astype(F32) + d_normed * gains[0:1, :] - cols[:, 8:9] * hid32
+    misc = 3 * size
+
+    @pl.when(pl.program_id(0) == 0)
+    def _():
+        g_output[...] = out[0 : g_output.shape[0], :].astype(F32)
+        for n, ref in ((1, g_gate), (2, g_value)):
+            ref[:, 0:half] = out[n * size : n * size + half, :].astype(F32)
+            ref[:, half : 2 * half] = out[n * size + half : n * size + 2 * half, :].astype(F32)
+        g_state[...] = out[misc : misc + half, 0:256].astype(F32)
+        step_t = jnp.transpose(out[misc : misc + half, 256:384].astype(F32))
+        heads = g_step.shape[0] // 2
+        own, rec = step_t[0:heads], step_t[64 : 64 + heads]
+        first = lax.axis_index("row") == 0
+        g_step[...] = jnp.concatenate([jnp.where(first, own, rec), jnp.where(first, rec, own)], axis=0)
+        small = out[misc + half : misc + half + 48, :].astype(F32)
+        small_a[...] = small[0:16, 0:256]
+        small_b[...] = small[16:24, :]
+        small_h[...] = jnp.transpose(small[24:40, 0:128])[0:8]
+
+
+def finish(size, heads, out, hid, cot, dn_sum, dn_col, proj_own, proj_col, trow, rows, rs, gains):
+    tokens, half = hid.shape
+    chan = out.shape[1]
+
+    def blk(cols):
+        return pl.BlockSpec((STEP, cols), lambda i: (i, 0))
+
+    def row(count):
+        return pl.BlockSpec((count, STEP), lambda i: (0, i))
+
+    def whole(shape):
+        return pl.BlockSpec(shape, lambda i: (0, 0))
+
+    shapes = [
+        (half, 2 * chan),
+        (half, 2 * chan),
+        (2 * heads, half),
+        (half, 256),
+        (16, 256),
+        (8, chan),
+        (8, 16),
+        (2 * chan, half),
+    ]
+    return pl.pallas_call(
+        functools.partial(finish_kernel, 2 * half, size),
+        grid=(tokens // STEP,),
+        in_specs=[
+            whole(out.shape),
+            blk(half),
+            blk(half),
+            blk(half),
+            blk(half),
+            blk(half),
+            blk(half),
+            row(16),
+            row(32),
+            row(8),
+            whole((8, half)),
+        ],
+        out_specs=[blk(half), blk(half)] + [whole(shape) for shape in shapes],
+        out_shape=[
+            jax.ShapeDtypeStruct((tokens, half), BF16),
+            jax.ShapeDtypeStruct((tokens, half), F32),
+        ]
+        + [jax.ShapeDtypeStruct(shape, F32) for shape in shapes],
+        cost_estimate=pl.CostEstimate(flops=20_000_000, bytes_accessed=20_000_000, transcendentals=0),
+        name="finish",
+    )(out, hid, cot, dn_sum, dn_col, proj_own, proj_col, trow, rows, rs, gains)
 
 
 def swap(x, axis):
@@ -696,9 +896,8 @@
     wo_part = cut(output_proj, 1 - r, chan, 0)
     wo_rec = swap(wo_part, "row")
     gain_f = gated_gain.astype(F32)
-    two = swap(jnp.stack([input_gain, gain_f]), "row")
-    gains = jnp.concatenate([input_gain[None], two[0:1], jnp.zeros((6, half), F32)], axis=0)
-    gated_rec = two[1]
+    gain_rec = swap(input_gain, "row")
+    gains = jnp.concatenate([input_gain[None], gain_rec[None], jnp.zeros((6, half), F32)], axis=0)
 
     skip_lane = jnp.repeat(skip_gain, chan // heads)
     vtap = jnp.concatenate(
@@ -720,7 +919,7 @@
     def arr(cols, dtype=F32):
         return jax.ShapeDtypeStruct((tokens, cols), dtype)
 
-    mixed, pre_gate, pre_value, conv_value, pre_shared, conv_shared, y_scan, states, rows, normed_t = pl.pallas_call(
+    mixed, po_own, po_rec, pre_gate, pre_value, conv_value, pre_shared, conv_shared, y_scan, states, rows, normed_t = pl.pallas_call(
         functools.partial(forward_kernel, steps_per_seq, width),
         grid=(grid,),
         in_specs=[
@@ -732,9 +931,13 @@
             whole((8, chan)),
             whole((8, 256)),
             whole((16, 128)),
+            whole((chan, half)),
+            whole((chan, half)),
         ],
         out_specs=[
             blk(chan),
+            blk(half),
+            blk(half),
             blk(chan),
             blk(chan),
             blk(chan),
@@ -742,11 +945,13 @@
             blk(256),
             blk(chan),
             blk(chan),
-            pl.BlockSpec((24, STEP), lambda i: (0, i)),
+            pl.BlockSpec((32, STEP), lambda i: (0, i)),
             pl.BlockSpec((width, STEP), lambda i: (0, i)),
         ],
         out_shape=[
             arr(chan, BF16),
+            arr(half, BF16),
+            arr(half, BF16),
             arr(chan),
             arr(chan),
             arr(chan),
@@ -754,7 +959,7 @@
             arr(256),
             arr(chan),
             arr(chan, BF16),
-            jax.ShapeDtypeStruct((24, tokens), F32),
+            jax.ShapeDtypeStruct((32, tokens), F32),
             jax.ShapeDtypeStruct((width, tokens), BF16),
         ],
         scratch_shapes=[
@@ -764,29 +969,10 @@
         ],
         cost_estimate=pl.CostEstimate(flops=12_000_000_000, bytes_accessed=40_000_000, transcendentals=8_000_000),
         name="forward_core",
-    )(hidden, hid_rec, gains, w_own, w_rec, vtap, stap, head_par)
-
-    mixed_rec = swap(mixed, "row")
-    own32 = mixed.astype(F32)
-    rec32 = mixed_rec.astype(F32)
-    weighted = (own32 * gain_f).astype(BF16)
-    weighted_rec = (rec32 * gated_rec).astype(BF16)
-    proj_part = dot(weighted, wo_own) + dot(weighted_rec, wo_part)
-    hidden32 = hidden.astype(F32)
-    cot32 = cotangent.astype(F32)
-    sums = jnp.stack([jnp.sum(own32 * own32, axis=1), jnp.sum(cot32 * proj_part, axis=1)])
-    sums = sums + swap(sums, "row")
-    sums = sums + swap(sums, "col")
-    proj_bf = proj_part.astype(BF16)
-    proj = proj_bf.astype(F32) + swap(proj_bf, "col").astype(F32)
-    scale = lax.rsqrt(sums[0] / inner_width + EPSILON)
-    result = (hidden32 + scale[:, None] * proj).astype(BF16)
-    scaled_cot = (scale[:, None] * cot32).astype(BF16)
-    g_out_own = dot_tn(weighted, scaled_cot)
-    g_out_rec = dot_tn(weighted_rec, scaled_cot)
-    trow = jnp.concatenate(
-        [scale[None], (sums[1] * scale**3 / inner_width)[None], jnp.zeros((6, tokens), F32)], axis=0
-    )
+    )(hidden, hid_rec, gains, w_own, w_rec, vtap, stap, head_par, wo_own, wo_rec)
+
+    proj_own, trow = mid_exchange(inner_width, rows, cotangent, po_own, po_rec)
+    proj_col = swap(proj_own, "col")
 
     lane_head = jnp.arange(chan) // (chan // heads)
     sel = (jnp.arange(16)[:, None] == lane_head[None, :]).astype(BF16)
@@ -798,7 +984,7 @@
     def rrow(count):
         return pl.BlockSpec((count, STEP), lambda i: (0, last - i))
 
-    p_all, dn_own, dn_rec, rsum, acc_v, acc_s, acc_h = pl.pallas_call(
+    p_all, dn_own, dn_rec, rsum, acc_v, acc_s, acc_h, acc_n, go_own, go_rec = pl.pallas_call(
         functools.partial(backward_kernel, steps_per_seq),
         grid=(grid,),
         in_specs=[
@@ -806,8 +992,8 @@
             rblk(half),
             whole((chan, half)),
             whole((chan, half)),
-            rrow(8),
-            rrow(24),
+            rrow(16),
+            rrow(32),
             rblk(chan),
             rblk(chan),
             rblk(chan),
@@ -822,6 +1008,8 @@
             whole((8, 256)),
             whole((16, 128)),
             whole((16, chan)),
+            rblk(half),
+            rblk(half),
         ],
         out_specs=[
             rblk(wide),
@@ -831,6 +1019,9 @@
             whole((56, chan)),
             whole((40, 256)),
             whole((16, 128)),
+            whole((16, half)),
+            whole((chan, half)),
+            whole((chan, half)),
         ],
         out_shape=[
             arr(wide, BF16),
@@ -840,6 +1031,9 @@
             jax.ShapeDtypeStruct((56, chan), F32),
             jax.ShapeDtypeStruct((40, 256), F32),
             jax.ShapeDtypeStruct((16, 128), F32),
+            jax.ShapeDtypeStruct((16, half), F32),
+            jax.ShapeDtypeStruct((chan, half), F32),
+            jax.ShapeDtypeStruct((chan, half), F32),
         ],
         scratch_shapes=[
             pltpu.VMEM((128, chan), F32),
@@ -871,55 +1065,34 @@
         stap,
         head_par,
         sel,
+        hidden,
+        hid_rec,
     )
 
     g_cat = dot(normed_t, p_all)
-    vsum = jnp.sum(acc_v.reshape(7, 8, chan), axis=1)
-    ssum = jnp.sum(acc_s.reshape(5, 8, 256), axis=1)
-    hsum = jnp.sum(acc_h.reshape(2, 8, 128), axis=2)
-    small_row = jnp.pad(ssum, ((0, 11), (0, 0)))
-    small_own = jnp.concatenate(
-        [vsum, jnp.pad(hsum.reshape(1, 16), ((0, 0), (0, chan - 16))), jnp.zeros((8, chan), F32)], axis=0
+    out, dn_sum, dn_col, rs = sum_over_dp(
+        dp, g_cat, go_own, go_rec, acc_v, acc_s, acc_h, acc_n, rsum, dn_own, dn_rec
     )
-    g_out = jnp.concatenate([g_out_own, g_out_rec], axis=0)
-    out, dn_sum, dn_col, rs = sum_over_dp(
-        dp, g_cat, g_out, small_row, small_own, rsum, hidden, dn_own, dn_rec
-    )
-    size, misc = big_rows(dp, 2 * half), 3 * big_rows(dp, 2 * half)
-
-    def side_by_side(start):
-        return jnp.concatenate([out[start : start + half], out[start + half : start + 2 * half]], axis=1).astype(F32)
-
-    g_output = out[0 : 2 * chan].astype(F32)
-    g_gate = side_by_side(size)
-    g_value = side_by_side(2 * size)
-    g_state = out[misc : misc + half, 0:256].astype(F32)
-    s_own = out[misc : misc + half, 256 : 256 + heads].astype(F32)
-    s_rec = out[misc : misc + half, 320 : 320 + heads].astype(F32)
-    g_step = jnp.where(r == 0, jnp.concatenate([s_own, s_rec], axis=1), jnp.concatenate([s_rec, s_own], axis=1))
-    small = out[misc + half : misc + half + 32].astype(F32)
-    g_norm = small[8:10, 0:256].reshape(512)[0:half]
-    d_normed = dn_sum.astype(F32) + dn_col.astype(F32)
-    recip = rows[16]
-    hidden_grad = (
-        cot32 + d_normed * input_gain - (rs[0] * recip * recip / width)[:, None] * hidden32
+    size = big_rows(dp, 2 * half)
+    result, hidden_grad, g_gate, g_value, g_step, g_state, sm_a, sm_b, sm_h, g_output = finish(
+        size, heads, out, hidden, cotangent, dn_sum, dn_col, proj_own, proj_col, trow, rows, rs, gains
     )
     return (
         result,
         hidden_grad,
         g_gate,
         g_value,
-        g_step,
+        g_step.T,
         g_state,
-        small[16:20],
-        small[20],
-        small[0:4, 0:256],
-        small[4, 0:256],
-        small[23, 0:heads],
-        small[23, 8 : 8 + heads],
-        jnp.sum(small[21].reshape(heads, chan // heads), axis=1),
-        g_norm,
-        small[22],
+        sm_b[0:4],
+        sm_b[4],
+        sm_a[0:4],
+        sm_a[4],
+        sm_h[0, 0:heads],
+        sm_h[0, 8 : 8 + heads],
+        jnp.sum(sm_b[5].reshape(heads, chan // heads), axis=1),
+        sm_a[8:10].reshape(512)[0:half],
+        sm_b[6],
         g_output,
     )
 

time: 219 us -> 193 us (0.88)
  other arithmetic: 24.7 us -> 3.72 us
  Pallas kernels: 153 us -> 161 us
  matrix products: 14.8 us -> 9.37 us
  local copies, waits for them, and re-layouts: 18.3 us -> 14.5 us
  waiting for transfers between devices: 2.22 us -> 0.02 us
    convert_element_type x7 -> x0, other arithmetic: 7.85 us -> none  [the longest x2 2.18 us: side_by_side(): jnp.concatenate([out[start:start + half], out[start + half:start + 2 * ha...]
    dot_general x2 -> x0, matrix products: 6.13 us -> none  [dot_tn(): lax.dot_general(a, b, (((0,), (0,)), ((), ())), preferred_element_type=F32)]
    reduce_sum x5 -> x1, other arithmetic: 5.62 us -> 0.63 us  [body(): jnp.sum(sm_b[5].reshape(heads, chan // heads), axis=1)]
    sub x1 -> x0, other arithmetic: 4.1 us -> none  [body(): cot32 + d_normed * input_gain]
    pallas_call x1, Pallas kernels: 21.5 us -> 25.6 us  [body(): pl.pallas_call(functools.partial(forward_kernel, steps_per_seq, width), g...]
    pallas_call x1 -> x3, Pallas kernels: 93.4 us -> 95.9 us  [the longest x1 67.9 us: sum_over_dp(): pl.pallas_call(functools.partial(sum_kernel, dp), in_specs=[vmem] * 9 + [...]
    concatenate x4 -> x1, other arithmetic: 3.13 us -> 0.67 us  [body(): jnp.concatenate([input_gain[None], gain_rec[None], jnp.zeros((6, half), F...]
    ppermute x9 -> x6, waiting for transfers between devices: 2.22 us -> 0.02 us  [swap(): return lax.ppermute(x, axis, SWAP)]
  transfers between devices with their start and end apart: 9 -> 6, of which waited for: 3 -> 0; matrix products, arithmetic and copies ran while one was open for 23% -> 9% of each run, Pallas kernels for 60% -> 77%
where the time goes in v3:
time: 193 us
  Pallas kernels  161 us (83%)
  local copies, waits for them, and re-layouts  14.5 us (8%)
  matrix products  9.37 us (5%)
  other arithmetic  3.72 us (2%)
  starting transfers between devices  3.42 us (2%)
    pallas_call x1, Pallas kernels, sum_over_dp(): pl.pallas_call(functools.partial(sum_kernel, dp), in_specs=[vmem] * 9 + [...  67.9 us
    pallas_call x1, Pallas kernels, body(): pl.pallas_call(functools.partial(backward_kernel, steps_per_seq), grid=(g...  39.2 us
    pallas_call x1, Pallas kernels, body(): pl.pallas_call(functools.partial(forward_kernel, steps_per_seq, width), g...  25.6 us
    pallas_call x1, Pallas kernels, mid_exchange(): pl.pallas_call(functools.partial(mid_kernel, inner_width), in_specs=[vmem...  16.3 us
    pallas_call x1, Pallas kernels, finish(): pl.pallas_call(functools.partial(finish_kernel, 2 * half, size), grid=(to...  11.7 us
    dot_general x1, matrix products, dot(): return jnp.dot(a, b, preferred_element_type=F32)  9.37 us
  transfers between devices with their start and end apart: 6, of which 0 were waited for; matrix products, arithmetic and copies ran while one was open for 9% of the time, Pallas kernels for 77%

profile of v3, /device:TPU:0, one launch (start us, length us, event | category | flops | bytes accessed | tf_op | source)
XLA Modules:
  0.0 192.6 jit_solution(5644150413375477478)
XLA Ops:
  1.2 1.9 constant_dynamic-slice_fusion
  3.6 0.8 constant_dynamic-slice_fusion.2
  5.0 1.1 fusion.3
  6.8 0.7 maximum_maximum_fusion.1.stap
  7.5 0.6 fusion.4.sel_ref
  8.4 0.6 concatenate.21.vtap
  9.1 0.7 maximum_maximum_fusion.gains
  9.8 0.7 broadcast_in_dim.48.head_par
  10.5 25.6 %forward_core.1 = (bf16[2048,384]{1,0:T(8,128)(2,1)}, bf16[2048,384]{1,0:T(8,128)(2,1)}, bf16[2048,384]{1,0:T(8,128)(2,1)}, f32[2048,384]{1,0:T(8,128)}, f32[204...) custom-call(bf16[2048,384]{1,0:T(8,128)(2,1)} %hid.1, ...), custom_call_target="tpu_custom_call" | custom-call | flops 12000000000 | bytes 40000000 | tf_op jit(solution)/shard_map/forward_core/pallas_call | solution.py:922
  36.0 16.3 %mid_exchange.1 = (bf16[2048,384]{1,0:T(8,128)(2,1)}, f32[16,2048]{1,0:T(8,128)}) custom-call(f32[32,2048]{1,0:T(8,128)} %get-tuple-element.55.rows_in, bf16[2048,384]{1,0:T(8,128)(2,1)} %cot.3, bf16[2048,384]{1,0:T(8,128)(2,1)} %get-tuple-element.56.po_own, bf16[2048,384]{1,0:T(8,128)(2,1)} %get-tuple-element.57.po_rec), custom_call_target="tpu_custom_call" | custom-call | flops 1000000 | bytes 20000000 | tf_op jit(solution)/shard_map/mid_exchange/pallas_call | solution.py:476
  52.4 2.2 %collective-permute-start.5 = (bf16[2048,384]{1,0:T(8,128)(2,1)}, bf16[2048,384]{1,0:T(8,128)(2,1)S(1)}, u32[]{:S(2)}, u32[]{:S(2)}) collective-permute-start(bf16[2048,384]{1,0:T(8,128)(2,1)} %get-tuple-element.80.proj_own), channel_id=1, source_target_pairs={{0,1},{1,0},{2,3},{3,2},{4,5},{5,4},{6,7},{7,6},{8,9},{9,8},{10,11... | collective-permute-start | bytes 4718600 | tf_op jit(solution)/shard_map/ppermute | solution.py:845
  54.6 39.2 %backward_core.1 = (bf16[2048,1152]{1,0:T(8,128)(2,1)}, bf16[2048,384]{1,0:T(8,128)(2,1)}, bf16[2048,384]{1,0:T(8,128)(2,1)}, f32[8,2048]{1,0:T(8,128)}, f32[56,...) custom-call(bf16[2048,384]{1,0:T(8,128)(2,1)} %cot.3, ...), custom_call_target="tpu_custom_call" | custom-call | flops 24000000000 | bytes 60000000 | tf_op jit(solution)/shard_map/backward_core/pallas_call | solution.py:987
  93.8 9.4 %fusion.9.g_cat = f32[768,1152]{1,0:T(8,128)} fusion(bf16[768,2048]{1,0:T(8,128)(2,1)} %get-tuple-element.54, bf16[2048,1152]{1,0:T(8,128)(2,1)} %get-tuple-element.67), kind=kOutput, calls=%fused_computation.36 | convolution fusion | flops 3623878656 | bytes 11403264 | tf_op jit(solution)/shard_map/dot_general | solution.py:21
  103.2 67.9 %sum_over_dp.1 = (bf16[2816,384]{1,0:T(8,128)(2,1)}, bf16[2048,384]{1,0:T(8,128)(2,1)}, bf16[2048,384]{1,0:T(8,128)(2,1)}, f32[8,2048]{1,0:T(8,128)}) custom-call(f32[768,1152]{1,0:T(8,128)} %fusion.9.g_cat, f32[384,384]{1,0:T(8,128)} %get-tuple-element.68.go_own, f32[384,384]{1,0:T(8,128)} %get-tuple-element.69.go_rec, f32[56,384]{1,0:T(8,128)} %get-tuple-element.70.acc_v, ...), custom_call_target="tpu_custom_call" | custom-call | flops 1000000 | bytes 150000000 | tf_op jit(solution)/shard_map/sum_over_dp/pallas_call | solution.py:712
  171.1 1.2 copy-done.1
  172.3 11.7 %finish.1 = (bf16[2048,384]{1,0:T(8,128)(2,1)}, f32[2048,384]{1,0:T(8,128)}, f32[384,768]{1,0:T(8,128)}, f32[384,768]{1,0:T(8,128)}, f32[12,384]{1,0:T(8,128)}, ...) custom-call(bf16[2816,384]{1,0:T(8,128)(2,1)} %get-tuple-element.77.out,, ...), custom_call_target="tpu_custom_call" | custom-call | flops 20000000 | bytes 20000000 | tf_op jit(solution)/shard_map/finish/pallas_call | solution.py:817
  184.0 1.3 slice.33
  185.3 0.7 slice_bitcast_fusion
  186.0 1.3 slice.32
  187.3 1.3 slice.30
  188.6 1.4 slice_reduce_fusion
  190.0 1.3 slice_bitcast_fusion.1
  191.3 0.6 copy.36
  192.0 0.6 reduce_sum.9
  (58 shorter events, 2.8 us)
Async XLA Ops:
  0.6 4.1 %copy-start.2 = (bf16[384,768]{1,0:T(8,128)(2,1)S(1)}, bf16[384,768]{1,0:T(8,128)(2,1)}, u32[]{:S(2)}) copy-start(bf16[384,768]{1,0:T(8,128)(2,1)} %param.18) | copy-start | bytes 1769476
  0.7 4.1 %copy-start.3 = (bf16[384,768]{1,0:T(8,128)(2,1)S(1)}, bf16[384,768]{1,0:T(8,128)(2,1)}, u32[]{:S(2)}) copy-start(bf16[384,768]{1,0:T(8,128)(2,1)} %param.17) | copy-start | bytes 1769476
  0.7 8.4 %collective-permute-start.1 = (f32[384]{0:T(512)}, f32[384]{0:T(512)S(1)}, u32[]{:S(2)}, u32[]{:S(2)}) collective-permute-start(f32[384]{0:T(512)} %param.28), channel_id=1, source_target_pairs={{0,2},{2,0},{1,3},{3,1},{4,6},{6,4},{5,7},{7,5},{8,10},{10,8},{9,1... | collective-permute-start | bytes 4616 | tf_op jit(solution)/shard_map/ppermute | solution.py:845
  1.2 3.8 %copy-start.4 = (bf16[384,256]{1,0:T(8,128)(2,1)S(1)}, bf16[384,256]{1,0:T(8,128)(2,1)}, u32[]{:S(2)}) copy-start(bf16[384,256]{1,0:T(8,128)(2,1)} %param.20) | copy-start | bytes 589828
  3.1 6.7 %collective-permute-start.3 = (bf16[384,384]{1,0:T(8,128)(2,1)S(1)}, bf16[384,384]{1,0:T(8,128)(2,1)S(1)}, u32[]{:S(2)}, u32[]{:S(2)}) collective-permute-start(bf16[384,384]{1,0:T(8,128)(2,1)S(1)} %get-tuple-element.95), channel_id=1, source_target_pairs={{0,2},{2,0},{1,3},{3,1},{4,6},{6,4},{5,7},{7,5},{8,10},{10,8},{9,1... | collective-permute-start | bytes 884744 | tf_op jit(solution)/shard_map/ppermute | solution.py:845
  3.2 6.6 %collective-permute-start = (bf16[2048,384]{1,0:T(8,128)(2,1)}, bf16[2048,384]{1,0:T(8,128)(2,1)}, u32[]{:S(2)}, u32[]{:S(2)}) collective-permute-start(bf16[2048,384]{1,0:T(8,128)(2,1)} %hid.1), channel_id=1, source_target_pairs={{0,2},{2,0},{1,3},{3,1},{4,6},{6,4},{5,7},{7,5},{8,10},{10,8},{9,1... | collective-permute-start | bytes 4718600 | tf_op jit(solution)/shard_map/ppermute | solution.py:845
  4.9 1.7 copy-start
  4.9 1.9 copy-start.6
  4.9 1.9 copy-start.9
  4.9 3.1 %copy-start.13 = (f32[6]{0:T(128)S(1)}, f32[6]{0:T(128)}, u32[]{:S(2)}) copy-start(f32[6]{0:T(128)} %param.25) | copy-start | bytes 76
  5.0 3.1 %copy-start.14 = (f32[6]{0:T(128)S(1)}, f32[6]{0:T(128)}, u32[]{:S(2)}) copy-start(f32[6]{0:T(128)} %param.26) | copy-start | bytes 76
  5.0 3.2 %copy-start.8 = (f32[384]{0:T(512)S(1)}, f32[384]{0:T(512)}, u32[]{:S(2)}) copy-start(f32[384]{0:T(512)} %param.28) | copy-start | bytes 4612
  5.0 3.3 %copy-start.7 = (f32[384]{0:T(512)S(1)}, f32[384]{0:T(512)}, u32[]{:S(2)}) copy-start(f32[384]{0:T(512)} %param.22) | copy-start | bytes 4612
  5.0 3.3 %copy-start.10 = (bf16[384]{0:T(512)(128)(2,1)S(1)}, bf16[384]{0:T(512)(128)(2,1)}, u32[]{:S(2)}) copy-start(bf16[384]{0:T(512)(128)(2,1)} %param.29) | copy-start | bytes 2308
  5.0 3.3 %copy-start.11 = (f32[6]{0:T(128)S(1)}, f32[6]{0:T(128)}, u32[]{:S(2)}) copy-start(f32[6]{0:T(128)} %param.27) | copy-start | bytes 76
  5.0 3.4 %copy-start.5 = (f32[4,384]{1,0:T(4,128)S(1)}, f32[4,384]{1,0:T(4,128)}, u32[]{:S(2)}) copy-start(f32[4,384]{1,0:T(4,128)} %param.21) | copy-start | bytes 18436
  6.1 3.6 %collective-permute-start.2 = (bf16[384,1152]{1,0:T(8,128)(2,1)S(1)}, bf16[384,1152]{1,0:T(8,128)(2,1)}, u32[]{:S(2)}, u32[]{:S(2)}) collective-permute-start(bf16[384,1152]{1,0:T(8,128)(2,1)S(1)} %get-tuple-element.101), channel_id=1, source_target_pairs={{0,2},{2,0},{1,3},{3,1},{4,6},{6,4},{5,7},{7,5},{8,10},{10,8},{9,1... | collective-permute-start | bytes 2654216 | tf_op jit(solution)/shard_map/ppermute | solution.py:845
  6.6 47.9 %collective-permute-start.4 = (bf16[2048,384]{1,0:T(8,128)(2,1)S(1)}, bf16[2048,384]{1,0:T(8,128)(2,1)}, u32[]{:S(2)}, u32[]{:S(2)}) collective-permute-start(bf16[2048,384]{1,0:T(8,128)(2,1)S(1)} %copy-done), channel_id=1, source_target_pairs={{0,2},{2,0},{1,3},{3,1},{4,6},{6,4},{5,7},{7,5},{8,10},{10,8},{9,1... | collective-permute-start | bytes 4718600 | tf_op jit(solution)/shard_map/ppermute | solution.py:845
  9.7 0.7 copy-start.12
  52.4 118.7 %collective-permute-start.5 = (bf16[2048,384]{1,0:T(8,128)(2,1)}, bf16[2048,384]{1,0:T(8,128)(2,1)S(1)}, u32[]{:S(2)}, u32[]{:S(2)}) collective-permute-start(bf16[2048,384]{1,0:T(8,128)(2,1)} %get-tuple-element.80.proj_own), channel_id=1, source_target_pairs={{0,1},{1,0},{2,3},{3,2},{4,5},{5,4},{6,7},{7,6},{8,9},{9,8},{10,11... | collective-permute-start | bytes 4718600 | tf_op jit(solution)/shard_map/ppermute | solution.py:845
  171.1 1.2 copy-start.1

commit v4 on v3

--- a/solution.py
+++ b/solution.py
@@ -79,6 +79,8 @@
 def forward_kernel(
     steps_per_seq,
     width,
+    inner_width,
+    col_blocks,
     hid_own,
     hid_rec,
     gains,
@@ -89,9 +91,11 @@
     head_par,
     wo_own,
     wo_rec,
+    cot,
     mixed_out,
-    po_own,
-    po_rec,
+    proj_out,
+    proj_col,
+    trow,
     pre_gate_out,
     pre_value_out,
     conv_value_out,
@@ -104,7 +108,95 @@
     state,
     vbuf,
     sbuf,
+    po_own,
+    po_send,
+    po_land,
+    proj_s,
+    sums,
+    sums_land,
+    row_send_sem,
+    row_recv_sem,
+    col_send_sem,
+    col_recv_sem,
+    sum_send_sem,
+    sum_recv_sem,
 ):
+    chan = mixed_out.shape[1]
+    pairs = chan // 128
+    step = pl.program_id(0)
+    blocks = pl.num_programs(0) - 1
+    r = lax.axis_index("row")
+    c = lax.axis_index("col")
+    targets = [{"row": 1 - r}, {"col": 1 - c}, {"row": 1 - r, "col": 1 - c}]
+
+    def span(i):
+        return pl.ds(pl.multiple_of(i * STEP, STEP), STEP)
+
+    def row_copy(i):
+        return remote(
+            po_send.at[span(i), :], po_land.at[span(i), :], row_send_sem.at[i], row_recv_sem.at[i], targets[0]
+        )
+
+    def col_copy(i):
+        return remote(
+            proj_s.at[span(i), :], proj_col.at[span(i), :], col_send_sem.at[i], col_recv_sem.at[i], targets[1]
+        )
+
+    @pl.when(step == 0)
+    def _():
+        greet(targets)
+
+    @pl.when(step > 0)
+    def _():
+        i = step - 1
+        row_copy(i).wait()
+        part = po_own[span(i), :].astype(F32) + po_land[span(i), :].astype(F32)
+        proj_s[span(i), :] = part.astype(BF16)
+
+        @pl.when(i < col_blocks)
+        def _():
+            col_copy(i).start()
+
+        dots = head_sums(jnp.ones((16, cot.shape[1]), BF16), part * cot[...].astype(F32))
+        sums[pl.ds(8 + i, 1), :] = dots[0:1]
+
+    @pl.when(step < blocks)
+    def _():
+        forward_block(
+            steps_per_seq,
+            width,
+            (hid_own, hid_rec, gains, w_own, w_rec, vtap, stap, head_par, wo_own, wo_rec),
+            (mixed_out, pre_gate_out, pre_value_out, conv_value_out, pre_shared_out, conv_shared_out),
+            (y_out, state_out, rows_out, nt_out),
+            (state, vbuf, sbuf, po_own.at[span(step), :], po_send.at[span(step), :], sums.at[pl.ds(step, 1), :]),
+        )
+        row_copy(step).start()
+
+    @pl.when(step == blocks)
+    def _():
+        ends = []
+        for i, target in enumerate(targets):
+            copy = remote(sums, sums_land.at[i], sum_send_sem.at[i], sum_recv_sem.at[i], target)
+            copy.start()
+            ends.append(copy)
+        proj_out[...] = proj_s[...]
+        for copy in ends:
+            copy.wait()
+        total = (sums[...] + sums_land[0]) + (sums_land[1] + sums_land[2])
+        scale = lax.rsqrt(total[0:8] / inner_width + EPSILON)
+        coef = total[8:16] * (scale * scale * scale) / inner_width
+        for i in range(trow.shape[1] // STEP):
+            trow[0:8, i * STEP : (i + 1) * STEP] = jnp.broadcast_to(scale[i : i + 1], (8, STEP))
+            trow[8:16, i * STEP : (i + 1) * STEP] = jnp.broadcast_to(coef[i : i + 1], (8, STEP))
+        for i in range(col_blocks):
+            col_copy(i).wait()
+
+
+def forward_block(steps_per_seq, width, weights_in, outs_a, outs_b, scratch):
+    hid_own, hid_rec, gains, w_own, w_rec, vtap, stap, head_par, wo_own, wo_rec = weights_in
+    mixed_out, pre_gate_out, pre_value_out, conv_value_out, pre_shared_out, conv_shared_out = outs_a
+    y_out, state_out, rows_out, nt_out = outs_b
+    state, vbuf, sbuf, po_own, po_send, square_row = scratch
     chan = mixed_out.shape[1]
     pairs = chan // 128
 
@@ -193,8 +285,8 @@
     mix = mixed_out[...].astype(F32)
     weighted = (mix * vtap[6:7, :]).astype(BF16)
     po_own[...] = dot(weighted, wo_own[...]).astype(BF16)
-    po_rec[...] = dot(weighted, wo_rec[...]).astype(BF16)
-    rows_out[24:32, :] = head_sums(jnp.ones((16, chan), BF16), mix * mix)
+    po_send[...] = dot(weighted, wo_rec[...]).astype(BF16)
+    square_row[...] = head_sums(jnp.ones((16, chan), BF16), mix * mix)[0:1]
 
 
 def backward_kernel(
@@ -421,81 +513,10 @@
     pl.semaphore_wait(barrier, len(targets))
 
 
-def mid_kernel(
-    inner_width,
-    rows_in,
-    cot,
-    po_own,
-    po_rec,
-    proj_out,
-    trow,
-    po_land,
-    sums,
-    sums_land,
-    po_send_sem,
-    po_recv_sem,
-    send_sem,
-    recv_sem,
-):
-    r = lax.axis_index("row")
-    c = lax.axis_index("col")
-    targets = [{"row": 1 - r}, {"col": 1 - c}, {"row": 1 - r, "col": 1 - c}]
-    greet(targets)
-    tokens, half = cot.shape
-    cut = tokens // DN_PARTS
-    copies = []
-    for i in range(DN_PARTS):
-        rows = pl.ds(i * cut, cut)
-        copy = remote(po_rec.at[rows, :], po_land.at[rows, :], po_send_sem.at[i], po_recv_sem.at[i], targets[0])
-        copy.start()
-        copies.append(copy)
-    ones = jnp.ones((16, half), BF16)
-    sums[0:8, :] = rows_in[24:32, :]
-    for i in range(DN_PARTS):
-        rows = slice(i * cut, (i + 1) * cut)
-        copies[i].wait()
-        part = po_own[rows, :].astype(F32) + po_land[rows, :].astype(F32)
-        proj_out[rows, :] = part.astype(BF16)
-        sums[8:16, rows] = head_sums(ones, part * cot[rows, :].astype(F32))
-    ends = []
-    for i, target in enumerate(targets):
-        copy = remote(sums, sums_land.at[i], send_sem.at[i], recv_sem.at[i], target)
-        copy.start()
-        ends.append(copy)
-    for copy in ends:
-        copy.wait()
-    total = (sums[...] + sums_land[0]) + (sums_land[1] + sums_land[2])
-    scale = lax.rsqrt(total[0:8] / inner_width + EPSILON)
-    trow[0:8, :] = scale
-    trow[8:16, :] = total[8:16] * (scale * scale * scale) / inner_width
-
-
-def mid_exchange(inner_width, rows, cot, po_own, po_rec):
-    tokens, half = cot.shape
-    vmem = pl.BlockSpec(memory_space=pltpu.VMEM)
-    return pl.pallas_call(
-        functools.partial(mid_kernel, inner_width),
-        in_specs=[vmem, vmem, vmem, pl.BlockSpec(memory_space=pl.ANY)],
-        out_specs=[vmem, vmem],
-        out_shape=[jax.ShapeDtypeStruct((tokens, half), BF16), jax.ShapeDtypeStruct((16, tokens), F32)],
-        scratch_shapes=[
-            pltpu.VMEM((tokens, half), BF16),
-            pltpu.VMEM((16, tokens), F32),
-            pltpu.VMEM((3, 16, tokens), F32),
-            pltpu.SemaphoreType.DMA((DN_PARTS,)),
-            pltpu.SemaphoreType.DMA((DN_PARTS,)),
-            pltpu.SemaphoreType.DMA((3,)),
-            pltpu.SemaphoreType.DMA((3,)),
-        ],
-        compiler_params=pltpu.CompilerParams(collective_id=1, has_side_effects=True),
-        cost_estimate=pl.CostEstimate(flops=1_000_000, bytes_accessed=20_000_000, transcendentals=0),
-        name="mid_exchange",
-    )(rows, cot, po_own, po_rec)
-
-
 def sum_kernel(
     dp,
-    g_cat,
+    normed_t_hbm,
+    p_hbm,
     go_own,
     go_rec,
     acc_v,
@@ -518,6 +539,11 @@
     col_land,
     dn_land,
     rs_land,
+    normed_t,
+    p_all,
+    go_send,
+    go_land,
+    load_sem,
     send_sem,
     recv_sem,
     pair_send,
@@ -525,9 +551,8 @@
     dn_send_sem,
     dn_recv_sem,
 ):
-    half = g_cat.shape[0] // 2
-    chan = go_own.shape[0]
-    wide = g_cat.shape[1]
+    chan, half = go_own.shape
+    wide = p_all.shape[1]
     size = big_rows(dp, 2 * half)
     misc = 3 * size
     tail = out.shape[0] - misc
@@ -546,10 +571,17 @@
     def sum8(ref, n):
         return jnp.sum(ref[8 * n : 8 * n + 8, :], axis=0, keepdims=True)
 
+    loads = [
+        pltpu.make_async_copy(normed_t_hbm, normed_t, load_sem.at[0]),
+        pltpu.make_async_copy(p_hbm, p_all, load_sem.at[1]),
+    ]
+    for load in loads:
+        load.start()
     greet([partner(k) for k in range(bits)] + [to_row, to_col])
-
-    row_send[0:half, 0:wide] = g_cat[half : 2 * half, :].astype(BF16)
-    row_send[0:half, wide : wide + half] = go_rec[...].astype(BF16)
+    go_send[...] = go_rec[...].astype(BF16)
+    go_copy = remote(go_send, go_land, pair_send.at[4], pair_recv.at[4], to_row)
+    go_copy.start()
+
     small = jnp.concatenate([sum8(acc_s, n) for n in range(5)] + [jnp.zeros((3, 256), F32)], axis=0)
     norm_own, norm_rec = [
         jnp.concatenate([sum8(acc_n, n), jnp.zeros((1, 512 - half), F32)], axis=1) for n in (0, 1)
@@ -558,9 +590,8 @@
     row_send[half : half + 16, 0:256] = jnp.concatenate(
         [small, norm_rec[:, 0:256], norm_rec[:, 256:512], pad6], axis=0
     ).astype(BF16)
-    row_send[half : half + 16, 256 : wide + half] = jnp.zeros((16, wide + half - 256), BF16)
+    row_send[half : half + 16, 256:wide] = jnp.zeros((16, wide - 256), BF16)
     row_copy = remote(row_send, row_land, pair_send.at[0], pair_recv.at[0], to_row)
-    row_copy.start()
 
     tokens = dn_own.shape[0]
     cut = tokens // DN_PARTS
@@ -637,30 +668,37 @@
     mine = pl.multiple_of(r * half, 128)
     other = pl.multiple_of((1 - r) * half, 128)
 
-    def fill(i, own, lo):
-        acc[span(i * size + mine, half), :] = own
-        acc[span(i * size + other, half), :] = row_land[0:half, lo : lo + chan].astype(F32)
+    def fill(i, theirs):
+        acc[span(i * size + other, half), :] = theirs.astype(F32)
         if size > 2 * half:
             acc[i * size + 2 * half : (i + 1) * size, :] = jnp.zeros((size - 2 * half, chan), F32)
-
-    for i in range(3):
-        acc_own = go_own[...] if i == 0 else g_cat[0:half, (i - 1) * chan : i * chan]
-        if i == 0:
-            row_copy.wait()
-        fill(i, acc_own, wide if i == 0 else (i - 1) * chan)
         start_level(i, 0)
-        if i == 0:
-            lo = 2 * chan
-            state = g_cat[0:half, lo : lo + 256] + row_land[0:half, lo : lo + 256].astype(F32)
-            extra = jnp.concatenate([small, norm_own[:, 0:256], norm_own[:, 256:512], pad6], axis=0)
-            extra = extra + row_land[half : half + 16, 0:256].astype(F32)
-            col_send[0:half, :] = state.astype(BF16)
-            col_send[half : half + 16, :] = extra.astype(BF16)
-            col_copy = remote(col_send, col_land, pair_send.at[1], pair_recv.at[1], to_col)
-            col_copy.start()
-            rs_row.wait()
-            rs_out[...] = rs_in[...] + rs_land[0]
-            rs_col.start()
+
+    acc[span(mine, half), :] = go_own[...]
+    go_copy.wait()
+    fill(0, go_land[...])
+    for load in loads:
+        load.wait()
+    for lo in range(0, wide, 384):
+        row_send[0:half, lo : lo + 384] = dot(normed_t[half : 2 * half, :], p_all[:, lo : lo + 384]).astype(BF16)
+    row_copy.start()
+    rs_row.wait()
+    rs_out[...] = rs_in[...] + rs_land[0]
+    rs_col.start()
+    lo = 2 * chan
+    acc[misc : misc + half, :] = dot(normed_t[0:half, :], p_all[:, lo:wide])
+    acc[span(size + mine, half), :] = dot(normed_t[0:half, :], p_all[:, 0:chan])
+    row_copy.wait()
+    fill(1, row_land[0:half, 0:chan])
+    state = acc[misc : misc + half, 0:256] + row_land[0:half, lo : lo + 256].astype(F32)
+    extra = jnp.concatenate([small, norm_own[:, 0:256], norm_own[:, 256:512], pad6], axis=0)
+    extra = extra + row_land[half : half + 16, 0:256].astype(F32)
+    col_send[0:half, :] = state.astype(BF16)
+    col_send[half : half + 16, :] = extra.astype(BF16)
+    col_copy = remote(col_send, col_land, pair_send.at[1], pair_recv.at[1], to_col)
+    col_copy.start()
+    acc[span(2 * size + mine, half), :] = dot(normed_t[0:half, :], p_all[:, chan : 2 * chan])
+    fill(2, row_land[0:half, chan : 2 * chan])
     for i in range(DN_PARTS):
         rows = slice(i * cut, (i + 1) * cut)
         dn_rows[i].wait()
@@ -669,7 +707,7 @@
 
     lo = 2 * chan + 256
     acc[misc : misc + half, 256:384] = jnp.concatenate(
-        [g_cat[0:half, lo : lo + 64], row_land[0:half, lo : lo + 64].astype(F32)], axis=1
+        [acc[misc : misc + half, 256:320], row_land[0:half, lo : lo + 64].astype(F32)], axis=1
     )
     acc[misc + half : misc + half + 16, 256:384] = jnp.zeros((16, 128), F32)
     first = misc + half + 16
@@ -699,10 +737,9 @@
     rs_out[...] = rs_out[...] + rs_land[1]
 
 
-def sum_over_dp(dp, g_cat, go_own, go_rec, acc_v, acc_s, acc_h, acc_n, rs, dn_own, dn_rec):
-    half = g_cat.shape[0] // 2
-    wide = g_cat.shape[1]
-    chan = go_own.shape[0]
+def sum_over_dp(dp, normed_t, p_all, go_own, go_rec, acc_v, acc_s, acc_h, acc_n, rs, dn_own, dn_rec):
+    chan, half = go_own.shape
+    wide = p_all.shape[1]
     rows = 3 * big_rows(dp, 2 * half) + big_rows(dp, half + 40)
     bits = dp.bit_length() - 1
     tokens = dn_own.shape[0]
@@ -711,30 +748,35 @@
     act = jax.ShapeDtypeStruct((tokens, half), BF16)
     return pl.pallas_call(
         functools.partial(sum_kernel, dp),
-        in_specs=[vmem] * 9 + [hbm],
+        in_specs=[hbm] * 2 + [vmem] * 8 + [hbm],
         out_specs=[vmem, vmem, hbm, vmem],
         out_shape=[jax.ShapeDtypeStruct((rows, chan), BF16), act, act, jax.ShapeDtypeStruct(rs.shape, F32)],
         scratch_shapes=[
             pltpu.VMEM((rows, chan), F32),
             pltpu.VMEM((rows, chan), BF16),
             pltpu.VMEM((rows, chan), BF16),
-            pltpu.VMEM((half + 16, wide + half), BF16),
-            pltpu.VMEM((half + 16, wide + half), BF16),
+            pltpu.VMEM((half + 16, wide), BF16),
+            pltpu.VMEM((half + 16, wide), BF16),
             pltpu.VMEM((half + 16, 256), BF16),
             pltpu.VMEM((half + 16, 256), BF16),
             pltpu.VMEM((tokens, half), BF16),
             pltpu.VMEM((2,) + rs.shape, F32),
+            pltpu.VMEM(normed_t.shape, BF16),
+            pltpu.VMEM(p_all.shape, BF16),
+            pltpu.VMEM((chan, half), BF16),
+            pltpu.VMEM((chan, half), BF16),
+            pltpu.SemaphoreType.DMA((2,)),
             pltpu.SemaphoreType.DMA((4, 2 * bits)),
             pltpu.SemaphoreType.DMA((4, 2 * bits)),
-            pltpu.SemaphoreType.DMA((4,)),
-            pltpu.SemaphoreType.DMA((4,)),
+            pltpu.SemaphoreType.DMA((5,)),
+            pltpu.SemaphoreType.DMA((5,)),
             pltpu.SemaphoreType.DMA((2, DN_PARTS)),
             pltpu.SemaphoreType.DMA((2, DN_PARTS)),
         ],
         compiler_params=pltpu.CompilerParams(collective_id=0, has_side_effects=True),
         cost_estimate=pl.CostEstimate(flops=1_000_000, bytes_accessed=150_000_000, transcendentals=0),
         name="sum_over_dp",
-    )(g_cat, go_own, go_rec, acc_v, acc_s, acc_h, acc_n, rs, dn_own, dn_rec)
+    )(normed_t, p_all, go_own, go_rec, acc_v, acc_s, acc_h, acc_n, rs, dn_own, dn_rec)
 
 
 def finish_kernel(
@@ -746,7 +788,9 @@
     dn_sum,
     dn_col,
     proj_own,
-    proj_col,
+    proj_first,
+    proj_rest,
+    sel,
     trow,
     rows_in,
     rs,
@@ -757,17 +801,24 @@
     g_value,
     g_step,
     g_state,
-    small_a,
-    small_b,
-    small_h,
+    g_filter,
+    g_shift,
+    g_kernel,
+    g_offset,
+    g_decay,
+    g_bias,
+    g_skip,
+    g_norm,
+    g_gated,
     g_output,
 ):
     half = hid.shape[1]
-    step_rows = hid.shape[0]
     hid32 = hid[...].astype(F32)
     recip = rows_in[16:24, :]
     cols = jnp.transpose(jnp.concatenate([trow[0:8, :], rs[...] * recip * recip / width], axis=0))
-    proj = proj_own[...].astype(F32) + proj_col[...].astype(F32)
+    early = pl.program_id(0) < pl.num_programs(0) // 2
+    proj_col = jnp.where(early, proj_first[...].astype(F32), proj_rest[...].astype(F32))
+    proj = proj_own[...].astype(F32) + proj_col
     result[...] = (hid32 + cols[:, 0:1] * proj).astype(BF16)
     d_normed = dn_sum[...].astype(F32) + dn_col[...].astype(F32)
     hidden_grad[...] = cot[...].astype(F32) + d_normed * gains[0:1, :] - cols[:, 8:9] * hid32
@@ -786,14 +837,25 @@
         first = lax.axis_index("row") == 0
         g_step[...] = jnp.concatenate([jnp.where(first, own, rec), jnp.where(first, rec, own)], axis=0)
         small = out[misc + half : misc + half + 48, :].astype(F32)
-        small_a[...] = small[0:16, 0:256]
-        small_b[...] = small[16:24, :]
-        small_h[...] = jnp.transpose(small[24:40, 0:128])[0:8]
-
-
-def finish(size, heads, out, hid, cot, dn_sum, dn_col, proj_own, proj_col, trow, rows, rs, gains):
+        g_kernel[...] = small[0:4, 0:256]
+        g_offset[...] = small[4, 0:256]
+        g_norm[0:256] = small[8, 0:256]
+        g_norm[256:half] = small[9, 0 : half - 256]
+        g_filter[...] = small[16:20]
+        g_shift[...] = small[20]
+        g_gated[...] = small[22]
+        head = jnp.transpose(small[24:40, 0:128])[0:8]
+        g_decay[...] = head[0, 0:heads]
+        g_bias[...] = head[0, 8 : 8 + heads]
+        skip = dot_nt(small[16:32].astype(BF16), sel[...])
+        g_skip[...] = skip[5, 0:heads]
+
+
+def finish(size, heads, out, hid, cot, dn_sum, dn_col, proj_own, proj_first, proj_rest, sel, trow, rows, rs, gains):
     tokens, half = hid.shape
     chan = out.shape[1]
+    grid = tokens // STEP
+    split = grid // 2
 
     def blk(cols):
         return pl.BlockSpec((STEP, cols), lambda i: (i, 0))
@@ -802,21 +864,27 @@
         return pl.BlockSpec((count, STEP), lambda i: (0, i))
 
     def whole(shape):
-        return pl.BlockSpec(shape, lambda i: (0, 0))
+        return pl.BlockSpec(shape, lambda i: (0,) * len(shape))
 
     shapes = [
         (half, 2 * chan),
         (half, 2 * chan),
         (2 * heads, half),
         (half, 256),
-        (16, 256),
-        (8, chan),
-        (8, 16),
+        (4, chan),
+        (chan,),
+        (4, 256),
+        (256,),
+        (heads,),
+        (heads,),
+        (heads,),
+        (half,),
+        (chan,),
         (2 * chan, half),
     ]
     return pl.pallas_call(
         functools.partial(finish_kernel, 2 * half, size),
-        grid=(tokens // STEP,),
+        grid=(grid,),
         in_specs=[
             whole(out.shape),
             blk(half),
@@ -824,9 +892,11 @@
             blk(half),
             blk(half),
             blk(half),
-            blk(half),
+            pl.BlockSpec((STEP, half), lambda i: (jnp.minimum(i, split - 1), 0)),
+            pl.BlockSpec((STEP, half), lambda i: (jnp.maximum(i - split, 0), 0)),
+            whole(sel.shape),
             row(16),
-            row(32),
+            row(24),
             row(8),
             whole((8, half)),
         ],
@@ -838,7 +908,7 @@
         + [jax.ShapeDtypeStruct(shape, F32) for shape in shapes],
         cost_estimate=pl.CostEstimate(flops=20_000_000, bytes_accessed=20_000_000, transcendentals=0),
         name="finish",
-    )(out, hid, cot, dn_sum, dn_col, proj_own, proj_col, trow, rows, rs, gains)
+    )(out, hid, cot, dn_sum, dn_col, proj_own, proj_first, proj_rest, sel, trow, rows, rs, gains)
 
 
 def swap(x, axis):
@@ -910,8 +980,14 @@
 
     wide = w_own.shape[1]
 
+    last = grid - 1
+    col_blocks = grid // 2
+
     def blk(cols):
-        return pl.BlockSpec((STEP, cols), lambda i: (i, 0))
+        return pl.BlockSpec((STEP, cols), lambda i: (jnp.minimum(i, last), 0))
+
+    def row_blk(count):
+        return pl.BlockSpec((count, STEP), lambda i: (0, jnp.minimum(i, last)))
 
     def whole(shape):
         return pl.BlockSpec(shape, lambda i: (0, 0))
@@ -919,9 +995,23 @@
     def arr(cols, dtype=F32):
         return jax.ShapeDtypeStruct((tokens, cols), dtype)
 
-    mixed, po_own, po_rec, pre_gate, pre_value, conv_value, pre_shared, conv_shared, y_scan, states, rows, normed_t = pl.pallas_call(
-        functools.partial(forward_kernel, steps_per_seq, width),
-        grid=(grid,),
+    (
+        mixed,
+        proj_own,
+        proj_first,
+        trow,
+        pre_gate,
+        pre_value,
+        conv_value,
+        pre_shared,
+        conv_shared,
+        y_scan,
+        states,
+        rows,
+        normed_t,
+    ) = pl.pallas_call(
+        functools.partial(forward_kernel, steps_per_seq, width, inner_width, col_blocks),
+        grid=(grid + 1,),
         in_specs=[
             blk(half),
             blk(half),
@@ -933,11 +1023,13 @@
             whole((16, 128)),
             whole((chan, half)),
             whole((chan, half)),
+            pl.BlockSpec((STEP, half), lambda i: (jnp.maximum(i - 1, 0), 0)),
         ],
         out_specs=[
             blk(chan),
-            blk(half),
-            blk(half),
+            whole((tokens, half)),
+            pl.BlockSpec(memory_space=pl.ANY),
+            whole((16, tokens)),
             blk(chan),
             blk(chan),
             blk(chan),
@@ -945,13 +1037,14 @@
             blk(256),
             blk(chan),
             blk(chan),
-            pl.BlockSpec((32, STEP), lambda i: (0, i)),
-            pl.BlockSpec((width, STEP), lambda i: (0, i)),
+            row_blk(24),
+            row_blk(width),
         ],
         out_shape=[
             arr(chan, BF16),
             arr(half, BF16),
-            arr(half, BF16),
+            jax.ShapeDtypeStruct((col_blocks * STEP, half), BF16),
+            jax.ShapeDtypeStruct((16, tokens), F32),
             arr(chan),
             arr(chan),
             arr(chan),
@@ -959,25 +1052,34 @@
             arr(256),
             arr(chan),
             arr(chan, BF16),
-            jax.ShapeDtypeStruct((32, tokens), F32),
+            jax.ShapeDtypeStruct((24, tokens), F32),
             jax.ShapeDtypeStruct((width, tokens), BF16),
         ],
         scratch_shapes=[
             pltpu.VMEM((128, chan), F32),
             pltpu.VMEM((STEP + 8, chan), F32),
             pltpu.VMEM((STEP + 8, 256), F32),
+            pltpu.VMEM((tokens, half), BF16),
+            pltpu.VMEM((tokens, half), BF16),
+            pltpu.VMEM((tokens, half), BF16),
+            pltpu.VMEM((tokens, half), BF16),
+            pltpu.VMEM((16, STEP), F32),
+            pltpu.VMEM((3, 16, STEP), F32),
+            pltpu.SemaphoreType.DMA((grid,)),
+            pltpu.SemaphoreType.DMA((grid,)),
+            pltpu.SemaphoreType.DMA((col_blocks,)),
+            pltpu.SemaphoreType.DMA((col_blocks,)),
+            pltpu.SemaphoreType.DMA((3,)),
+            pltpu.SemaphoreType.DMA((3,)),
         ],
+        compiler_params=pltpu.CompilerParams(collective_id=1, has_side_effects=True),
         cost_estimate=pl.CostEstimate(flops=12_000_000_000, bytes_accessed=40_000_000, transcendentals=8_000_000),
         name="forward_core",
-    )(hidden, hid_rec, gains, w_own, w_rec, vtap, stap, head_par, wo_own, wo_rec)
-
-    proj_own, trow = mid_exchange(inner_width, rows, cotangent, po_own, po_rec)
-    proj_col = swap(proj_own, "col")
+    )(hidden, hid_rec, gains, w_own, w_rec, vtap, stap, head_par, wo_own, wo_rec, cotangent)
+    proj_rest = swap(proj_own[col_blocks * STEP :], "col")
 
     lane_head = jnp.arange(chan) // (chan // heads)
     sel = (jnp.arange(16)[:, None] == lane_head[None, :]).astype(BF16)
-    last = grid - 1
-
     def rblk(cols):
         return pl.BlockSpec((STEP, cols), lambda i: (last - i, 0))
 
@@ -993,7 +1095,7 @@
             whole((chan, half)),
             whole((chan, half)),
             rrow(16),
-            rrow(32),
+            rrow(24),
             rblk(chan),
             rblk(chan),
             rblk(chan),
@@ -1069,32 +1171,28 @@
         hid_rec,
     )
 
-    g_cat = dot(normed_t, p_all)
     out, dn_sum, dn_col, rs = sum_over_dp(
-        dp, g_cat, go_own, go_rec, acc_v, acc_s, acc_h, acc_n, rsum, dn_own, dn_rec
+        dp, normed_t, p_all, go_own, go_rec, acc_v, acc_s, acc_h, acc_n, rsum, dn_own, dn_rec
     )
     size = big_rows(dp, 2 * half)
-    result, hidden_grad, g_gate, g_value, g_step, g_state, sm_a, sm_b, sm_h, g_output = finish(
-        size, heads, out, hidden, cotangent, dn_sum, dn_col, proj_own, proj_col, trow, rows, rs, gains
+    outs = finish(
+        size,
+        heads,
+        out,
+        hidden,
+        cotangent,
+        dn_sum,
+        dn_col,
+        proj_own,
+        proj_first,
+        proj_rest,
+        sel,
+        trow,
+        rows,
+        rs,
+        gains,
     )
-    return (
-        result,
-        hidden_grad,
-        g_gate,
-        g_value,
-        g_step.T,
-        g_state,
-        sm_b[0:4],
-        sm_b[4],
-        sm_a[0:4],
-        sm_a[4],
-        sm_h[0, 0:heads],
-        sm_h[0, 8 : 8 + heads],
-        jnp.sum(sm_b[5].reshape(heads, chan // heads), axis=1),
-        sm_a[8:10].reshape(512)[0:half],
-        sm_b[6],
-        g_output,
-    )
+    return tuple(outs[0:4]) + (outs[4].T,) + tuple(outs[5:])
 
 
 def solution(mesh):

time: 193 us -> 179 us (0.927)
  matrix products: 9.37 us -> 0 us
  local copies, waits for them, and re-layouts: 14.5 us -> 7.07 us
  Pallas kernels: 161 us -> 164 us
    dot_general x1 -> x0, matrix products: 9.37 us -> none  [dot(): return jnp.dot(a, b, preferred_element_type=F32)]
    slice x4 -> x1, local copies, waits for them, and re-layouts: 5.27 us -> 1.21 us  [body(): proj_rest = swap(proj_own[col_blocks * STEP:], 'col')]
    pallas_call x4 -> x3, Pallas kernels: 122 us -> 124 us  [the longest x1 69.6 us: sum_over_dp(): pl.pallas_call(functools.partial(sum_kernel, dp), in_specs=[hbm] * 2 + [v...]
    unnamed x34 -> x30, local copies, waits for them, and re-layouts: 3.39 us -> 1.31 us
  transfers between devices with their start and end apart: 6 -> 6, of which waited for: 0 -> 0; matrix products, arithmetic and copies ran while one was open for 9% -> 5% of each run, Pallas kernels for 77% -> 85%
where the time goes in v4:
time: 179 us; the launch traced here: 178 us
  Pallas kernels  164 us (92%)
  local copies, waits for them, and re-layouts  7.07 us (4%)
  starting transfers between devices  3.27 us (2%)
  other arithmetic  3.09 us (2%)
    pallas_call x1, Pallas kernels, sum_over_dp(): pl.pallas_call(functools.partial(sum_kernel, dp), in_specs=[hbm] * 2 + [v...  69.6 us
    pallas_call x1, Pallas kernels, body(): pl.pallas_call(functools.partial(forward_kernel, steps_per_seq, width, in...  43 us
    pallas_call x1, Pallas kernels, body(): pl.pallas_call(functools.partial(backward_kernel, steps_per_seq), grid=(g...  39.2 us
    pallas_call x1, Pallas kernels, finish(): pl.pallas_call(functools.partial(finish_kernel, 2 * half, size), grid=(gr...  11.9 us
  transfers between devices with their start and end apart: 6, of which 0 were waited for; matrix products, arithmetic and copies ran while one was open for 5% of the time, Pallas kernels for 85%

profile of v4, /device:TPU:0, one launch (start us, length us, event | category | flops | bytes accessed | tf_op | source)
XLA Modules:
  0.0 178.2 jit_solution(8147470014434003045)
XLA Ops:
  0.7 0.6 collective-permute-start
  1.2 0.8 constant_dynamic-slice_fusion.2
  2.0 0.2 copy.34
  2.2 0.2 copy.35
  2.4 1.4 constant_dynamic-slice_fusion.3
  3.9 1.1 fusion.3
  5.0 0.8 constant_dynamic-slice_fusion
  5.7 0.5 collective-permute-start.3
  6.3 0.5 collective-permute-start.4
  6.7 0.1 pad.22.clone
  6.8 0.7 maximum_maximum_fusion.1.stap
  7.5 0.6 fusion.4.sel_ref.sel
  8.2 0.1 pad.33.clone
  8.3 0.1 broadcast_in_dim_reshape.3
  8.5 0.6 concatenate.21.vtap
  9.1 0.7 maximum_maximum_fusion.gains
  9.8 0.7 broadcast_in_dim.48.head_par
  10.5 43.0 %forward_core.1 = (bf16[2048,384]{1,0:T(8,128)(2,1)}, bf16[2048,384]{1,0:T(8,128)(2,1)}, bf16[1024,384]{1,0:T(8,128)(2,1)}, f32[16,2048]{1,0:T(8,128)}, f32[2048...) custom-call(bf16[2048,384]{1,0:T(8,128)(2,1)} %hid.1, ...), custom_call_target="tpu_custom_call" | custom-call | flops 12000000000 | bytes 40000000 | tf_op jit(solution)/shard_map/forward_core/pallas_call | solution.py:1012
  53.4 1.2 slice.3
  54.7 1.7 collective-permute-start.5
  56.4 39.2 %backward_core.1 = (bf16[2048,1152]{1,0:T(8,128)(2,1)}, bf16[2048,384]{1,0:T(8,128)(2,1)}, bf16[2048,384]{1,0:T(8,128)(2,1)}, f32[8,2048]{1,0:T(8,128)}, f32[56,...) custom-call(bf16[2048,384]{1,0:T(8,128)(2,1)} %cot.3, ...), custom_call_target="tpu_custom_call" | custom-call | flops 24000000000 | bytes 60000000 | tf_op jit(solution)/shard_map/backward_core/pallas_call | solution.py:1089
  95.6 69.6 %sum_over_dp.1 = (bf16[2816,384]{1,0:T(8,128)(2,1)}, bf16[2048,384]{1,0:T(8,128)(2,1)}, bf16[2048,384]{1,0:T(8,128)(2,1)}, f32[8,2048]{1,0:T(8,128)}) custom-call(bf16[768,2048]{1,0:T(8,128)(2,1)} %get-tuple-element.59.normed_t_hbm, bf16[2048,1152]{1,0:T(8,128)(2,1)} %get-tuple-element.70.p_hbm, f32[384,384]{1,0:T(8,128)} %get-tuple-element.71.go_own, ...), custom_call_target="tpu_custom_call" | custom-call | flops 1000000 | bytes 150000000 | tf_op jit(solution)/shard_map/sum_over_dp/pallas_call | solution.py:749
  165.3 0.9 copy-done.1
  166.1 11.9 %finish.1 = (bf16[2048,384]{1,0:T(8,128)(2,1)}, f32[2048,384]{1,0:T(8,128)}, f32[384,768]{1,0:T(8,128)}, f32[384,768]{1,0:T(8,128)}, f32[12,384]{1,0:T(8,128)}, ...) custom-call(bf16[2816,384]{1,0:T(8,128)(2,1)} %get-tuple-element.80., ...), custom_call_target="tpu_custom_call" | custom-call | flops 20000000 | bytes 20000000 | tf_op jit(solution)/shard_map/finish/pallas_call | solution.py:885
  (46 shorter events, 0.3 us)
Async XLA Ops:
  0.6 3.1 %copy-start.3 = (bf16[384,256]{1,0:T(8,128)(2,1)S(1)}, bf16[384,256]{1,0:T(8,128)(2,1)}, u32[]{:S(2)}) copy-start(bf16[384,256]{1,0:T(8,128)(2,1)} %param.20) | copy-start | bytes 589828
  0.7 9.1 %collective-permute-start = (bf16[2048,384]{1,0:T(8,128)(2,1)}, bf16[2048,384]{1,0:T(8,128)(2,1)}, u32[]{:S(2)}, u32[]{:S(2)}) collective-permute-start(bf16[2048,384]{1,0:T(8,128)(2,1)} %hid.1), channel_id=1, source_target_pairs={{0,2},{2,0},{1,3},{3,1},{4,6},{6,4},{5,7},{7,5},{8,10},{10,8},{9,1... | collective-permute-start | bytes 4718600 | tf_op jit(solution)/shard_map/ppermute | solution.py:915
  3.7 1.2 copy-start.2
  3.7 2.5 %copy-start.7 = (f32[384]{0:T(512)S(1)}, f32[384]{0:T(512)}, u32[]{:S(2)}) copy-start(f32[384]{0:T(512)} %param.28) | copy-start | bytes 4612
  3.8 2.5 %copy-start = (bf16[2048,384]{1,0:T(8,128)(2,1)S(1)}, bf16[2048,384]{1,0:T(8,128)(2,1)}, u32[]{:S(2)}) copy-start(bf16[2048,384]{1,0:T(8,128)(2,1)} %cot.3) | copy-start | bytes 4718596
  3.8 3.1 %copy-start.5 = (f32[4,256]{1,0:T(4,128)S(1)}, f32[4,256]{1,0:T(4,128)}, u32[]{:S(2)}) copy-start(f32[4,256]{1,0:T(4,128)} %param.23) | copy-start | bytes 12292
  3.8 3.0 %copy-start.8 = (f32[256]{0:T(256)S(1)}, f32[256]{0:T(256)}, u32[]{:S(2)}) copy-start(f32[256]{0:T(256)} %param.24) | copy-start | bytes 3076
  3.8 4.3 %copy-start.12 = (f32[6]{0:T(128)S(1)}, f32[6]{0:T(128)}, u32[]{:S(2)}) copy-start(f32[6]{0:T(128)} %param.25) | copy-start | bytes 76
  3.8 4.3 %copy-start.13 = (f32[6]{0:T(128)S(1)}, f32[6]{0:T(128)}, u32[]{:S(2)}) copy-start(f32[6]{0:T(128)} %param.26) | copy-start | bytes 76
  3.8 4.5 %copy-start.10 = (f32[6]{0:T(128)S(1)}, f32[6]{0:T(128)}, u32[]{:S(2)}) copy-start(f32[6]{0:T(128)} %param.27) | copy-start | bytes 76
  3.8 4.6 %copy-start.6 = (f32[384]{0:T(512)S(1)}, f32[384]{0:T(512)}, u32[]{:S(2)}) copy-start(f32[384]{0:T(512)} %param.22) | copy-start | bytes 4612
  3.8 4.6 %copy-start.9 = (bf16[384]{0:T(512)(128)(2,1)S(1)}, bf16[384]{0:T(512)(128)(2,1)}, u32[]{:S(2)}) copy-start(bf16[384]{0:T(512)(128)(2,1)} %param.29) | copy-start | bytes 2308
  3.9 4.6 %copy-start.4 = (f32[4,384]{1,0:T(4,128)S(1)}, f32[4,384]{1,0:T(4,128)}, u32[]{:S(2)}) copy-start(f32[4,384]{1,0:T(4,128)} %param.21) | copy-start | bytes 18436
  4.9 4.8 %collective-permute-start.2 = (bf16[384,1152]{1,0:T(8,128)(2,1)S(1)}, bf16[384,1152]{1,0:T(8,128)(2,1)}, u32[]{:S(2)}, u32[]{:S(2)}) collective-permute-start(bf16[384,1152]{1,0:T(8,128)(2,1)S(1)} %get-tuple-element.108), channel_id=1, source_target_pairs={{0,2},{2,0},{1,3},{3,1},{4,6},{6,4},{5,7},{7,5},{8,10},{10,8},{9,1... | collective-permute-start | bytes 2654216 | tf_op jit(solution)/shard_map/ppermute | solution.py:915
  5.7 4.0 %collective-permute-start.3 = (bf16[384,384]{1,0:T(8,128)(2,1)S(1)}, bf16[384,384]{1,0:T(8,128)(2,1)S(1)}, u32[]{:S(2)}, u32[]{:S(2)}) collective-permute-start(bf16[384,384]{1,0:T(8,128)(2,1)S(1)} %get-tuple-element.102), channel_id=1, source_target_pairs={{0,2},{2,0},{1,3},{3,1},{4,6},{6,4},{5,7},{7,5},{8,10},{10,8},{9,1... | collective-permute-start | bytes 884744 | tf_op jit(solution)/shard_map/ppermute | solution.py:915
  6.2 2.9 %collective-permute-start.1 = (f32[384]{0:T(512)S(1)}, f32[384]{0:T(512)S(1)}, u32[]{:S(2)}, u32[]{:S(2)}) collective-permute-start(f32[384]{0:T(512)S(1)} %copy-done.7), channel_id=1, source_target_pairs={{0,2},{2,0},{1,3},{3,1},{4,6},{6,4},{5,7},{7,5},{8,10},{10,8},{9,1... | collective-permute-start | bytes 4616 | tf_op jit(solution)/shard_map/ppermute | solution.py:915
  6.3 50.1 %collective-permute-start.4 = (bf16[2048,384]{1,0:T(8,128)(2,1)S(1)}, bf16[2048,384]{1,0:T(8,128)(2,1)}, u32[]{:S(2)}, u32[]{:S(2)}) collective-permute-start(bf16[2048,384]{1,0:T(8,128)(2,1)S(1)} %copy-done), channel_id=1, source_target_pairs={{0,2},{2,0},{1,3},{3,1},{4,6},{6,4},{5,7},{7,5},{8,10},{10,8},{9,1... | collective-permute-start | bytes 4718600 | tf_op jit(solution)/shard_map/ppermute | solution.py:915
  9.8 0.7 copy-start.11
  54.7 110.6 %collective-permute-start.5 = (bf16[1024,384]{1,0:T(8,128)(2,1)S(1)}, bf16[1024,384]{1,0:T(8,128)(2,1)S(1)}, u32[]{:S(2)}, u32[]{:S(2)}) collective-permute-start(bf16[1024,384]{1,0:T(8,128)(2,1)S(1)} %slice.3), channel_id=1, source_target_pairs={{0,1},{1,0},{2,3},{3,2},{4,5},{5,4},{6,7},{7,6},{8,9},{9,8},{10,11... | collective-permute-start | bytes 2359304 | tf_op jit(solution)/shard_map/ppermute | solution.py:915
  165.3 0.9 copy-start.1

commit v5 on v4

--- a/solution.py
+++ b/solution.py
@@ -15,6 +15,9 @@
 BF16 = jnp.bfloat16
 SWAP = [(0, 1), (1, 0)]
 DN_PARTS = 4
+AR_SPLIT = 2
+AR_FAR = (1, 3)
+AR_MISC = 3
 
 
 def dot(a, b):
@@ -49,6 +52,10 @@
     parts = jnp.concatenate([hi, mid, low, jnp.zeros_like(x)], axis=0).astype(BF16)
     out = dot(parts, mat)
     return out[0:8] + out[8:16] + out[16:24]
+
+
+def plain_sums(sel, z):
+    return dot_nt(sel, z.astype(BF16))[0:8]
 
 
 def head_sums(sel, z):
@@ -146,20 +153,6 @@
     def _():
         greet(targets)
 
-    @pl.when(step > 0)
-    def _():
-        i = step - 1
-        row_copy(i).wait()
-        part = po_own[span(i), :].astype(F32) + po_land[span(i), :].astype(F32)
-        proj_s[span(i), :] = part.astype(BF16)
-
-        @pl.when(i < col_blocks)
-        def _():
-            col_copy(i).start()
-
-        dots = head_sums(jnp.ones((16, cot.shape[1]), BF16), part * cot[...].astype(F32))
-        sums[pl.ds(8 + i, 1), :] = dots[0:1]
-
     @pl.when(step < blocks)
     def _():
         forward_block(
@@ -170,6 +163,23 @@
             (y_out, state_out, rows_out, nt_out),
             (state, vbuf, sbuf, po_own.at[span(step), :], po_send.at[span(step), :], sums.at[pl.ds(step, 1), :]),
         )
+
+    @pl.when(step > 0)
+    def _():
+        i = step - 1
+        row_copy(i).wait()
+        part = po_own[span(i), :].astype(F32) + po_land[span(i), :].astype(F32)
+        proj_s[span(i), :] = part.astype(BF16)
+
+        @pl.when(i < col_blocks)
+        def _():
+            col_copy(i).start()
+
+        dots = plain_sums(jnp.ones((16, cot.shape[1]), BF16), part * cot[...].astype(F32))
+        sums[pl.ds(8 + i, 1), :] = dots[0:1]
+
+    @pl.when(step < blocks)
+    def _():
         row_copy(step).start()
 
     @pl.when(step == blocks)
@@ -286,7 +296,7 @@
     weighted = (mix * vtap[6:7, :]).astype(BF16)
     po_own[...] = dot(weighted, wo_own[...]).astype(BF16)
     po_send[...] = dot(weighted, wo_rec[...]).astype(BF16)
-    square_row[...] = head_sums(jnp.ones((16, chan), BF16), mix * mix)[0:1]
+    square_row[...] = plain_sums(jnp.ones((16, chan), BF16), mix * mix)[0:1]
 
 
 def backward_kernel(
@@ -435,8 +445,8 @@
             z_sum = z_sum + head_sums(
                 sel_p, dys_bf.astype(F32) * y_in[lo:hi, pl0:pl1] - xh_bf.astype(F32) * inner
             )
-            e_sum = e_sum + head_sums(sel_p, xh * outer)
-            f_sum = f_sum + head_sums(sel_p, xs * u)
+            e_sum = e_sum + plain_sums(sel_p, xh * outer)
+            f_sum = f_sum + plain_sums(sel_p, xs * u)
             decay_row = jnp.exp(last)
             gh_row = decay_row * jnp.sum(g * held.astype(F32), axis=0, keepdims=True)
             gh = gh + jnp.sum(sel_f[:, pl0:pl1] * gh_row, axis=1, keepdims=True)
@@ -478,8 +488,8 @@
     p_out[:, chan : 2 * chan] = (recip * d_value).astype(BF16)
     p_out[:, 2 * chan : 2 * chan + 256] = (recip * d_shared).astype(BF16)
     ones = jnp.ones((16, chan), BF16)
-    rsum_out[...] += head_sums(ones, d_gate * gate + d_value * pv)
-    rsum_out[...] += head_sums(ones[:, 0:256], d_shared * ps)
+    rsum_out[...] += plain_sums(ones, d_gate * gate + d_value * pv)
+    rsum_out[...] += plain_sums(ones[:, 0:256], d_shared * ps)
     pb = p_out[...]
     for n, (hid, weight, dn) in enumerate(((hid_own, w_own, dn_own), (hid_rec, w_rec, dn_rec))):
         part = dot_nt(pb, weight[...])
@@ -489,6 +499,11 @@
 
 def unit_rows(dp):
     return 16 * dp
+
+
+def misc_rows(dp, rows):
+    unit = max(unit_rows(dp), 256)
+    return pl.cdiv(rows, unit) * unit
 
 
 def big_rows(dp, rows):
@@ -554,8 +569,8 @@
     chan, half = go_own.shape
     wide = p_all.shape[1]
     size = big_rows(dp, 2 * half)
-    misc = 3 * size
-    tail = out.shape[0] - misc
+    tail = out.shape[0] - 3 * size
+    misc = 0
     bits = dp.bit_length() - 1
     me = lax.axis_index("dp")
     r = lax.axis_index("row")
@@ -612,13 +627,12 @@
     for copy in dn_rows:
         copy.start()
 
-    orders = [
-        tuple(range(bits)),
-        tuple(range(1, bits)) + (0,),
-        tuple(range(bits)),
-        tuple(range(bits)),
-    ]
-    bounds = [(0, size), (size, size), (2 * size, size), (misc, tail)]
+    near = tuple(range(bits))
+    far = tuple(range(1, bits)) + (0,)
+    part_rows = size // AR_SPLIT
+    bounds = [(tail + n * part_rows, part_rows) for n in range(3 * AR_SPLIT)] + [(misc, tail)]
+    orders = [far if n in AR_FAR else near for n in range(3 * AR_SPLIT + 1)]
+    misc_chunk = 3 * AR_SPLIT
     lows = {}
     flying = {}
 
@@ -669,12 +683,13 @@
     other = pl.multiple_of((1 - r) * half, 128)
 
     def fill(i, theirs):
-        acc[span(i * size + other, half), :] = theirs.astype(F32)
+        acc[span(tail + i * size + other, half), :] = theirs.astype(F32)
         if size > 2 * half:
-            acc[i * size + 2 * half : (i + 1) * size, :] = jnp.zeros((size - 2 * half, chan), F32)
-        start_level(i, 0)
-
-    acc[span(mine, half), :] = go_own[...]
+            acc[tail + i * size + 2 * half : tail + (i + 1) * size, :] = jnp.zeros((size - 2 * half, chan), F32)
+        for n in range(AR_SPLIT):
+            start_level(i * AR_SPLIT + n, 0)
+
+    acc[span(tail + mine, half), :] = go_own[...]
     go_copy.wait()
     fill(0, go_land[...])
     for load in loads:
@@ -687,7 +702,7 @@
     rs_col.start()
     lo = 2 * chan
     acc[misc : misc + half, :] = dot(normed_t[0:half, :], p_all[:, lo:wide])
-    acc[span(size + mine, half), :] = dot(normed_t[0:half, :], p_all[:, 0:chan])
+    acc[span(tail + size + mine, half), :] = dot(normed_t[0:half, :], p_all[:, 0:chan])
     row_copy.wait()
     fill(1, row_land[0:half, 0:chan])
     state = acc[misc : misc + half, 0:256] + row_land[0:half, lo : lo + 256].astype(F32)
@@ -697,7 +712,7 @@
     col_send[half : half + 16, :] = extra.astype(BF16)
     col_copy = remote(col_send, col_land, pair_send.at[1], pair_recv.at[1], to_col)
     col_copy.start()
-    acc[span(2 * size + mine, half), :] = dot(normed_t[0:half, :], p_all[:, chan : 2 * chan])
+    acc[span(tail + 2 * size + mine, half), :] = dot(normed_t[0:half, :], p_all[:, chan : 2 * chan])
     fill(2, row_land[0:half, chan : 2 * chan])
     for i in range(DN_PARTS):
         rows = slice(i * cut, (i + 1) * cut)
@@ -719,18 +734,19 @@
     )
     if misc + tail > first + 24:
         acc[first + 24 : misc + tail, :] = jnp.zeros((misc + tail - first - 24, chan), F32)
-    end_level(0, 0)
+    for n in range(AR_SPLIT):
+        end_level(n, 0)
     col_copy.wait()
     acc[misc : misc + half + 16, 0:256] = col_send[...].astype(F32) + col_land[...].astype(F32)
-    start_level(3, 0)
-    end_level(1, 0)
-    end_level(2, 0)
+    start_level(misc_chunk, 0)
+    for n in range(AR_SPLIT, misc_chunk):
+        end_level(n, 0)
     for level in range(1, 2 * bits):
-        for i in (0, 1):
-            end_level(i, level)
-        end_level(3, level - 1)
-        end_level(2, level)
-    end_level(3, 2 * bits - 1)
+        for n in range(misc_chunk):
+            end_level(n, level)
+            if n == AR_MISC:
+                end_level(misc_chunk, level - 1)
+    end_level(misc_chunk, 2 * bits - 1)
     rs_col.wait()
     for copy in dn_cols:
         copy.wait()
@@ -740,7 +756,7 @@
 def sum_over_dp(dp, normed_t, p_all, go_own, go_rec, acc_v, acc_s, acc_h, acc_n, rs, dn_own, dn_rec):
     chan, half = go_own.shape
     wide = p_all.shape[1]
-    rows = 3 * big_rows(dp, 2 * half) + big_rows(dp, half + 40)
+    rows = 3 * big_rows(dp, 2 * half) + misc_rows(dp, half + 48)
     bits = dp.bit_length() - 1
     tokens = dn_own.shape[0]
     vmem = pl.BlockSpec(memory_space=pltpu.VMEM)
@@ -766,8 +782,8 @@
             pltpu.VMEM((chan, half), BF16),
             pltpu.VMEM((chan, half), BF16),
             pltpu.SemaphoreType.DMA((2,)),
-            pltpu.SemaphoreType.DMA((4, 2 * bits)),
-            pltpu.SemaphoreType.DMA((4, 2 * bits)),
+            pltpu.SemaphoreType.DMA((3 * AR_SPLIT + 1, 2 * bits)),
+            pltpu.SemaphoreType.DMA((3 * AR_SPLIT + 1, 2 * bits)),
             pltpu.SemaphoreType.DMA((5,)),
             pltpu.SemaphoreType.DMA((5,)),
             pltpu.SemaphoreType.DMA((2, DN_PARTS)),
@@ -781,8 +797,12 @@
 
 def finish_kernel(
     width,
-    size,
-    out,
+    out_rows,
+    gate_a,
+    gate_b,
+    value_a,
+    value_b,
+    misc,
     hid,
     cot,
     dn_sum,
@@ -822,21 +842,23 @@
     result[...] = (hid32 + cols[:, 0:1] * proj).astype(BF16)
     d_normed = dn_sum[...].astype(F32) + dn_col[...].astype(F32)
     hidden_grad[...] = cot[...].astype(F32) + d_normed * gains[0:1, :] - cols[:, 8:9] * hid32
-    misc = 3 * size
+    @pl.when(pl.program_id(0) < half // 128)
+    def _():
+        g_output[...] = out_rows[...].astype(F32)
+        g_gate[:, 0:half] = gate_a[...].astype(F32)
+        g_gate[:, half : 2 * half] = gate_b[...].astype(F32)
+        g_value[:, 0:half] = value_a[...].astype(F32)
+        g_value[:, half : 2 * half] = value_b[...].astype(F32)
 
     @pl.when(pl.program_id(0) == 0)
     def _():
-        g_output[...] = out[0 : g_output.shape[0], :].astype(F32)
-        for n, ref in ((1, g_gate), (2, g_value)):
-            ref[:, 0:half] = out[n * size : n * size + half, :].astype(F32)
-            ref[:, half : 2 * half] = out[n * size + half : n * size + 2 * half, :].astype(F32)
-        g_state[...] = out[misc : misc + half, 0:256].astype(F32)
-        step_t = jnp.transpose(out[misc : misc + half, 256:384].astype(F32))
+        g_state[...] = misc[0:half, 0:256].astype(F32)
+        step_t = jnp.transpose(misc[0:half, 256:384].astype(F32))
         heads = g_step.shape[0] // 2
         own, rec = step_t[0:heads], step_t[64 : 64 + heads]
         first = lax.axis_index("row") == 0
         g_step[...] = jnp.concatenate([jnp.where(first, own, rec), jnp.where(first, rec, own)], axis=0)
-        small = out[misc + half : misc + half + 48, :].astype(F32)
+        small = misc[half : half + 48, :].astype(F32)
         g_kernel[...] = small[0:4, 0:256]
         g_offset[...] = small[4, 0:256]
         g_norm[0:256] = small[8, 0:256]
@@ -854,21 +876,29 @@
 def finish(size, heads, out, hid, cot, dn_sum, dn_col, proj_own, proj_first, proj_rest, sel, trow, rows, rs, gains):
     tokens, half = hid.shape
     chan = out.shape[1]
-    grid = tokens // STEP
-    split = grid // 2
+    size_f = tokens // 4
+    grid = 4
+    split = 2
 
     def blk(cols):
-        return pl.BlockSpec((STEP, cols), lambda i: (i, 0))
+        return pl.BlockSpec((size_f, cols), lambda i: (i, 0))
 
     def row(count):
-        return pl.BlockSpec((count, STEP), lambda i: (0, i))
+        return pl.BlockSpec((count, size_f), lambda i: (0, i))
 
     def whole(shape):
         return pl.BlockSpec(shape, lambda i: (0,) * len(shape))
 
-    shapes = [
-        (half, 2 * chan),
-        (half, 2 * chan),
+    parts = half // 128
+    tail = out.shape[0] - 3 * size
+
+    def part(start):
+        return pl.BlockSpec((128, chan), lambda i: (start // 128 + jnp.minimum(i, parts - 1), 0))
+
+    def streamed(rows, cols):
+        return pl.BlockSpec((rows // parts, cols), lambda i: (jnp.minimum(i, parts - 1), 0))
+
+    small = [
         (2 * heads, half),
         (half, 256),
         (4, chan),
@@ -880,27 +910,35 @@
         (heads,),
         (half,),
         (chan,),
-        (2 * chan, half),
     ]
+    big = (half, 2 * chan)
+    shapes = [big, big] + small + [(2 * chan, half)]
     return pl.pallas_call(
-        functools.partial(finish_kernel, 2 * half, size),
+        functools.partial(finish_kernel, 2 * half),
         grid=(grid,),
         in_specs=[
-            whole(out.shape),
+            pl.BlockSpec((256, half), lambda i: (tail // 256 + jnp.minimum(i, parts - 1), 0)),
+            part(tail + size),
+            part(tail + size + half),
+            part(tail + 2 * size),
+            part(tail + 2 * size + half),
+            whole((tail, chan)),
             blk(half),
             blk(half),
             blk(half),
             blk(half),
             blk(half),
-            pl.BlockSpec((STEP, half), lambda i: (jnp.minimum(i, split - 1), 0)),
-            pl.BlockSpec((STEP, half), lambda i: (jnp.maximum(i - split, 0), 0)),
+            pl.BlockSpec((size_f, half), lambda i: (jnp.minimum(i, split - 1), 0)),
+            pl.BlockSpec((size_f, half), lambda i: (jnp.maximum(i - split, 0), 0)),
             whole(sel.shape),
             row(16),
             row(24),
             row(8),
             whole((8, half)),
         ],
-        out_specs=[blk(half), blk(half)] + [whole(shape) for shape in shapes],
+        out_specs=[blk(half), blk(half), streamed(*big), streamed(*big)]
+        + [whole(shape) for shape in small]
+        + [streamed(2 * chan, half)],
         out_shape=[
             jax.ShapeDtypeStruct((tokens, half), BF16),
             jax.ShapeDtypeStruct((tokens, half), F32),
@@ -908,7 +946,26 @@
         + [jax.ShapeDtypeStruct(shape, F32) for shape in shapes],
         cost_estimate=pl.CostEstimate(flops=20_000_000, bytes_accessed=20_000_000, transcendentals=0),
         name="finish",
-    )(out, hid, cot, dn_sum, dn_col, proj_own, proj_first, proj_rest, sel, trow, rows, rs, gains)
+    )(
+        out,
+        out,
+        out,
+        out,
+        out,
+        out,
+        hid,
+        cot,
+        dn_sum,
+        dn_col,
+        proj_own,
+        proj_first,
+        proj_rest,
+        sel,
+        trow,
+        rows,
+        rs,
+        gains,
+    )
 
 
 def swap(x, axis):

time: 179 us -> 163 us (0.911)
  Pallas kernels: 164 us -> 148 us
    pallas_call x1, Pallas kernels: 43 us -> 34.8 us  [body(): pl.pallas_call(functools.partial(forward_kernel, steps_per_seq, width, in...]
    pallas_call x1, Pallas kernels: 69.6 us -> 65.5 us  [sum_over_dp(): pl.pallas_call(functools.partial(sum_kernel, dp), in_specs=[hbm] * 2 + [v...]
    pallas_call x1, Pallas kernels: 11.9 us -> 9.35 us  [finish(): pl.pallas_call(functools.partial(finish_kernel, 2 * half), grid=(grid,),...]
  transfers between devices with their start and end apart: 6 -> 6, of which waited for: 0 -> 0; matrix products, arithmetic and copies ran while one was open for 5% -> 6% of each run, Pallas kernels for 85% -> 85%
where the time goes in v5:
time: 163 us; the launch traced here: 162 us
  Pallas kernels  148 us (91%)
  local copies, waits for them, and re-layouts  7.07 us (4%)
  starting transfers between devices  3.27 us (2%)
  other arithmetic  3.09 us (2%)
    pallas_call x1, Pallas kernels, sum_over_dp(): pl.pallas_call(functools.partial(sum_kernel, dp), in_specs=[hbm] * 2 + [v...  65.5 us
    pallas_call x1, Pallas kernels, body(): pl.pallas_call(functools.partial(backward_kernel, steps_per_seq), grid=(g...  38.3 us
    pallas_call x1, Pallas kernels, body(): pl.pallas_call(functools.partial(forward_kernel, steps_per_seq, width, in...  34.8 us
    pallas_call x1, Pallas kernels, finish(): pl.pallas_call(functools.partial(finish_kernel, 2 * half), grid=(grid,),...  9.35 us
    ppermute x6, starting transfers between devices, swap(): return lax.ppermute(x, axis, SWAP)  3.27 us
  transfers between devices with their start and end apart: 6, of which 0 were waited for; matrix products, arithmetic and copies ran while one was open for 6% of the time, Pallas kernels for 85%

profile of v5, /device:TPU:0, one launch (start us, length us, event | category | flops | bytes accessed | tf_op | source)
XLA Modules:
  0.0 162.3 jit_solution(11721533278211058609)
XLA Ops:
  0.7 0.6 collective-permute-start
  1.2 0.8 constant_dynamic-slice_fusion.2
  2.0 0.2 copy.34
  2.2 0.2 copy.35
  2.4 1.4 constant_dynamic-slice_fusion.3
  3.9 1.1 fusion.3
  5.0 0.8 constant_dynamic-slice_fusion
  5.7 0.5 collective-permute-start.3
  6.3 0.5 collective-permute-start.4
  6.7 0.1 pad.22.clone
  6.8 0.7 maximum_maximum_fusion.1.stap
  7.5 0.6 fusion.4.sel_ref.sel
  8.2 0.1 pad.33.clone
  8.3 0.1 broadcast_in_dim_reshape.3
  8.5 0.6 concatenate.21.vtap
  9.1 0.7 maximum_maximum_fusion.gains
  9.8 0.7 broadcast_in_dim.48.head_par
  10.5 34.8 %forward_core.1 = (bf16[2048,384]{1,0:T(8,128)(2,1)}, bf16[2048,384]{1,0:T(8,128)(2,1)}, bf16[1024,384]{1,0:T(8,128)(2,1)}, f32[16,2048]{1,0:T(8,128)}, f32[2048...) custom-call(bf16[2048,384]{1,0:T(8,128)(2,1)} %hid.1, ...), custom_call_target="tpu_custom_call" | custom-call | flops 12000000000 | bytes 40000000 | tf_op jit(solution)/shard_map/forward_core/pallas_call | solution.py:1069
  45.3 1.2 slice.3
  46.5 1.7 %collective-permute-start.5 = (bf16[1024,384]{1,0:T(8,128)(2,1)S(1)}, bf16[1024,384]{1,0:T(8,128)(2,1)S(1)}, u32[]{:S(2)}, u32[]{:S(2)}) collective-permute-start(bf16[1024,384]{1,0:T(8,128)(2,1)S(1)} %slice.3), channel_id=1, source_target_pairs={{0,1},{1,0},{2,3},{3,2},{4,5},{5,4},{6,7},{7,6},{8,9},{9,8},{10,11... | collective-permute-start | bytes 2359304 | tf_op jit(solution)/shard_map/ppermute | solution.py:972
  48.2 38.3 %backward_core.1 = (bf16[2048,1152]{1,0:T(8,128)(2,1)}, bf16[2048,384]{1,0:T(8,128)(2,1)}, bf16[2048,384]{1,0:T(8,128)(2,1)}, f32[8,2048]{1,0:T(8,128)}, f32[56,...) custom-call(bf16[2048,384]{1,0:T(8,128)(2,1)} %cot.3, ...), custom_call_target="tpu_custom_call" | custom-call | flops 24000000000 | bytes 60000000 | tf_op jit(solution)/shard_map/backward_core/pallas_call | solution.py:1146
  86.5 65.5 %sum_over_dp.1 = (bf16[2816,384]{1,0:T(8,128)(2,1)}, bf16[2048,384]{1,0:T(8,128)(2,1)}, bf16[2048,384]{1,0:T(8,128)(2,1)}, f32[8,2048]{1,0:T(8,128)}) custom-call(bf16[768,2048]{1,0:T(8,128)(2,1)} %get-tuple-element.59.normed_t_hbm, bf16[2048,1152]{1,0:T(8,128)(2,1)} %get-tuple-element.70.p_hbm, f32[384,384]{1,0:T(8,128)} %get-tuple-element.71.go_own, ...), custom_call_target="tpu_custom_call" | custom-call | flops 1000000 | bytes 150000000 | tf_op jit(solution)/shard_map/sum_over_dp/pallas_call | solution.py:765
  152.0 0.9 copy-done.1
  152.8 9.4 %finish.1 = (bf16[2048,384]{1,0:T(8,128)(2,1)}, f32[2048,384]{1,0:T(8,128)}, f32[384,768]{1,0:T(8,128)}, f32[384,768]{1,0:T(8,128)}, f32[12,384]{1,0:T(8,128)}, ...) custom-call(bf16[2816,384]{1,0:T(8,128)(2,1)} %get-tuple-element.80., ...), custom_call_target="tpu_custom_call" | custom-call | flops 20000000 | bytes 20000000 | tf_op jit(solution)/shard_map/finish/pallas_call | solution.py:916
  (46 shorter events, 0.3 us)
Async XLA Ops:
  0.6 3.1 %copy-start.3 = (bf16[384,256]{1,0:T(8,128)(2,1)S(1)}, bf16[384,256]{1,0:T(8,128)(2,1)}, u32[]{:S(2)}) copy-start(bf16[384,256]{1,0:T(8,128)(2,1)} %param.20) | copy-start | bytes 589828
  0.7 9.1 %collective-permute-start = (bf16[2048,384]{1,0:T(8,128)(2,1)}, bf16[2048,384]{1,0:T(8,128)(2,1)}, u32[]{:S(2)}, u32[]{:S(2)}) collective-permute-start(bf16[2048,384]{1,0:T(8,128)(2,1)} %hid.1), channel_id=1, source_target_pairs={{0,2},{2,0},{1,3},{3,1},{4,6},{6,4},{5,7},{7,5},{8,10},{10,8},{9,1... | collective-permute-start | bytes 4718600 | tf_op jit(solution)/shard_map/ppermute | solution.py:972
  3.7 1.2 copy-start.2
  3.7 2.5 %copy-start.7 = (f32[384]{0:T(512)S(1)}, f32[384]{0:T(512)}, u32[]{:S(2)}) copy-start(f32[384]{0:T(512)} %param.28) | copy-start | bytes 4612
  3.8 2.5 %copy-start = (bf16[2048,384]{1,0:T(8,128)(2,1)S(1)}, bf16[2048,384]{1,0:T(8,128)(2,1)}, u32[]{:S(2)}) copy-start(bf16[2048,384]{1,0:T(8,128)(2,1)} %cot.3) | copy-start | bytes 4718596
  3.8 3.1 %copy-start.5 = (f32[4,256]{1,0:T(4,128)S(1)}, f32[4,256]{1,0:T(4,128)}, u32[]{:S(2)}) copy-start(f32[4,256]{1,0:T(4,128)} %param.23) | copy-start | bytes 12292
  3.8 3.0 %copy-start.8 = (f32[256]{0:T(256)S(1)}, f32[256]{0:T(256)}, u32[]{:S(2)}) copy-start(f32[256]{0:T(256)} %param.24) | copy-start | bytes 3076
  3.8 4.3 %copy-start.12 = (f32[6]{0:T(128)S(1)}, f32[6]{0:T(128)}, u32[]{:S(2)}) copy-start(f32[6]{0:T(128)} %param.25) | copy-start | bytes 76
  3.8 4.3 %copy-start.13 = (f32[6]{0:T(128)S(1)}, f32[6]{0:T(128)}, u32[]{:S(2)}) copy-start(f32[6]{0:T(128)} %param.26) | copy-start | bytes 76
  3.8 4.5 %copy-start.10 = (f32[6]{0:T(128)S(1)}, f32[6]{0:T(128)}, u32[]{:S(2)}) copy-start(f32[6]{0:T(128)} %param.27) | copy-start | bytes 76
  3.8 4.6 %copy-start.6 = (f32[384]{0:T(512)S(1)}, f32[384]{0:T(512)}, u32[]{:S(2)}) copy-start(f32[384]{0:T(512)} %param.22) | copy-start | bytes 4612
  3.8 4.6 %copy-start.9 = (bf16[384]{0:T(512)(128)(2,1)S(1)}, bf16[384]{0:T(512)(128)(2,1)}, u32[]{:S(2)}) copy-start(bf16[384]{0:T(512)(128)(2,1)} %param.29) | copy-start | bytes 2308
  3.9 4.6 %copy-start.4 = (f32[4,384]{1,0:T(4,128)S(1)}, f32[4,384]{1,0:T(4,128)}, u32[]{:S(2)}) copy-start(f32[4,384]{1,0:T(4,128)} %param.21) | copy-start | bytes 18436
  4.9 4.8 %collective-permute-start.2 = (bf16[384,1152]{1,0:T(8,128)(2,1)S(1)}, bf16[384,1152]{1,0:T(8,128)(2,1)}, u32[]{:S(2)}, u32[]{:S(2)}) collective-permute-start(bf16[384,1152]{1,0:T(8,128)(2,1)S(1)} %get-tuple-element.108), channel_id=1, source_target_pairs={{0,2},{2,0},{1,3},{3,1},{4,6},{6,4},{5,7},{7,5},{8,10},{10,8},{9,1... | collective-permute-start | bytes 2654216 | tf_op jit(solution)/shard_map/ppermute | solution.py:972
  5.7 4.0 %collective-permute-start.3 = (bf16[384,384]{1,0:T(8,128)(2,1)S(1)}, bf16[384,384]{1,0:T(8,128)(2,1)S(1)}, u32[]{:S(2)}, u32[]{:S(2)}) collective-permute-start(bf16[384,384]{1,0:T(8,128)(2,1)S(1)} %get-tuple-element.102), channel_id=1, source_target_pairs={{0,2},{2,0},{1,3},{3,1},{4,6},{6,4},{5,7},{7,5},{8,10},{10,8},{9,1... | collective-permute-start | bytes 884744 | tf_op jit(solution)/shard_map/ppermute | solution.py:972
  6.2 2.9 %collective-permute-start.1 = (f32[384]{0:T(512)S(1)}, f32[384]{0:T(512)S(1)}, u32[]{:S(2)}, u32[]{:S(2)}) collective-permute-start(f32[384]{0:T(512)S(1)} %copy-done.7), channel_id=1, source_target_pairs={{0,2},{2,0},{1,3},{3,1},{4,6},{6,4},{5,7},{7,5},{8,10},{10,8},{9,1... | collective-permute-start | bytes 4616 | tf_op jit(solution)/shard_map/ppermute | solution.py:972
  6.3 41.9 %collective-permute-start.4 = (bf16[2048,384]{1,0:T(8,128)(2,1)S(1)}, bf16[2048,384]{1,0:T(8,128)(2,1)}, u32[]{:S(2)}, u32[]{:S(2)}) collective-permute-start(bf16[2048,384]{1,0:T(8,128)(2,1)S(1)} %copy-done), channel_id=1, source_target_pairs={{0,2},{2,0},{1,3},{3,1},{4,6},{6,4},{5,7},{7,5},{8,10},{10,8},{9,1... | collective-permute-start | bytes 4718600 | tf_op jit(solution)/shard_map/ppermute | solution.py:972
  9.8 0.7 copy-start.11
  46.5 105.5 %collective-permute-start.5 = (bf16[1024,384]{1,0:T(8,128)(2,1)S(1)}, bf16[1024,384]{1,0:T(8,128)(2,1)S(1)}, u32[]{:S(2)}, u32[]{:S(2)}) collective-permute-start(bf16[1024,384]{1,0:T(8,128)(2,1)S(1)} %slice.3), channel_id=1, source_target_pairs={{0,1},{1,0},{2,3},{3,2},{4,5},{5,4},{6,7},{7,6},{8,9},{9,8},{10,11... | collective-permute-start | bytes 2359304 | tf_op jit(solution)/shard_map/ppermute | solution.py:972
  152.0 0.9 copy-start.1

commit v6 on v1

v6 whole, which is shorter than its diff:
```python
import functools

import jax
import jax.numpy as jnp
from jax import lax
from jax.experimental import pallas as pl
from jax.experimental.pallas import tpu as pltpu
from jax.sharding import PartitionSpec as P

LEN = 2048
EPSILON = 1e-05
SUB = 128
STEP = 256
F32 = jnp.float32
BF16 = jnp.bfloat16
SWAP = [(0, 1), (1, 0)]
AR_SPLIT = 2
PROJ_EARLY = 5
DN_LATE = 2
EARLY_STEPS = [3, 5, 6, 7]


def dot(a, b):
    return jnp.dot(a, b, preferred_element_type=F32)


def dot_nt(a, b):
    return lax.dot_general(a, b, (((1,), (1,)), ((), ())), preferred_element_type=F32)


def dot_tn(a, b):
    return lax.dot_general(a, b, (((0,), (0,)), ((), ())), preferred_element_type=F32)


def sigmoid(x):
    return 0.5 * jnp.tanh(0.5 * x) + 0.5


def softplus(x):
    return jnp.maximum(x, 0.0) + jnp.log1p(jnp.exp(-jnp.abs(x)))


def fold8(x):
    return jnp.sum(x.reshape(x.shape[0] // 8, 8, x.shape[1]), axis=0)


def row_scan(x, mat):
    hi = x.astype(BF16).astype(F32)
    rest = x - hi
    mid = rest.astype(BF16).astype(F32)
    low = rest - mid
    parts = jnp.concatenate([hi, mid, low, jnp.zeros_like(x)], axis=0).astype(BF16)
    out = dot(parts, mat)
    return out[0:8] + out[8:16] + out[16:24]


def plain_sums(sel, z):
    return dot_nt(sel, z.astype(BF16))[0:8]


def head_sums(sel, z):
    hi = z.astype(BF16)
    low = (z - hi.astype(F32)).astype(BF16)
    return (dot_nt(sel, hi) + dot_nt(sel, low))[0:8]


def iota(shape, dim):
    return lax.broadcasted_iota(jnp.int32, shape, dim)


def spread(cols, first, rows):
    lane = iota((rows, 128), 1)
    return jnp.where(
        lane < 64,
        jnp.broadcast_to(cols[:, first : first + 1], (rows, 128)),
        jnp.broadcast_to(cols[:, first + 1 : first + 2], (rows, 128)),
    )


def pair_stack(x):
    lane = iota(x.shape, 1)
    zero = jnp.zeros_like(x)
    return jnp.concatenate([jnp.where(lane < 64, x, zero), jnp.where(lane < 64, zero, x)], axis=0)


def forward_block(fresh, width, weights_in, outs_a, outs_b, scratch):
    hid_own, hid_rec, gains, w_own, w_rec, vtap, stap, head_par, wo_own, wo_rec = weights_in
    mixed_out, pre_gate_out, pre_value_out, conv_value_out, pre_shared_out, conv_shared_out = outs_a
    y_out, state_out, rows_out, nt_out = outs_b
    state, vbuf, sbuf, po_own, po_send, square_row = scratch
    chan = mixed_out.shape[1]
    pairs = chan // 128

    @pl.when(fresh)
    def _():
        state[...] = jnp.zeros_like(state)
        vbuf[0:8, :] = jnp.zeros((8, vbuf.shape[1]), F32)
        sbuf[0:8, :] = jnp.zeros((8, sbuf.shape[1]), F32)

    h0 = hid_own[...].astype(F32)
    h1 = hid_rec[...].astype(F32)
    square = jnp.sum(h0 * h0, axis=1, keepdims=True) + jnp.sum(h1 * h1, axis=1, keepdims=True)
    recip = lax.rsqrt(square / width + EPSILON)
    n0 = (h0 * gains[0:1, :]).astype(BF16)
    n1 = (h1 * gains[1:2, :]).astype(BF16)
    half = n0.shape[1]
    nt_out[0:half, :] = jnp.transpose(n0)
    nt_out[half : 2 * half, :] = jnp.transpose(n1)
    q = dot(n0, w_own[...]) + dot(n1, w_rec[...])
    pre = q * recip
    gate = pre[:, 0:chan]
    pre_gate_out[...] = gate
    pre_value = pre[:, chan : 2 * chan]
    pre_value_out[...] = pre_value.astype(BF16)
    pre_shared = pre[:, 2 * chan : 2 * chan + 256]
    pre_shared_out[...] = pre_shared.astype(BF16)
    vbuf[8 : 8 + STEP, :] = pre_value
    sbuf[8 : 8 + STEP, :] = pre_shared
    conv = jnp.broadcast_to(vtap[4:5, :], (STEP, chan))
    conv_s = jnp.broadcast_to(stap[4:5, :], (STEP, 256))
    for k in range(4):
        conv = conv + vbuf[5 + k : 5 + k + STEP, :] * vtap[k : k + 1, :]
        conv_s = conv_s + sbuf[5 + k : 5 + k + STEP, :] * stap[k : k + 1, :]
    vbuf[0:8, :] = vbuf[STEP : STEP + 8, :]
    sbuf[0:8, :] = sbuf[STEP : STEP + 8, :]
    conv_value_out[...] = conv
    conv_shared_out[...] = conv_s
    x = conv * sigmoid(conv)
    act = conv_s * sigmoid(conv_s)

    head_rows = jnp.transpose(pre[:, 2 * chan + 256 : 2 * chan + 384])[0:8]
    v = head_rows + head_par[0:8, 0:1]
    steps = softplus(v)
    logd = head_par[8:16, 0:1] * steps
    rows_out[0:8, :] = v
    rows_out[16:24, :] = jnp.transpose(jnp.broadcast_to(recip, (STEP, 128)))[0:8]

    upper = (iota((SUB, SUB), 0) <= iota((SUB, SUB), 1)).astype(F32).astype(BF16)
    causal = iota((SUB, SUB), 0) >= iota((SUB, SUB), 1)
    sg = gate * sigmoid(gate)
    for sub in range(STEP // SUB):
        lo, hi = sub * SUB, (sub + 1) * SUB
        cum_r = row_scan(logd[:, lo:hi], upper)
        rows_out[8:16, lo:hi] = cum_r
        cols = jnp.transpose(jnp.concatenate([cum_r, steps[:, lo:hi]], axis=0))
        b_in = act[lo:hi, 0:128]
        b_bf = b_in.astype(BF16)
        c_bf = act[lo:hi, 128:256].astype(BF16)
        b_t = jnp.transpose(b_in).astype(BF16)
        scores = dot_nt(c_bf, b_bf)
        for p in range(pairs):
            pl0, pl1 = p * 128, (p + 1) * 128
            c0 = jnp.broadcast_to(cols[:, 2 * p : 2 * p + 1], (SUB, 128))
            c1 = jnp.broadcast_to(cols[:, 2 * p + 1 : 2 * p + 2], (SUB, 128))
            weights = []
            for col, h in ((c0, 2 * p), (c1, 2 * p + 1)):
                gap = jnp.where(causal, col - cum_r[h : h + 1, :], -1e30)
                weights.append((scores * jnp.exp(gap)).astype(BF16))
            lane = iota((SUB, 128), 1)
            cum_e = jnp.where(lane < 64, c0, c1)
            step_e = spread(cols, 8 + 2 * p, SUB)
            xs = x[lo:hi, pl0:pl1]
            xh = step_e * xs
            inside = dot(jnp.concatenate(weights, axis=1), pair_stack(xh.astype(BF16)))
            held = state[:, pl0:pl1]
            held_bf = held.astype(BF16)
            state_out[lo:hi, pl0:pl1] = held_bf
            carried = dot(c_bf, held_bf)
            y = inside + carried * jnp.exp(cum_e)
            y_out[lo:hi, pl0:pl1] = y
            last = cum_e[SUB - 1 : SUB, :]
            tail = (xh * jnp.exp(last - cum_e)).astype(BF16)
            state[:, pl0:pl1] = held * jnp.exp(last) + dot(b_t, tail)
            y = y + vtap[5:6, pl0:pl1] * xs
            mixed_out[lo:hi, pl0:pl1] = (y * sg[lo:hi, pl0:pl1]).astype(BF16)
    mix = mixed_out[...].astype(F32)
    weighted = (mix * vtap[6:7, :]).astype(BF16)
    po_own[...] = dot(weighted, wo_own[...]).astype(BF16)
    po_send[...] = dot(weighted, wo_rec[...]).astype(BF16)
    square_row[...] = plain_sums(jnp.ones((16, chan), BF16), mix * mix)[0:1]


def early_levels(dp):
    return dp.bit_length()


def early_steps(dp, blocks):
    count = early_levels(dp)
    if count == 4 and blocks == 8:
        return EARLY_STEPS
    return [max(2, blocks - count + n) if blocks > count else blocks - 1 for n in range(count)]


def early_orders(dp):
    bits = dp.bit_length() - 1
    near = tuple(range(bits))
    far = tuple(range(1, bits)) + (0,)
    return [far if n % 2 else near for n in range(2 * AR_SPLIT)]


def partner_of(me, k):
    return {"dp": me + (1 - 2 * lax.rem(me // (1 << k), 2)) * (1 << k)}


def levels(dp, me, bounds, orders, acc, stage, land, out, send_sem, recv_sem):
    bits = dp.bit_length() - 1

    def span(start, rows):
        return pl.ds(pl.multiple_of(start, 16), rows)

    def bit_of(k):
        return lax.rem(me // (1 << k), 2)

    def low_at(i, count):
        low, rows = bounds[i]
        for n in range(count):
            low = low + bit_of(orders[i][n]) * (rows >> (n + 1))
        return low

    def places(i, level):
        base, rows = bounds[i]
        if level < bits:
            k = orders[i][level]
            part = rows >> (level + 1)
            give = span(low_at(i, level) + (1 - bit_of(k)) * part, part)
            where = span(base + rows - (rows >> level), part)
            return k, give, where, span(low_at(i, level + 1), part)
        back = 2 * bits - 1 - level
        own = span(low_at(i, back + 1), rows >> (back + 1))
        return orders[i][back], own, own, None

    def copy_of(i, level):
        k, give, where, _ = places(i, level)
        src, dst = (stage, land) if level < bits else (out, out)
        return remote(
            src.at[give, :], dst.at[where, :], send_sem.at[i, level], recv_sem.at[i, level], partner_of(me, k)
        )

    def start_level(i, level):
        if level < bits:
            give = places(i, level)[1]
            stage[give, :] = acc[give, :].astype(BF16)
        copy_of(i, level).start()

    def end_level(i, level, go_on=True):
        copy_of(i, level).wait()
        if level < bits:
            _, _, where, keep = places(i, level)
            total = acc[keep, :] + land[where, :].astype(F32)
            acc[keep, :] = total
            if level == bits - 1:
                out[keep, :] = total.astype(BF16)
        if go_on and level + 1 < 2 * bits:
            start_level(i, level + 1)

    return start_level, end_level


def gate_block(ins, outs):
    cot_own, cot_rec, wo_own, wo_rec, trow, rows_in, mixed, pre_gate, conv_value, y_in, vtap = ins
    acc_v, go_own, go_rec, dy_out, p_gate, rs_gate = outs
    chan = mixed.shape[1]
    tcol = jnp.transpose(jnp.concatenate([trow[...], rows_in[16:24, :]], axis=0))
    scale = tcol[:, 0:1]
    coef = tcol[:, 8:9]
    recip = tcol[:, 16:17]
    s0 = (cot_own[...].astype(F32) * scale).astype(BF16)
    s1 = (cot_rec[...].astype(F32) * scale).astype(BF16)
    d_weighted = dot_nt(s0, wo_own[...]) + dot_nt(s1, wo_rec[...])
    mix = mixed[...].astype(F32)
    acc_v[48:56, :] += fold8(d_weighted * mix)
    weighted_t = jnp.transpose((mix * vtap[6:7, :]).astype(BF16))
    go_own[...] += dot(weighted_t, s0)
    go_rec[...] += dot(weighted_t, s1)
    d_mixed = d_weighted * vtap[6:7, :] - coef * mix
    gate = pre_gate[...]
    sig = sigmoid(gate)
    silu = gate * sig
    conv = conv_value[...]
    sig_v = sigmoid(conv)
    x = conv * sig_v
    y_scan = y_in[...]
    y = y_scan + vtap[5:6, :] * x
    dy = d_mixed * silu
    d_gate = d_mixed * y * (sig + silu * (1.0 - sig))
    acc_v[40:48, :] += fold8(dy * x)
    dy_out[...] = dy.astype(BF16)
    p_gate[...] = (recip * d_gate).astype(BF16)
    rs_gate[...] = plain_sums(jnp.ones((16, chan), BF16), d_gate * gate)


def scan_block(fresh, ins, weights_in, outs, scratch):
    rows_in, pre_value, conv_value, pre_shared, conv_shared, y_in, state_in, hid_own, hid_rec = ins
    w_own, w_rec, vtap, stap, head_par, sel_ref, dy_in, p_gate, rs_gate = weights_in
    p_out, rsum_out, acc_v, acc_s, acc_h, acc_n, dn_own, dn_rec = outs
    grad, vbuf, sbuf, dxbuf, dbbuf = scratch
    chan = conv_value.shape[1]
    pairs = chan // 128

    @pl.when(fresh)
    def _():
        grad[...] = jnp.zeros_like(grad)
        vbuf[STEP : STEP + 8, :] = jnp.zeros((8, vbuf.shape[1]), F32)
        sbuf[STEP : STEP + 8, :] = jnp.zeros((8, sbuf.shape[1]), F32)

    recip = jnp.transpose(rows_in[16:24, :])[:, 0:1]
    conv = conv_value[...]
    sig_v = sigmoid(conv)
    x = conv * sig_v
    dy_bf = dy_in[...]
    conv_s = conv_shared[...]
    sig_s = sigmoid(conv_s)
    act = conv_s * sig_s

    sel = sel_ref[...]
    sel_f = sel.astype(F32)[0:8]
    v = rows_in[0:8, :]
    steps = softplus(v)
    logd = head_par[8:16, 0:1] * steps
    lower = (iota((SUB, SUB), 0) >= iota((SUB, SUB), 1)).astype(F32).astype(BF16)
    strict = (iota((SUB, SUB), 0) < iota((SUB, SUB), 1)).astype(F32).astype(BF16)
    causal_t = iota((SUB, SUB), 0) <= iota((SUB, SUB), 1)
    for sub in reversed(range(STEP // SUB)):
        lo, hi = sub * SUB, (sub + 1) * SUB
        cum_r = rows_in[8:16, lo:hi]
        cols = jnp.transpose(jnp.concatenate([cum_r, steps[:, lo:hi]], axis=0))
        b_bf = act[lo:hi, 0:128].astype(BF16)
        c_in = act[lo:hi, 128:256]
        c_bf = c_in.astype(BF16)
        c_t = jnp.transpose(c_in).astype(BF16)
        scores_t = dot_nt(b_bf, c_bf)
        d_scores = jnp.zeros((SUB, SUB), F32)
        db = jnp.zeros((SUB, 128), F32)
        dc = jnp.zeros((SUB, 128), F32)
        z_sum = jnp.zeros((8, SUB), F32)
        e_sum = jnp.zeros((8, SUB), F32)
        f_sum = jnp.zeros((8, SUB), F32)
        gh = jnp.zeros((8, 1), F32)
        for p in range(pairs):
            pl0, pl1 = p * 128, (p + 1) * 128
            c0 = jnp.broadcast_to(cols[:, 2 * p : 2 * p + 1], (SUB, 128))
            c1 = jnp.broadcast_to(cols[:, 2 * p + 1 : 2 * p + 2], (SUB, 128))
            decays = []
            for col, h in ((c0, 2 * p), (c1, 2 * p + 1)):
                gap = jnp.where(causal_t, cum_r[h : h + 1, :] - col, -1e30)
                decays.append(jnp.exp(gap))
            weights = [(scores_t * d).astype(BF16) for d in decays]
            lane = iota((SUB, 128), 1)
            cum_e = jnp.where(lane < 64, c0, c1)
            step_e = spread(cols, 8 + 2 * p, SUB)
            xs = x[lo:hi, pl0:pl1]
            xh = step_e * xs
            xh_bf = xh.astype(BF16)
            dys_bf = dy_bf[lo:hi, pl0:pl1]
            dys = dys_bf.astype(F32)
            stack = pair_stack(dys_bf)
            inner = dot(jnp.concatenate(weights, axis=1), stack)
            d_pair = dot_nt(xh_bf, stack)
            d_scores = d_scores + decays[0] * d_pair[:, 0:128] + decays[1] * d_pair[:, 128:256]
            last = cum_e[SUB - 1 : SUB, :]
            tail_e = jnp.exp(last - cum_e)
            g = grad[:, pl0:pl1]
            g_bf = g.astype(BF16)
            outer = dot(b_bf, g_bf) * tail_e
            u = inner + outer
            dxbuf[lo:hi, pl0:pl1] = step_e * u + vtap[5:6, pl0:pl1] * dys
            db = db + dot_nt((xh * tail_e).astype(BF16), g_bf)
            dya = (dys * jnp.exp(cum_e)).astype(BF16)
            held = state_in[lo:hi, pl0:pl1]
            dc = dc + dot_nt(dya, held)
            sel_p = sel[:, pl0:pl1]
            z_sum = z_sum + head_sums(
                sel_p, dys * y_in[lo:hi, pl0:pl1] - xh_bf.astype(F32) * inner
            )
            e_sum = e_sum + plain_sums(sel_p, xh * outer)
            f_sum = f_sum + plain_sums(sel_p, xs * u)
            decay_row = jnp.exp(last)
            gh_row = decay_row * jnp.sum(g * held.astype(F32), axis=0, keepdims=True)
            gh = gh + jnp.sum(sel_f[:, pl0:pl1] * gh_row, axis=1, keepdims=True)
            grad[:, pl0:pl1] = g * decay_row + dot(c_t, dya)
        ds_bf = d_scores.astype(BF16)
        dbbuf[lo:hi, 0:128] = db + dot(ds_bf, c_bf)
        dbbuf[lo:hi, 128:256] = dc + dot(jnp.transpose(d_scores).astype(BF16), b_bf)
        d_log = row_scan(z_sum, lower) + row_scan(e_sum, strict) + gh
        d_step = (f_sum + d_log * head_par[8:16, 0:1]) * sigmoid(v[:, lo:hi])
        acc_h[0:8, :] += d_log * logd[:, lo:hi]
        acc_h[8:16, :] += d_step
        pre_step = v[:, lo:hi] - head_par[0:8, 0:1]
        rsum_out[:, lo:hi] += jnp.broadcast_to(
            jnp.sum(d_step * pre_step, axis=0, keepdims=True), (8, SUB)
        )
        d_cols = jnp.transpose(jnp.concatenate([d_step, jnp.zeros((120, SUB), F32)], axis=0))
        p_out[lo:hi, chan + 256 : chan + 384] = (recip[lo:hi] * d_cols).astype(BF16)

    d_conv = dxbuf[...] * (sig_v + x * (1.0 - sig_v))
    d_conv_s = dbbuf[...] * (sig_s + act * (1.0 - sig_s))
    vbuf[0:STEP, :] = d_conv
    sbuf[0:STEP, :] = d_conv_s
    acc_v[32:40, :] += fold8(d_conv)
    acc_s[32:40, :] += fold8(d_conv_s)
    pv = pre_value[...].astype(F32)
    ps = pre_shared[...].astype(F32)
    d_value = jnp.zeros((STEP, chan), F32)
    d_shared = jnp.zeros((STEP, 256), F32)
    for k in range(4):
        moved = vbuf[3 - k : 3 - k + STEP, :]
        d_value = d_value + vtap[k : k + 1, :] * moved
        acc_v[8 * k : 8 * k + 8, :] += fold8(pv * moved)
        moved = sbuf[3 - k : 3 - k + STEP, :]
        d_shared = d_shared + stap[k : k + 1, :] * moved
        acc_s[8 * k : 8 * k + 8, :] += fold8(ps * moved)
    vbuf[STEP : STEP + 8, :] = vbuf[0:8, :]
    sbuf[STEP : STEP + 8, :] = sbuf[0:8, :]
    p_out[:, 0:chan] = (recip * d_value).astype(BF16)
    p_out[:, chan : chan + 256] = (recip * d_shared).astype(BF16)
    ones = jnp.ones((16, chan), BF16)
    rsum_out[...] += plain_sums(ones, d_value * pv)
    rsum_out[...] += plain_sums(ones[:, 0:256], d_shared * ps)
    pg = p_gate[...]
    pb = p_out[...]
    for n, (hid, weight, dn) in enumerate(((hid_own, w_own, dn_own), (hid_rec, w_rec, dn_rec))):
        part = dot_nt(pg, weight[:, 0:chan]) + dot_nt(pb, weight[:, chan:])
        dn[...] = part.astype(BF16)
        acc_n[8 * n : 8 * n + 8, :] += fold8(part * hid[...].astype(F32))


def unit_rows(dp):
    return 16 * dp


def misc_rows(dp, rows):
    unit = max(unit_rows(dp), 256)
    return pl.cdiv(rows, unit) * unit


def big_rows(dp, rows):
    return pl.cdiv(rows, unit_rows(dp)) * unit_rows(dp)


def remote(src, dst, send, recv, target):
    return pltpu.make_async_remote_copy(
        src_ref=src,
        dst_ref=dst,
        send_sem=send,
        recv_sem=recv,
        device_id=target,
        device_id_type=pl.DeviceIdType.MESH,
    )


def greet(targets):
    barrier = pltpu.get_barrier_semaphore()
    for target in targets:
        pl.semaphore_signal(barrier, inc=1, device_id=target, device_id_type=pl.DeviceIdType.MESH)
    pl.semaphore_wait(barrier, len(targets))


def layer_kernel(
    seq_len,
    dp,
    inner_width,
    hid_own_hbm,
    hid_rec_hbm,
    cot_own_hbm,
    cot_rec_hbm,
    gains,
    w_own,
    w_rec,
    vtap,
    stap,
    head_par,
    wo_own,
    wo_rec,
    sel,
    sums_out,
    proj_out,
    proj_col,
    dn_out,
    dn_col,
    trow,
    rs_out,
    recip_out,
    hid_own,
    hid_rec,
    cot_own,
    cot_rec,
    pre_gate,
    pre_value,
    conv_value,
    pre_shared,
    conv_shared,
    y_scan,
    states,
    mixed,
    rows,
    normed_t,
    p_gate,
    p_all,
    dy_s,
    rs_in,
    state,
    vbuf,
    sbuf,
    dxbuf,
    dbbuf,
    pair_own,
    pair_send,
    pair_land,
    proj_s,
    dn_sum,
    sums,
    sums_land,
    go_own,
    go_rec,
    swap_send,
    swap_land,
    row_send,
    row_land,
    col_send,
    col_land,
    rs_land,
    acc_v,
    acc_s,
    acc_h,
    acc_n,
    acc,
    stage,
    land,
    out,
    load_sem,
    save_sem,
    po_sem,
    dn_sem,
    col_sem,
    sum_sem,
    swap_sem,
    ar_send_sem,
    ar_recv_sem,
    out_sem,
):
    tokens, half = hid_own.shape
    chan = mixed.shape[1]
    width = 2 * half
    wide = p_all.shape[1]
    blocks = tokens // STEP
    steps_per_seq = seq_len // STEP
    size = big_rows(dp, width)
    tail = out.shape[0] - 3 * size
    bits = dp.bit_length() - 1
    me = lax.axis_index("dp")
    r = lax.axis_index("row")
    c = lax.axis_index("col")
    to_row, to_col, to_both = {"row": 1 - r}, {"col": 1 - c}, {"row": 1 - r, "col": 1 - c}
    part_rows = size // AR_SPLIT
    near = tuple(range(bits))
    far = tuple(range(1, bits)) + (0,)
    bounds = [(tail + n * part_rows, part_rows) for n in range(3 * AR_SPLIT)] + [(0, tail)]
    orders = [far if n % 2 else near for n in range(3 * AR_SPLIT)] + [near]
    firsts, values, misc = range(2 * AR_SPLIT), range(2 * AR_SPLIT, 3 * AR_SPLIT), 3 * AR_SPLIT
    start_level, end_level = levels(dp, me, bounds, orders, acc, stage, land, out, ar_send_sem, ar_recv_sem)

    def span(i):
        return pl.ds(pl.multiple_of(i * STEP, STEP), STEP)

    def load(n, i):
        src, dst = ((hid_own_hbm, hid_own), (hid_rec_hbm, hid_rec), (cot_own_hbm, cot_own), (cot_rec_hbm, cot_rec))[n]
        return pltpu.make_async_copy(src.at[span(i), :], dst.at[span(i), :], load_sem.at[n, i])

    def save(n, i):
        src, dst = ((proj_s, proj_out), (dn_sum, dn_out))[n]
        return pltpu.make_async_copy(src.at[span(i), :], dst.at[span(i), :], save_sem.at[n, i])

    def pair_copy(sem, i):
        return remote(pair_send.at[span(i), :], pair_land.at[span(i), :], sem.at[0, i], sem.at[1, i], to_row)

    def col_copy(n, i):
        src, dst = ((proj_s, proj_col), (dn_sum, dn_col))[n]
        return remote(src.at[span(i), :], dst.at[span(i), :], col_sem.at[n, 0, i], col_sem.at[n, 1, i], to_col)

    def small_copy(src, dst, n, target):
        return remote(src, dst, swap_sem.at[0, n], swap_sem.at[1, n], target)

    for n in range(4):
        for i in range(blocks):
            load(n, i).start()
    greet([partner_of(me, k) for k in range(bits)] + [to_row, to_col, to_both])
    for ref in (acc_v, acc_s, acc_h, acc_n, go_own, go_rec):
        ref[...] = jnp.zeros_like(ref)

    def take_proj(i):
        pair_copy(po_sem, i).wait()
        part = pair_own[span(i), :].astype(F32) + pair_land[span(i), :].astype(F32)
        proj_s[span(i), :] = part.astype(BF16)
        save(0, i).start()

        @pl.when(i < PROJ_EARLY)
        def _():
            col_copy(0, i).start()

        load(2, i).wait()
        dots = plain_sums(jnp.ones((16, half), BF16), part * cot_own[span(i), :].astype(F32))
        sums[pl.ds(8 + i, 1), :] = dots[0:1]

    @pl.loop(0, blocks)
    def _(i):
        here = span(i)
        load(0, i).wait()
        load(1, i).wait()
        forward_block(
            i % steps_per_seq == 0,
            width,
            (
                hid_own.at[here, :],
                hid_rec.at[here, :],
                gains,
                w_own,
                w_rec,
                vtap,
                stap,
                head_par,
                wo_own,
                wo_rec,
            ),
            (
                mixed.at[here, :],
                pre_gate.at[here, :],
                pre_value.at[here, :],
                conv_value.at[here, :],
                pre_shared.at[here, :],
                conv_shared.at[here, :],
            ),
            (y_scan.at[here, :], states.at[here, :], rows.at[:, here], normed_t.at[:, here]),
            (state, vbuf, sbuf, pair_own.at[here, :], pair_send.at[here, :], sums.at[pl.ds(i, 1), :]),
        )

        @pl.when(i > 0)
        def _():
            take_proj(i - 1)

        pair_copy(po_sem, i).start()

    take_proj(blocks - 1)
    ends = []
    for n, target in enumerate((to_row, to_col, to_both)):
        copy = remote(sums, sums_land.at[n], sum_sem.at[0, n], sum_sem.at[1, n], target)
        copy.start()
        ends.append(copy)
    for i in range(PROJ_EARLY, blocks):
        col_copy(0, i).start()
    recip_out[...] = rows[16:24, :]
    for i in range(blocks):
        load(3, i).wait()
    for copy in ends:
        copy.wait()
    total = (sums[...] + sums_land[0]) + (sums_land[1] + sums_land[2])
    scale = lax.rsqrt(total[0:8] / inner_width + EPSILON)
    coef = total[8:16] * (scale * scale * scale) / inner_width
    for i in range(blocks):
        trow[0:8, i * STEP : (i + 1) * STEP] = jnp.broadcast_to(scale[i : i + 1], (8, STEP))
        trow[8:16, i * STEP : (i + 1) * STEP] = jnp.broadcast_to(coef[i : i + 1], (8, STEP))

    @pl.loop(0, blocks)
    def _(i):
        here = span(i)
        gate_block(
            (
                cot_own.at[here, :],
                cot_rec.at[here, :],
                wo_own,
                wo_rec,
                trow.at[:, here],
                rows.at[:, here],
                mixed.at[here, :],
                pre_gate.at[here, :],
                conv_value.at[here, :],
                y_scan.at[here, :],
                vtap,
            ),
            (acc_v, go_own, go_rec, dy_s.at[here, :], p_gate.at[here, :], rs_in.at[:, here]),
        )

    def chunk_rows(n, side):
        return pl.ds(pl.multiple_of(tail + n * size + side * half, 128), half)

    swaps = [small_copy(swap_send.at[n], swap_land.at[n], n, to_row) for n in range(2)]
    swap_send[0] = go_rec[...].astype(BF16)
    swaps[0].start()
    swap_send[1] = dot(normed_t[half:width, :], p_gate[...]).astype(BF16)
    swaps[1].start()
    acc[chunk_rows(0, r), :] = go_own[...]
    acc[chunk_rows(1, r), :] = dot(normed_t[0:half, :], p_gate[...])
    if size > width:
        for n in range(3):
            acc[tail + n * size + width : tail + (n + 1) * size, :] = jnp.zeros((size - width, chan), F32)
    for n in range(2):
        swaps[n].wait()
        acc[chunk_rows(n, 1 - r), :] = swap_land[n].astype(F32)
        for i in range(AR_SPLIT):
            start_level(n * AR_SPLIT + i, 0)

    def take_dn(i):
        pair_copy(dn_sem, i).wait()
        part = pair_own[span(i), :].astype(F32) + pair_land[span(i), :].astype(F32)
        dn_sum[span(i), :] = part.astype(BF16)
        save(1, i).start()

    @pl.loop(0, blocks)
    def _(later):
        i = blocks - 1 - later
        here = span(i)
        scan_block(
            later % steps_per_seq == 0,
            (
                rows.at[:, here],
                pre_value.at[here, :],
                conv_value.at[here, :],
                pre_shared.at[here, :],
                conv_shared.at[here, :],
                y_scan.at[here, :],
                states.at[here, :],
                hid_own.at[here, :],
                hid_rec.at[here, :],
            ),
            (
                w_own,
                w_rec,
                vtap,
                stap,
                head_par,
                sel,
                dy_s.at[here, :],
                p_gate.at[here, :],
                rs_in.at[:, here],
            ),
            (
                p_all.at[here, :],
                rs_in.at[:, here],
                acc_v,
                acc_s,
                acc_h,
                acc_n,
                pair_own.at[here, :],
                pair_send.at[here, :],
            ),
            (state, vbuf, sbuf, dxbuf, dbbuf),
        )

        @pl.when(later > 0)
        def _():
            take_dn(i + 1)

            @pl.when(i + 1 >= DN_LATE)
            def _():
                col_copy(1, i + 1).start()

        pair_copy(dn_sem, i).start()
        for level, when in enumerate(early_steps(dp, blocks)):

            @pl.when(later == when)
            def _(level=level):
                for n in firsts:
                    end_level(n, level)

    def sum8(ref, n):
        return jnp.sum(ref[8 * n : 8 * n + 8, :], axis=0, keepdims=True)

    small = jnp.concatenate([sum8(acc_s, n) for n in range(5)] + [jnp.zeros((3, 256), F32)], axis=0)
    norm_own, norm_rec = [
        jnp.concatenate([sum8(acc_n, n), jnp.zeros((1, 512 - half), F32)], axis=1) for n in (0, 1)
    ]
    pad6 = jnp.zeros((6, 256), F32)
    row_send[half : half + 16, 0:256] = jnp.concatenate(
        [small, norm_rec[:, 0:256], norm_rec[:, 256:512], pad6], axis=0
    ).astype(BF16)
    row_send[half : half + 16, 256:wide] = jnp.zeros((16, wide - 256), BF16)
    for lo in range(0, wide, 384):
        row_send[0:half, lo : lo + 384] = dot(normed_t[half:width, :], p_all[:, lo : lo + 384]).astype(BF16)
    row_copy = small_copy(row_send, row_land, 2, to_row)
    row_copy.start()
    rs_row = small_copy(rs_in, rs_land.at[0], 3, to_row)
    rs_row.start()
    acc[0:half, :] = dot(normed_t[0:half, :], p_all[:, chan:wide])
    acc[chunk_rows(2, r), :] = dot(normed_t[0:half, :], p_all[:, 0:chan])
    row_copy.wait()
    acc[chunk_rows(2, 1 - r), :] = row_land[0:half, 0:chan].astype(F32)
    for n in values:
        start_level(n, 0)
    gate_sums = acc[0:half, 0:256] + row_land[0:half, chan : chan + 256].astype(F32)
    extra = jnp.concatenate([small, norm_own[:, 0:256], norm_own[:, 256:512], pad6], axis=0)
    extra = extra + row_land[half : half + 16, 0:256].astype(F32)
    col_send[0:half, :] = gate_sums.astype(BF16)
    col_send[half : half + 16, :] = extra.astype(BF16)
    mid_copy = small_copy(col_send, col_land, 4, to_col)
    mid_copy.start()
    rs_row.wait()
    rs_out[...] = rs_in[...] + rs_land[0]
    rs_col = small_copy(rs_out, rs_land.at[1], 5, to_col)
    rs_col.start()
    take_dn(0)
    for i in reversed(range(DN_LATE)):
        col_copy(1, i).start()

    acc[0:half, 256:384] = jnp.concatenate(
        [acc[0:half, 256:320], row_land[0:half, chan + 256 : chan + 320].astype(F32)], axis=1
    )
    acc[half : half + 16, 256:384] = jnp.zeros((16, 128), F32)
    first = half + 16
    acc[first : first + 8, :] = jnp.concatenate(
        [sum8(acc_v, n) for n in range(7)] + [jnp.zeros((1, chan), F32)], axis=0
    )
    acc[first + 8 : first + 24, :] = jnp.broadcast_to(
        jnp.sum(acc_h[...], axis=1, keepdims=True), (16, chan)
    )
    if tail > first + 24:
        acc[first + 24 : tail, :] = jnp.zeros((tail - first - 24, chan), F32)
    mid_copy.wait()
    acc[0 : half + 16, 0:256] = col_send[...].astype(F32) + col_land[...].astype(F32)
    start_level(misc, 0)
    early = early_levels(dp)
    done = []

    def save_chunk(n):
        rows_n = pl.ds(*bounds[n])
        copy = pltpu.make_async_copy(out.at[rows_n, :], sums_out.at[rows_n, :], out_sem.at[n])
        copy.start()
        done.append(copy)

    def end(n, level):
        end_level(n, level)
        if level == 2 * bits - 1:
            save_chunk(n)

    if early >= 2 * bits:
        for n in firsts:
            save_chunk(n)

    for level in range(2 * bits):
        if early + level < 2 * bits:
            for n in firsts:
                end(n, early + level)
        for n in values:
            end(n, level)
        end(misc, level)
    for copy in done:
        copy.wait()
    rs_col.wait()
    rs_out[...] = rs_out[...] + rs_land[1]
    for i in range(blocks):
        for n in range(2):
            save(n, i).wait()
            col_copy(n, i).wait()


def layer(seq_len, dp, hidden, hid_rec, cot, cot_rec, gains, w_own, w_rec, vtap, stap, head_par, wo_own, wo_rec, sel):
    tokens, half = hidden.shape
    chan = vtap.shape[1]
    wide = w_own.shape[1] - chan
    bits = dp.bit_length() - 1
    size = big_rows(dp, 2 * half)
    tail = misc_rows(dp, half + 48)
    total = tail + 3 * size
    blocks = tokens // STEP
    vmem = pl.BlockSpec(memory_space=pltpu.VMEM)
    hbm = pl.BlockSpec(memory_space=pl.ANY)

    def act(cols=half, dtype=BF16):
        return jax.ShapeDtypeStruct((tokens, cols), dtype)

    def room(*shape, dtype=BF16):
        return pltpu.VMEM(shape, dtype)

    def flags(*shape):
        return pltpu.SemaphoreType.DMA(shape)

    return pl.pallas_call(
        functools.partial(layer_kernel, seq_len, dp, 4 * chan),
        in_specs=[hbm] * 4 + [vmem] * 9,
        out_specs=[hbm, hbm, hbm, hbm, hbm, vmem, vmem, vmem],
        out_shape=[
            jax.ShapeDtypeStruct((total, chan), BF16),
            act(),
            act(),
            act(),
            act(),
            jax.ShapeDtypeStruct((16, tokens), F32),
            jax.ShapeDtypeStruct((8, tokens), F32),
            jax.ShapeDtypeStruct((8, tokens), F32),
        ],
        scratch_shapes=[
            room(tokens, half),
            room(tokens, half),
            room(tokens, half),
            room(tokens, half),
            room(tokens, chan, dtype=F32),
            room(tokens, chan),
            room(tokens, chan, dtype=F32),
            room(tokens, 256),
            room(tokens, 256, dtype=F32),
            room(tokens, chan, dtype=F32),
            room(tokens, chan),
            room(tokens, chan),
            room(24, tokens, dtype=F32),
            room(2 * half, tokens),
            room(tokens, chan),
            room(tokens, wide),
            room(tokens, chan),
            room(8, tokens, dtype=F32),
            room(128, chan, dtype=F32),
            room(STEP + 8, chan, dtype=F32),
            room(STEP + 8, 256, dtype=F32),
            room(STEP, chan, dtype=F32),
            room(STEP, 256, dtype=F32),
            room(tokens, half),
            room(tokens, half),
            room(tokens, half),
            room(tokens, half),
            room(tokens, half),
            room(16, STEP, dtype=F32),
            room(3, 16, STEP, dtype=F32),
            room(chan, half, dtype=F32),
            room(chan, half, dtype=F32),
            room(2, half, chan),
            room(2, half, chan),
            room(half + 16, wide),
            room(half + 16, wide),
            room(half + 16, 256),
            room(half + 16, 256),
            room(2, 8, tokens, dtype=F32),
            room(56, chan, dtype=F32),
            room(40, 256, dtype=F32),
            room(16, 128, dtype=F32),
            room(16, half, dtype=F32),
            room(total, chan, dtype=F32),
            room(total, chan),
            room(total, chan),
            room(total, chan),
            flags(4, blocks),
            flags(2, blocks),
            flags(2, blocks),
            flags(2, blocks),
            flags(2, 2, blocks),
            flags(2, 3),
            flags(2, 6),
            flags(3 * AR_SPLIT + 1, 2 * bits),
            flags(3 * AR_SPLIT + 1, 2 * bits),
            flags(3 * AR_SPLIT + 1),
        ],
        compiler_params=pltpu.CompilerParams(
            collective_id=0, has_side_effects=True, vmem_limit_bytes=67_000_000
        ),
        name="layer",
    )(hidden, hid_rec, cot, cot_rec, gains, w_own, w_rec, vtap, stap, head_par, wo_own, wo_rec, sel)


def finish_kernel(
    width,
    out_rows,
    gate_a,
    gate_b,
    value_a,
    value_b,
    misc,
    hid,
    cot,
    dn_sum,
    dn_col,
    proj_own,
    proj_col,
    sel,
    trow,
    recip_in,
    rs,
    gains,
    result,
    hidden_grad,
    g_gate,
    g_value,
    g_step,
    g_state,
    g_filter,
    g_shift,
    g_kernel,
    g_offset,
    g_decay,
    g_bias,
    g_skip,
    g_norm,
    g_gated,
    g_output,
):
    half = hid.shape[1]
    hid32 = hid[...].astype(F32)
    recip = recip_in[...]
    cols = jnp.transpose(jnp.concatenate([trow[0:8, :], rs[...] * recip * recip / width], axis=0))
    proj = proj_own[...].astype(F32) + proj_col[...].astype(F32)
    result[...] = (hid32 + cols[:, 0:1] * proj).astype(BF16)
    d_normed = dn_sum[...].astype(F32) + dn_col[...].astype(F32)
    hidden_grad[...] = cot[...].astype(F32) + d_normed * gains[0:1, :] - cols[:, 8:9] * hid32
    @pl.when(pl.program_id(0) < half // 128)
    def _():
        g_output[...] = out_rows[...].astype(F32)
        g_gate[:, 0:half] = gate_a[...].astype(F32)
        g_gate[:, half : 2 * half] = gate_b[...].astype(F32)
        g_value[:, 0:half] = value_a[...].astype(F32)
        g_value[:, half : 2 * half] = value_b[...].astype(F32)

    @pl.when(pl.program_id(0) == 0)
    def _():
        g_state[...] = misc[0:half, 0:256].astype(F32)
        step_t = jnp.transpose(misc[0:half, 256:384].astype(F32))
        heads = g_step.shape[0] // 2
        own, rec = step_t[0:heads], step_t[64 : 64 + heads]
        first = lax.axis_index("row") == 0
        g_step[...] = jnp.concatenate([jnp.where(first, own, rec), jnp.where(first, rec, own)], axis=0)
        small = misc[half : half + 48, :].astype(F32)
        g_kernel[...] = small[0:4, 0:256]
        g_offset[...] = small[4, 0:256]
        g_norm[0:256] = small[8, 0:256]
        g_norm[256:half] = small[9, 0 : half - 256]
        g_filter[...] = small[16:20]
        g_shift[...] = small[20]
        g_gated[...] = small[22]
        head = jnp.transpose(small[24:40, 0:128])[0:8]
        g_decay[...] = head[0, 0:heads]
        g_bias[...] = head[0, 8 : 8 + heads]
        skip = dot_nt(small[16:32].astype(BF16), sel[...])
        g_skip[...] = skip[5, 0:heads]


def finish(size, heads, out, hid, cot, dn_sum, dn_col, proj_own, proj_col, sel, trow, recip, rs, gains):
    tokens, half = hid.shape
    chan = out.shape[1]
    size_f = tokens // 4
    grid = 4

    def blk(cols):
        return pl.BlockSpec((size_f, cols), lambda i: (i, 0))

    def row(count):
        return pl.BlockSpec((count, size_f), lambda i: (0, i))

    def whole(shape):
        return pl.BlockSpec(shape, lambda i: (0,) * len(shape))

    parts = half // 128
    tail = out.shape[0] - 3 * size

    def part(start):
        return pl.BlockSpec((128, chan), lambda i: (start // 128 + jnp.minimum(i, parts - 1), 0))

    def streamed(rows, cols):
        return pl.BlockSpec((rows // parts, cols), lambda i: (jnp.minimum(i, parts - 1), 0))

    small = [
        (2 * heads, half),
        (half, 256),
        (4, chan),
        (chan,),
        (4, 256),
        (256,),
        (heads,),
        (heads,),
        (heads,),
        (half,),
        (chan,),
    ]
    big = (half, 2 * chan)
    shapes = [big, big] + small + [(2 * chan, half)]
    return pl.pallas_call(
        functools.partial(finish_kernel, 2 * half),
        grid=(grid,),
        in_specs=[
            pl.BlockSpec((256, half), lambda i: (tail // 256 + jnp.minimum(i, parts - 1), 0)),
            part(tail + size),
            part(tail + size + half),
            part(tail + 2 * size),
            part(tail + 2 * size + half),
            whole((tail, chan)),
            blk(half),
            blk(half),
            blk(half),
            blk(half),
            blk(half),
            blk(half),
            whole(sel.shape),
            row(16),
            row(8),
            row(8),
            whole((8, half)),
        ],
        out_specs=[blk(half), blk(half), streamed(*big), streamed(*big)]
        + [whole(shape) for shape in small]
        + [streamed(2 * chan, half)],
        out_shape=[
            jax.ShapeDtypeStruct((tokens, half), BF16),
            jax.ShapeDtypeStruct((tokens, half), F32),
        ]
        + [jax.ShapeDtypeStruct(shape, F32) for shape in shapes],
        cost_estimate=pl.CostEstimate(flops=20_000_000, bytes_accessed=20_000_000, transcendentals=0),
        name="finish",
    )(
        out,
        out,
        out,
        out,
        out,
        out,
        hid,
        cot,
        dn_sum,
        dn_col,
        proj_own,
        proj_col,
        sel,
        trow,
        recip,
        rs,
        gains,
    )


def swap(x, axis):
    return lax.ppermute(x, axis, SWAP)


def body(
    hidden,
    gate_proj,
    value_proj,
    step_proj,
    state_proj,
    value_filter,
    value_shift,
    shared_kernel,
    shared_offset,
    decay_log,
    step_bias,
    skip_gain,
    input_gain,
    gated_gain,
    output_proj,
    cotangent,
):
    tokens, half = hidden.shape
    width = 2 * half
    chan = gated_gain.shape[0]
    inner_width = 4 * chan
    heads = decay_log.shape[0]
    r = lax.axis_index("row")
    dp = lax.axis_size("dp")
    seq_len = min(LEN, tokens)

    def cut(x, start, size, axis):
        return lax.dynamic_slice_in_dim(x, start * size, size, axis)

    def packed(side):
        return jnp.concatenate(
            [
                cut(gate_proj, side, chan, 1),
                cut(value_proj, side, chan, 1),
                state_proj,
                jnp.pad(cut(step_proj, side, heads, 1), ((0, 0), (0, 128 - heads))),
            ],
            axis=1,
        )

    w_own = packed(r)
    w_rec = swap(packed(1 - r), "row")
    hid_rec = swap(hidden, "row")
    cot_rec = swap(cotangent, "row")
    wo_own = cut(output_proj, r, chan, 0)
    wo_part = cut(output_proj, 1 - r, chan, 0)
    wo_rec = swap(wo_part, "row")
    gain_f = gated_gain.astype(F32)
    gain_rec = swap(input_gain, "row")
    gains = jnp.concatenate([input_gain[None], gain_rec[None], jnp.zeros((6, half), F32)], axis=0)

    skip_lane = jnp.repeat(skip_gain, chan // heads)
    vtap = jnp.concatenate(
        [value_filter, value_shift[None], skip_lane[None], gain_f[None], jnp.zeros((1, chan), F32)], axis=0
    )
    stap = jnp.concatenate([shared_kernel, shared_offset[None], jnp.zeros((3, 256), F32)], axis=0)
    pad_h = (0, 8 - heads)
    head_par = jnp.concatenate([jnp.pad(step_bias, pad_h), jnp.pad(-jnp.exp(decay_log), pad_h)])
    head_par = jnp.broadcast_to(head_par[:, None], (16, 128))

    lane_head = jnp.arange(chan) // (chan // heads)
    sel = (jnp.arange(16)[:, None] == lane_head[None, :]).astype(BF16)
    out, proj_own, proj_col, dn_sum, dn_col, trow, rs, recip = layer(
        seq_len,
        dp,
        hidden,
        hid_rec,
        cotangent,
        cot_rec,
        gains,
        w_own,
        w_rec,
        vtap,
        stap,
        head_par,
        wo_own,
        wo_rec,
        sel,
    )
    outs = finish(
        big_rows(dp, width),
        heads,
        out,
        hidden,
        cotangent,
        dn_sum,
        dn_col,
        proj_own,
        proj_col,
        sel,
        trow,
        recip,
        rs,
        gains,
    )
    return tuple(outs[0:4]) + (outs[4].T,) + tuple(outs[5:])


def solution(mesh):
    in_specs = (
        P("dp", "row"),
        P("row", "col"),
        P("row", "col"),
        P("row", "col"),
        P("row", None),
        P(None, ("col", "row")),
        P(("col", "row")),
        P(),
        P(),
        P(("col", "row")),
        P(("col", "row")),
        P(("col", "row")),
        P("row"),
        P(("col", "row")),
        P("col", "row"),
        P("dp", "row"),
    )
    out_specs = (
        P("dp", "row"),
        P("dp", "row"),
        P("row", "col"),
        P("row", "col"),
        P("row", "col"),
        P("row", None),
        P(None, ("col", "row")),
        P(("col", "row")),
        P(),
        P(),
        P(("col", "row")),
        P(("col", "row")),
        P(("col", "row")),
        P("row"),
        P(("col", "row")),
        P("col", "row"),
    )
    return jax.shard_map(body, mesh=mesh, in_specs=in_specs, out_specs=out_specs, check_vma=False)
```

time: 286 us -> 146 us (0.51)
  waiting for transfers between devices: 89.4 us -> 0.82 us
  Pallas kernels: 59.4 us -> 134 us
  blocking collectives: 39.9 us -> 0 us
  other arithmetic: 29.2 us -> 3.08 us
  local copies, waits for them, and re-layouts: 26.1 us -> 5.74 us
  matrix products: 15.7 us -> 0 us
  between operations: 14.5 us -> 0.98 us
  starting transfers between devices: 11.2 us -> 1.58 us
    pallas_call x2, Pallas kernels: 59.4 us -> 134 us  [the longest x1 125 us: layer(): pl.pallas_call(functools.partial(layer_kernel, seq_len, dp, 4 * chan), in...]
    ppermute x16 -> x5, waiting for transfers between devices: 60.8 us -> 0.82 us  [swap(): return lax.ppermute(x, axis, SWAP)]
    psum x1 -> x0, blocking collectives: 39.9 us -> none  [body(): lax.psum((g_gate, g_value, g_step, g_state, vsum[0:4], vsum[4], s_part[0:...]
    psum x1 -> x0, waiting for transfers between devices: 28.5 us -> none  [body(): lax.psum((g_gate, g_value, g_step, g_state, vsum[0:4], vsum[4], s_part[0:...]
    dot_general x6 -> x0, matrix products: 15.7 us -> none  [the longest x4 12 us: dot_tn(): lax.dot_general(a, b, (((0,), (0,)), ((), ())), preferred_element_type=F32)]
    reduce_sum x6 -> x0, other arithmetic: 10.6 us -> none  [the longest x1 5.22 us: body(): g_norm = jnp.sum(d_normed * hidden32, axis=0)]
    ppermute x16 -> x5, starting transfers between devices: 11.1 us -> 1.58 us  [swap(): return lax.ppermute(x, axis, SWAP)]
    unnamed x80 -> x30, local copies, waits for them, and re-layouts: 9.98 us -> 1.34 us
  transfers between devices with their start and end apart: 17 -> 5, of which waited for: 6 -> 1; matrix products, arithmetic and copies ran while one was open for 19% -> 5% of each run, Pallas kernels for 0% -> 0%
where the time goes in v6:
time: 146 us
  Pallas kernels  134 us (92%)
  local copies, waits for them, and re-layouts  5.74 us (4%)
  other arithmetic  3.08 us (2%)
  starting transfers between devices  1.58 us (1%)
    pallas_call x1, Pallas kernels, layer(): pl.pallas_call(functools.partial(layer_kernel, seq_len, dp, 4 * chan), in...  125 us
    pallas_call x1, Pallas kernels, finish(): pl.pallas_call(functools.partial(finish_kernel, 2 * half), grid=(grid,),...  9.28 us
  transfers between devices with their start and end apart: 5, of which 1 were waited for; matrix products, arithmetic and copies ran while one was open for 5% of the time, Pallas kernels for 0%

profile of v6, /device:TPU:0, one launch (start us, length us, event | category | flops | bytes accessed | tf_op | source)
XLA Modules:
  0.0 146.1 jit_solution(1071352131726939261)
XLA Ops:
  0.7 0.6 collective-permute-start.2
  1.2 1.9 %constant_dynamic-slice_fusion = (bf16[384,384]{1,0:T(8,128)(2,1)S(1)}, bf16[384,384]{1,0:T(8,128)(2,1)}) fusion(bf16[768,384]{1,0:T(8,128)(2,1)} %param.30, s32[]{:T(128)S(6)} %select_n.29, s32[]{:T(128)S(6)} %select_n.27), kind=kLoop, calls=%fused_computation.17 | loop fusion | bytes 1179656 | tf_op jit(solution)/shard_map/dynamic_slice | solution.py:1154
  3.1 0.1 collective-permute-start.4
  3.2 0.4 collective-permute-start
  3.6 0.1 collective-permute-start.1
  3.7 0.8 constant_dynamic-slice_fusion.2
  4.5 0.2 copy.35
  4.6 0.2 copy.34
  4.9 0.1 constant_dynamic-slice_fusion.3
  5.1 1.1 fusion.3
  6.2 0.4 collective-permute-start.3
  6.6 0.1 pad.22.clone
  6.7 0.7 maximum_maximum_fusion.1.stap
  7.4 0.6 fusion.4.sel
  8.0 0.1 fusion.8
  8.1 0.1 pad.33.clone
  8.2 0.1 broadcast_in_dim_reshape.3
  8.3 0.6 concatenate.21.vtap
  9.0 0.7 maximum_maximum_fusion.gains
  9.6 0.8 collective-permute-done.3.w_rec
  10.4 0.9 copy-done
  11.4 0.7 broadcast_in_dim.48.head_par
  12.0 124.7 %layer.1 = (bf16[2816,384]{1,0:T(8,128)(2,1)}, bf16[2048,384]{1,0:T(8,128)(2,1)}, bf16[2048,384]{1,0:T(8,128)(2,1)}, bf16[2048,384]{1,0:T(8,128)(2,1)}, bf16[204...) custom-call(bf16[2048,384]{1,0:T(8,128)(2,1)} %hid.1, ...), custom_call_target="tpu_custom_call" | custom-call | tf_op jit(solution)/shard_map/layer/pallas_call | solution.py:875
  136.7 9.3 %finish.1 = (bf16[2048,384]{1,0:T(8,128)(2,1)}, f32[2048,384]{1,0:T(8,128)}, f32[384,768]{1,0:T(8,128)}, f32[384,768]{1,0:T(8,128)}, f32[12,384]{1,0:T(8,128)}, ...) custom-call(bf16[2816,384]{1,0:T(8,128)(2,1)} %get-tuple-element.40., ...), custom_call_target="tpu_custom_call" | custom-call | flops 20000000 | bytes 20000000 | tf_op jit(solution)/shard_map/finish/pallas_call | solution.py:1069
  (41 shorter events, 0.2 us)
Async XLA Ops:
  0.6 4.2 %copy-start.1 = (bf16[384,768]{1,0:T(8,128)(2,1)S(1)}, bf16[384,768]{1,0:T(8,128)(2,1)}, u32[]{:S(2)}) copy-start(bf16[384,768]{1,0:T(8,128)(2,1)} %param.18) | copy-start | bytes 1769476
  0.7 4.2 %copy-start.2 = (bf16[384,768]{1,0:T(8,128)(2,1)S(1)}, bf16[384,768]{1,0:T(8,128)(2,1)}, u32[]{:S(2)}) copy-start(bf16[384,768]{1,0:T(8,128)(2,1)} %param.17) | copy-start | bytes 1769476
  0.7 8.3 %collective-permute-start.2 = (f32[384]{0:T(512)}, f32[384]{0:T(512)S(1)}, u32[]{:S(2)}, u32[]{:S(2)}) collective-permute-start(f32[384]{0:T(512)} %param.28), channel_id=1, source_target_pairs={{0,2},{2,0},{1,3},{3,1},{4,6},{6,4},{5,7},{7,5},{8,10},{10,8},{9,1... | collective-permute-start | bytes 4616 | tf_op jit(solution)/shard_map/ppermute | solution.py:1123
  1.2 3.9 %copy-start.4 = (bf16[384,256]{1,0:T(8,128)(2,1)S(1)}, bf16[384,256]{1,0:T(8,128)(2,1)}, u32[]{:S(2)}) copy-start(bf16[384,256]{1,0:T(8,128)(2,1)} %param.20) | copy-start | bytes 589828
  3.1 6.5 %collective-permute-start.4 = (bf16[384,384]{1,0:T(8,128)(2,1)S(1)}, bf16[384,384]{1,0:T(8,128)(2,1)S(1)}, u32[]{:S(2)}, u32[]{:S(2)}) collective-permute-start(bf16[384,384]{1,0:T(8,128)(2,1)S(1)} %get-tuple-element.64), channel_id=1, source_target_pairs={{0,2},{2,0},{1,3},{3,1},{4,6},{6,4},{5,7},{7,5},{8,10},{10,8},{9,1... | collective-permute-start | bytes 884744 | tf_op jit(solution)/shard_map/ppermute | solution.py:1123
  3.2 8.2 %collective-permute-start = (bf16[2048,384]{1,0:T(8,128)(2,1)}, bf16[2048,384]{1,0:T(8,128)(2,1)}, u32[]{:S(2)}, u32[]{:S(2)}) collective-permute-start(bf16[2048,384]{1,0:T(8,128)(2,1)} %hid.1), channel_id=1, source_target_pairs={{0,2},{2,0},{1,3},{3,1},{4,6},{6,4},{5,7},{7,5},{8,10},{10,8},{9,1... | collective-permute-start | bytes 4718600 | tf_op jit(solution)/shard_map/ppermute | solution.py:1123
  3.6 7.8 %collective-permute-start.1 = (bf16[2048,384]{1,0:T(8,128)(2,1)}, bf16[2048,384]{1,0:T(8,128)(2,1)}, u32[]{:S(2)}, u32[]{:S(2)}) collective-permute-start(bf16[2048,384]{1,0:T(8,128)(2,1)} %cot.1), channel_id=1, source_target_pairs={{0,2},{2,0},{1,3},{3,1},{4,6},{6,4},{5,7},{7,5},{8,10},{10,8},{9,1... | collective-permute-start | bytes 4718600 | tf_op jit(solution)/shard_map/ppermute | solution.py:1123
  5.0 1.7 %copy-start.12 = (f32[6]{0:T(128)S(1)}, f32[6]{0:T(128)}, u32[]{:S(2)}) copy-start(f32[6]{0:T(128)} %param.25) | copy-start | bytes 76
  5.0 1.7 %copy-start.6 = (f32[4,256]{1,0:T(4,128)S(1)}, f32[4,256]{1,0:T(4,128)}, u32[]{:S(2)}) copy-start(f32[4,256]{1,0:T(4,128)} %param.23) | copy-start | bytes 12292
  5.0 1.7 %copy-start.9 = (f32[256]{0:T(256)S(1)}, f32[256]{0:T(256)}, u32[]{:S(2)}) copy-start(f32[256]{0:T(256)} %param.24) | copy-start | bytes 3076
  5.0 3.0 %copy-start.13 = (f32[6]{0:T(128)S(1)}, f32[6]{0:T(128)}, u32[]{:S(2)}) copy-start(f32[6]{0:T(128)} %param.26) | copy-start | bytes 76
  5.0 3.0 %copy-start.8 = (f32[384]{0:T(512)S(1)}, f32[384]{0:T(512)}, u32[]{:S(2)}) copy-start(f32[384]{0:T(512)} %param.28) | copy-start | bytes 4612
  5.1 3.1 %copy-start.7 = (f32[384]{0:T(512)S(1)}, f32[384]{0:T(512)}, u32[]{:S(2)}) copy-start(f32[384]{0:T(512)} %param.22) | copy-start | bytes 4612
  5.1 3.1 %copy-start.10 = (bf16[384]{0:T(512)(128)(2,1)S(1)}, bf16[384]{0:T(512)(128)(2,1)}, u32[]{:S(2)}) copy-start(bf16[384]{0:T(512)(128)(2,1)} %param.29) | copy-start | bytes 2308
  5.1 3.1 %copy-start.11 = (f32[6]{0:T(128)S(1)}, f32[6]{0:T(128)}, u32[]{:S(2)}) copy-start(f32[6]{0:T(128)} %param.27) | copy-start | bytes 76
  5.1 3.2 %copy-start.5 = (f32[4,384]{1,0:T(4,128)S(1)}, f32[4,384]{1,0:T(4,128)}, u32[]{:S(2)}) copy-start(f32[4,384]{1,0:T(4,128)} %param.21) | copy-start | bytes 18436
  6.2 4.3 %collective-permute-start.3 = (bf16[384,1152]{1,0:T(8,128)(2,1)S(1)}, bf16[384,1152]{1,0:T(8,128)(2,1)S(1)}, u32[]{:S(2)}, u32[]{:S(2)}) collective-permute-start(bf16[384,1152]{1,0:T(8,128)(2,1)S(1)} %get-tuple-element.70), channel_id=1, source_target_pairs={{0,2},{2,0},{1,3},{3,1},{4,6},{6,4},{5,7},{7,5},{8,10},{10,8},{9,1... | collective-permute-start | bytes 2654216 | tf_op jit(solution)/shard_map/ppermute | solution.py:1123
  9.6 1.7 %copy-start.3 = (bf16[384,384]{1,0:T(8,128)(2,1)}, bf16[384,384]{1,0:T(8,128)(2,1)S(1)}, u32[]{:S(2)}) copy-start(bf16[384,384]{1,0:T(8,128)(2,1)S(1)} %collective-permute-done.4.wo_rec) | copy-start | bytes 884740
  10.4 0.9 copy-start

commit v7 on v6

--- a/solution.py
+++ b/solution.py
@@ -13,11 +13,9 @@
 STEP = 256
 F32 = jnp.float32
 BF16 = jnp.bfloat16
-SWAP = [(0, 1), (1, 0)]
 AR_SPLIT = 2
-PROJ_EARLY = 5
-DN_LATE = 2
-EARLY_STEPS = [3, 5, 6, 7]
+EARLY_NEAR = [1, 2, 3, 4, 5, 7]
+EARLY_FAR = [1, 3, 4, 5, 7]
 
 
 def dot(a, b):
@@ -83,19 +81,13 @@
     return jnp.concatenate([jnp.where(lane < 64, x, zero), jnp.where(lane < 64, zero, x)], axis=0)
 
 
-def forward_block(fresh, width, weights_in, outs_a, outs_b, scratch):
+def forward_block(width, weights_in, outs_a, outs_b, scratch):
     hid_own, hid_rec, gains, w_own, w_rec, vtap, stap, head_par, wo_own, wo_rec = weights_in
     mixed_out, pre_gate_out, pre_value_out, conv_value_out, pre_shared_out, conv_shared_out = outs_a
     y_out, state_out, rows_out, nt_out = outs_b
-    state, vbuf, sbuf, po_own, po_send, square_row = scratch
+    state, vbuf, sbuf, po_own, po_send, square_rows = scratch
     chan = mixed_out.shape[1]
     pairs = chan // 128
-
-    @pl.when(fresh)
-    def _():
-        state[...] = jnp.zeros_like(state)
-        vbuf[0:8, :] = jnp.zeros((8, vbuf.shape[1]), F32)
-        sbuf[0:8, :] = jnp.zeros((8, sbuf.shape[1]), F32)
 
     h0 = hid_own[...].astype(F32)
     h1 = hid_rec[...].astype(F32)
@@ -128,8 +120,9 @@
     x = conv * sigmoid(conv)
     act = conv_s * sigmoid(conv_s)
 
-    head_rows = jnp.transpose(pre[:, 2 * chan + 256 : 2 * chan + 384])[0:8]
-    v = head_rows + head_par[0:8, 0:1]
+    head_rows = jnp.transpose(pre[:, 2 * chan + 256 : 2 * chan + 384])
+    first = lax.axis_index("row") == 0
+    v = jnp.where(first, head_rows[0:8], head_rows[6:14]) + head_par[0:8, 0:1]
     steps = softplus(v)
     logd = head_par[8:16, 0:1] * steps
     rows_out[0:8, :] = v
@@ -177,25 +170,15 @@
     weighted = (mix * vtap[6:7, :]).astype(BF16)
     po_own[...] = dot(weighted, wo_own[...]).astype(BF16)
     po_send[...] = dot(weighted, wo_rec[...]).astype(BF16)
-    square_row[...] = plain_sums(jnp.ones((16, chan), BF16), mix * mix)[0:1]
-
-
-def early_levels(dp):
-    return dp.bit_length()
+    square_rows[0:4, :] = plain_sums(jnp.ones((16, chan), BF16), mix * mix)[0:4]
 
 
 def early_steps(dp, blocks):
-    count = early_levels(dp)
-    if count == 4 and blocks == 8:
-        return EARLY_STEPS
-    return [max(2, blocks - count + n) if blocks > count else blocks - 1 for n in range(count)]
-
-
-def early_orders(dp):
-    bits = dp.bit_length() - 1
-    near = tuple(range(bits))
-    far = tuple(range(1, bits)) + (0,)
-    return [far if n % 2 else near for n in range(2 * AR_SPLIT)]
+    count = 2 * (dp.bit_length() - 1)
+    if count == 6 and blocks == 8:
+        return EARLY_NEAR, EARLY_FAR
+    steps = [min(blocks - 1, 1 + n * (blocks - 1) // count) for n in range(count)]
+    return steps, steps[:-1]
 
 
 def partner_of(me, k):
@@ -289,19 +272,13 @@
     rs_gate[...] = plain_sums(jnp.ones((16, chan), BF16), d_gate * gate)
 
 
-def scan_block(fresh, ins, weights_in, outs, scratch):
-    rows_in, pre_value, conv_value, pre_shared, conv_shared, y_in, state_in, hid_own, hid_rec = ins
-    w_own, w_rec, vtap, stap, head_par, sel_ref, dy_in, p_gate, rs_gate = weights_in
-    p_out, rsum_out, acc_v, acc_s, acc_h, acc_n, dn_own, dn_rec = outs
+def scan_block(ins, weights_in, outs, scratch):
+    rows_in, pre_value, conv_value, pre_shared, conv_shared, y_in, state_in = ins
+    vtap, stap, head_par, sel_ref, dy_in = weights_in
+    p_out, rsum_out, acc_v, acc_s, acc_h = outs
     grad, vbuf, sbuf, dxbuf, dbbuf = scratch
     chan = conv_value.shape[1]
     pairs = chan // 128
-
-    @pl.when(fresh)
-    def _():
-        grad[...] = jnp.zeros_like(grad)
-        vbuf[STEP : STEP + 8, :] = jnp.zeros((8, vbuf.shape[1]), F32)
-        sbuf[STEP : STEP + 8, :] = jnp.zeros((8, sbuf.shape[1]), F32)
 
     recip = jnp.transpose(rows_in[16:24, :])[:, 0:1]
     conv = conv_value[...]
@@ -389,7 +366,13 @@
         rsum_out[:, lo:hi] += jnp.broadcast_to(
             jnp.sum(d_step * pre_step, axis=0, keepdims=True), (8, SUB)
         )
-        d_cols = jnp.transpose(jnp.concatenate([d_step, jnp.zeros((120, SUB), F32)], axis=0))
+        zeros = jnp.zeros((6, SUB), F32)
+        both = jnp.where(
+            lax.axis_index("row") == 0,
+            jnp.concatenate([d_step[0:6], zeros, zeros[0:4]], axis=0),
+            jnp.concatenate([zeros, d_step[0:6], zeros[0:4]], axis=0),
+        )
+        d_cols = jnp.transpose(jnp.concatenate([both, jnp.zeros((112, SUB), F32)], axis=0))
         p_out[lo:hi, chan + 256 : chan + 384] = (recip[lo:hi] * d_cols).astype(BF16)
 
     d_conv = dxbuf[...] * (sig_v + x * (1.0 - sig_v))
@@ -416,12 +399,18 @@
     ones = jnp.ones((16, chan), BF16)
     rsum_out[...] += plain_sums(ones, d_value * pv)
     rsum_out[...] += plain_sums(ones[:, 0:256], d_shared * ps)
+
+
+def width_block(valid, ins, outs):
+    p_gate, p_all, hid_own, hid_rec, w_own, w_rec = ins
+    dn_own, dn_rec, acc_n = outs
+    chan = p_gate.shape[1]
     pg = p_gate[...]
-    pb = p_out[...]
+    pb = p_all[...]
     for n, (hid, weight, dn) in enumerate(((hid_own, w_own, dn_own), (hid_rec, w_rec, dn_rec))):
         part = dot_nt(pg, weight[:, 0:chan]) + dot_nt(pb, weight[:, chan:])
         dn[...] = part.astype(BF16)
-        acc_n[8 * n : 8 * n + 8, :] += fold8(part * hid[...].astype(F32))
+        acc_n[8 * n : 8 * n + 8, :] += jnp.where(valid, fold8(part * hid[...].astype(F32)), 0.0)
 
 
 def unit_rows(dp):
@@ -459,19 +448,22 @@
     seq_len,
     dp,
     inner_width,
-    hid_own_hbm,
-    hid_rec_hbm,
-    cot_own_hbm,
-    cot_rec_hbm,
-    gains,
-    w_own,
-    w_rec,
-    vtap,
-    stap,
-    head_par,
-    wo_own,
-    wo_rec,
-    sel,
+    hid_hbm,
+    cot_hbm,
+    gate_w,
+    value_w,
+    state_w,
+    out_w,
+    step_t,
+    value_filter,
+    value_shift,
+    shared_kernel,
+    shared_offset,
+    decay_log,
+    step_bias,
+    skip_gain,
+    input_gain,
+    gated_gain,
     sums_out,
     proj_out,
     proj_col,
@@ -480,6 +472,18 @@
     trow,
     rs_out,
     recip_out,
+    state_out,
+    w_own,
+    w_rec,
+    wo_own,
+    wo_rec,
+    vtap,
+    stap,
+    head_par,
+    head_rows,
+    gains,
+    gains_land,
+    sel,
     hid_own,
     hid_rec,
     cot_own,
@@ -510,13 +514,13 @@
     dn_sum,
     sums,
     sums_land,
-    go_own,
     go_rec,
     swap_send,
     swap_land,
-    row_send,
-    row_land,
-    col_send,
+    extra_send,
+    extra_land,
+    extra_sum,
+    shared_sum,
     col_land,
     rs_land,
     acc_v,
@@ -528,6 +532,8 @@
     land,
     out,
     load_sem,
+    feed_sem,
+    weight_sem,
     save_sem,
     po_sem,
     dn_sem,
@@ -563,8 +569,35 @@
         return pl.ds(pl.multiple_of(i * STEP, STEP), STEP)
 
     def load(n, i):
-        src, dst = ((hid_own_hbm, hid_own), (hid_rec_hbm, hid_rec), (cot_own_hbm, cot_own), (cot_rec_hbm, cot_rec))[n]
+        src, dst = ((hid_hbm, hid_own), (cot_hbm, cot_own))[n]
         return pltpu.make_async_copy(src.at[span(i), :], dst.at[span(i), :], load_sem.at[n, i])
+
+    def feed(n, i):
+        src, dst = ((hid_hbm, hid_rec), (cot_hbm, cot_rec))[n]
+        return remote(src.at[span(i), :], dst.at[span(i), :], feed_sem.at[0, n, i], feed_sem.at[1, n, i], to_row)
+
+    def weight_parts(side, to_w, to_wo):
+        cols = pl.ds(pl.multiple_of(side * chan, 128), chan)
+        return (
+            (gate_w.at[:, cols], to_w.at[:, 0:chan]),
+            (value_w.at[:, cols], to_w.at[:, chan : 2 * chan]),
+            (state_w, to_w.at[:, 2 * chan : 2 * chan + 256]),
+            (out_w.at[cols, :], to_wo),
+        )
+
+    own_weights = [
+        pltpu.make_async_copy(src, dst, weight_sem.at[0, n])
+        for n, (src, dst) in enumerate(weight_parts(r, w_own, wo_own))
+    ]
+    rec_weights = [
+        remote(src, dst, weight_sem.at[1, n], weight_sem.at[2, n], to_row)
+        for n, (src, dst) in enumerate(weight_parts(1 - r, w_rec, wo_rec))
+    ]
+    step_cols = pl.ds(2 * chan + 256, 128)
+    rec_weights.append(
+        remote(w_own.at[:, step_cols], w_rec.at[:, step_cols], weight_sem.at[1, 4], weight_sem.at[2, 4], to_row)
+    )
+    rec_weights.append(remote(gains, gains_land, weight_sem.at[1, 5], weight_sem.at[2, 5], to_row))
 
     def save(n, i):
         src, dst = ((proj_s, proj_out), (dn_sum, dn_out))[n]
@@ -573,41 +606,79 @@
     def pair_copy(sem, i):
         return remote(pair_send.at[span(i), :], pair_land.at[span(i), :], sem.at[0, i], sem.at[1, i], to_row)
 
-    def col_copy(n, i):
-        src, dst = ((proj_s, proj_col), (dn_sum, dn_col))[n]
-        return remote(src.at[span(i), :], dst.at[span(i), :], col_sem.at[n, 0, i], col_sem.at[n, 1, i], to_col)
-
     def small_copy(src, dst, n, target):
         return remote(src, dst, swap_sem.at[0, n], swap_sem.at[1, n], target)
 
-    for n in range(4):
+    for copy in own_weights:
+        copy.start()
+    for n in range(2):
         for i in range(blocks):
             load(n, i).start()
+    heads = decay_log.shape[0]
+    sel[...] = (iota(sel.shape, 0) == iota(sel.shape, 1) // 64).astype(F32).astype(BF16)
+    head_rows[...] = jnp.zeros_like(head_rows)
+    for n, ref in enumerate((step_bias, decay_log, skip_gain)):
+        head_rows[n, 0:heads] = ref[...]
+    head_cols = jnp.transpose(head_rows[...])[0:8]
+    real = iota((8, 128), 0) < heads
+    head_par[0:8, :] = jnp.broadcast_to(head_cols[:, 0:1], (8, 128))
+    head_par[8:16, :] = jnp.where(real, -jnp.exp(jnp.broadcast_to(head_cols[:, 1:2], (8, 128))), 0.0)
+    vtap[0:4, :] = value_filter[...]
+    vtap[4, :] = value_shift[...]
+    vtap[5:6, :] = jnp.sum(sel[0:8, :].astype(F32) * head_cols[:, 2:3], axis=0, keepdims=True)
+    vtap[6, :] = gated_gain[...].astype(F32)
+    stap[0:4, :] = shared_kernel[...]
+    stap[4, :] = shared_offset[...]
+    gains[...] = jnp.zeros_like(gains)
+    gains[0, :] = input_gain[...]
+    dxbuf[0:128, :] = jnp.zeros((128, half), F32)
+    dxbuf[0 : step_t.shape[0], :] = step_t[...].astype(F32)
+    w_own[:, 2 * chan + 256 : 2 * chan + 384] = jnp.transpose(dxbuf[0:128, :]).astype(BF16)
     greet([partner_of(me, k) for k in range(bits)] + [to_row, to_col, to_both])
-    for ref in (acc_v, acc_s, acc_h, acc_n, go_own, go_rec):
+    for copy in rec_weights:
+        copy.start()
+    for n in range(2):
+        for i in range(blocks):
+            feed(n, i).start()
+
+    def chunk_rows(n, side):
+        return pl.ds(pl.multiple_of(tail + n * size + side * half, 128), half)
+
+    go_own = acc.at[chunk_rows(0, r), :]
+    for ref in (acc_v, acc_s, acc_h, acc_n, go_rec):
         ref[...] = jnp.zeros_like(ref)
+    go_own[...] = jnp.zeros((chan, half), F32)
+
+    for copy in own_weights + rec_weights:
+        copy.wait()
+    gains[1:2, :] = gains_land[0:1, :]
+
+    def sums_copy(n, i):
+        target = (to_row, to_col, to_both)[n]
+        return remote(sums.at[i], sums_land.at[n, i], sum_sem.at[0, n, i], sum_sem.at[1, n, i], target)
 
     def take_proj(i):
         pair_copy(po_sem, i).wait()
         part = pair_own[span(i), :].astype(F32) + pair_land[span(i), :].astype(F32)
         proj_s[span(i), :] = part.astype(BF16)
+        dots = plain_sums(jnp.ones((16, half), BF16), part * cot_own[span(i), :].astype(F32))
+        sums[i, 4:8, :] = dots[4:8]
+        for n in range(3):
+            sums_copy(n, i).start()
         save(0, i).start()
 
-        @pl.when(i < PROJ_EARLY)
-        def _():
-            col_copy(0, i).start()
-
-        load(2, i).wait()
-        dots = plain_sums(jnp.ones((16, half), BF16), part * cot_own[span(i), :].astype(F32))
-        sums[pl.ds(8 + i, 1), :] = dots[0:1]
-
-    @pl.loop(0, blocks)
-    def _(i):
+    def take_sums(i):
+        for n in range(3):
+            sums_copy(n, i).wait()
+        total = (sums[i] + sums_land[0, i]) + (sums_land[1, i] + sums_land[2, i])
+        scale = lax.rsqrt(total[0:1] / inner_width + EPSILON)
+        coef = total[4:5] * (scale * scale * scale) / inner_width
+        trow[0:8, span(i)] = jnp.broadcast_to(scale, (8, STEP))
+        trow[8:16, span(i)] = jnp.broadcast_to(coef, (8, STEP))
+
+    def forward(i):
         here = span(i)
-        load(0, i).wait()
-        load(1, i).wait()
         forward_block(
-            i % steps_per_seq == 0,
             width,
             (
                 hid_own.at[here, :],
@@ -630,37 +701,10 @@
                 conv_shared.at[here, :],
             ),
             (y_scan.at[here, :], states.at[here, :], rows.at[:, here], normed_t.at[:, here]),
-            (state, vbuf, sbuf, pair_own.at[here, :], pair_send.at[here, :], sums.at[pl.ds(i, 1), :]),
+            (state, vbuf, sbuf, pair_own.at[here, :], pair_send.at[here, :], sums.at[i]),
         )
 
-        @pl.when(i > 0)
-        def _():
-            take_proj(i - 1)
-
-        pair_copy(po_sem, i).start()
-
-    take_proj(blocks - 1)
-    ends = []
-    for n, target in enumerate((to_row, to_col, to_both)):
-        copy = remote(sums, sums_land.at[n], sum_sem.at[0, n], sum_sem.at[1, n], target)
-        copy.start()
-        ends.append(copy)
-    for i in range(PROJ_EARLY, blocks):
-        col_copy(0, i).start()
-    recip_out[...] = rows[16:24, :]
-    for i in range(blocks):
-        load(3, i).wait()
-    for copy in ends:
-        copy.wait()
-    total = (sums[...] + sums_land[0]) + (sums_land[1] + sums_land[2])
-    scale = lax.rsqrt(total[0:8] / inner_width + EPSILON)
-    coef = total[8:16] * (scale * scale * scale) / inner_width
-    for i in range(blocks):
-        trow[0:8, i * STEP : (i + 1) * STEP] = jnp.broadcast_to(scale[i : i + 1], (8, STEP))
-        trow[8:16, i * STEP : (i + 1) * STEP] = jnp.broadcast_to(coef[i : i + 1], (8, STEP))
-
-    @pl.loop(0, blocks)
-    def _(i):
+    def gate(i):
         here = span(i)
         gate_block(
             (
@@ -679,15 +723,59 @@
             (acc_v, go_own, go_rec, dy_s.at[here, :], p_gate.at[here, :], rs_in.at[:, here]),
         )
 
-    def chunk_rows(n, side):
-        return pl.ds(pl.multiple_of(tail + n * size + side * half, 128), half)
+    first_part = max(1, blocks // 4)
+    proj_parts = [(0, first_part), (first_part, blocks)]
+    half_way = blocks // 2
+    dn_parts = [(half_way, blocks), (0, half_way)] if half_way else [(0, blocks)]
+
+    def wide_copy(n, part, index):
+        src, dst = ((proj_s, proj_col), (dn_sum, dn_col))[n]
+        rows_n = pl.ds(part[0] * STEP, (part[1] - part[0]) * STEP)
+        return remote(src.at[rows_n, :], dst.at[rows_n, :], col_sem.at[n, 0, index], col_sem.at[n, 1, index], to_col)
+
+    @pl.loop(0, blocks)
+    def _(i):
+        load(0, i).wait()
+        feed(0, i).wait()
+
+        @pl.when(i % steps_per_seq == 0)
+        def _():
+            state[...] = jnp.zeros_like(state)
+            vbuf[0:8, :] = jnp.zeros((8, chan), F32)
+            sbuf[0:8, :] = jnp.zeros((8, 256), F32)
+
+        forward(i)
+        load(1, i).wait()
+        feed(1, i).wait()
+
+        @pl.when(i > 0)
+        def _():
+            take_proj(i - 1)
+
+        pair_copy(po_sem, i).start()
+        if first_part < blocks:
+
+            @pl.when(i == first_part)
+            def _():
+                wide_copy(0, proj_parts[0], 0).start()
+
+    take_proj(blocks - 1)
+    if first_part < blocks:
+        wide_copy(0, proj_parts[1], 1).start()
+    else:
+        wide_copy(0, proj_parts[0], 0).start()
+    recip_out[...] = rows[16:24, :]
+
+    @pl.loop(0, blocks)
+    def _(i):
+        take_sums(i)
+        gate(i)
 
     swaps = [small_copy(swap_send.at[n], swap_land.at[n], n, to_row) for n in range(2)]
     swap_send[0] = go_rec[...].astype(BF16)
     swaps[0].start()
     swap_send[1] = dot(normed_t[half:width, :], p_gate[...]).astype(BF16)
     swaps[1].start()
-    acc[chunk_rows(0, r), :] = go_own[...]
     acc[chunk_rows(1, r), :] = dot(normed_t[0:half, :], p_gate[...])
     if size > width:
         for n in range(3):
@@ -704,12 +792,29 @@
         dn_sum[span(i), :] = part.astype(BF16)
         save(1, i).start()
 
+    def over_width(valid, i):
+        here = span(i)
+        width_block(
+            valid,
+            (p_gate.at[here, :], p_all.at[here, :], hid_own.at[here, :], hid_rec.at[here, :], w_own, w_rec),
+            (pair_own.at[here, :], pair_send.at[here, :], acc_n),
+        )
+
+    p_all[span(blocks - 1), :] = jnp.zeros((STEP, wide), BF16)
+
     @pl.loop(0, blocks)
     def _(later):
         i = blocks - 1 - later
         here = span(i)
+
+        @pl.when(later % steps_per_seq == 0)
+        def _():
+            state[...] = jnp.zeros_like(state)
+            vbuf[STEP : STEP + 8, :] = jnp.zeros((8, chan), F32)
+            sbuf[STEP : STEP + 8, :] = jnp.zeros((8, 256), F32)
+
+        over_width(later > 0, jnp.minimum(i + 1, blocks - 1))
         scan_block(
-            later % steps_per_seq == 0,
             (
                 rows.at[:, here],
                 pre_value.at[here, :],
@@ -718,48 +823,37 @@
                 conv_shared.at[here, :],
                 y_scan.at[here, :],
                 states.at[here, :],
-                hid_own.at[here, :],
-                hid_rec.at[here, :],
             ),
-            (
-                w_own,
-                w_rec,
-                vtap,
-                stap,
-                head_par,
-                sel,
-                dy_s.at[here, :],
-                p_gate.at[here, :],
-                rs_in.at[:, here],
-            ),
-            (
-                p_all.at[here, :],
-                rs_in.at[:, here],
-                acc_v,
-                acc_s,
-                acc_h,
-                acc_n,
-                pair_own.at[here, :],
-                pair_send.at[here, :],
-            ),
+            (vtap, stap, head_par, sel, dy_s.at[here, :]),
+            (p_all.at[here, :], rs_in.at[:, here], acc_v, acc_s, acc_h),
             (state, vbuf, sbuf, dxbuf, dbbuf),
         )
 
+        @pl.when(later > 1)
+        def _():
+            take_dn(i + 2)
+            for index, part in enumerate(dn_parts[:-1]):
+
+                @pl.when(i + 2 == part[0])
+                def _(index=index, part=part):
+                    wide_copy(1, part, index).start()
+
         @pl.when(later > 0)
         def _():
-            take_dn(i + 1)
-
-            @pl.when(i + 1 >= DN_LATE)
-            def _():
-                col_copy(1, i + 1).start()
-
-        pair_copy(dn_sem, i).start()
-        for level, when in enumerate(early_steps(dp, blocks)):
-
-            @pl.when(later == when)
-            def _(level=level):
-                for n in firsts:
-                    end_level(n, level)
+            pair_copy(dn_sem, i + 1).start()
+
+        for kind, steps in enumerate(early_steps(dp, blocks)):
+            for level, when in enumerate(steps):
+
+                @pl.when(later == when)
+                def _(kind=kind, level=level):
+                    for n in firsts[kind::2]:
+                        end_level(n, level)
+
+    over_width(True, 0)
+    pair_copy(dn_sem, 0).start()
+    if blocks > 1:
+        take_dn(1)
 
     def sum8(ref, n):
         return jnp.sum(ref[8 * n : 8 * n + 8, :], axis=0, keepdims=True)
@@ -769,54 +863,64 @@
         jnp.concatenate([sum8(acc_n, n), jnp.zeros((1, 512 - half), F32)], axis=1) for n in (0, 1)
     ]
     pad6 = jnp.zeros((6, 256), F32)
-    row_send[half : half + 16, 0:256] = jnp.concatenate(
-        [small, norm_rec[:, 0:256], norm_rec[:, 256:512], pad6], axis=0
-    ).astype(BF16)
-    row_send[half : half + 16, 256:wide] = jnp.zeros((16, wide - 256), BF16)
-    for lo in range(0, wide, 384):
-        row_send[0:half, lo : lo + 384] = dot(normed_t[half:width, :], p_all[:, lo : lo + 384]).astype(BF16)
-    row_copy = small_copy(row_send, row_land, 2, to_row)
-    row_copy.start()
+    misc_row = small_copy(swap_send.at[0], swap_land.at[0], 4, to_row)
+    value_row = small_copy(swap_send.at[1], swap_land.at[1], 5, to_row)
+    swap_send[1] = dot(normed_t[half:width, :], p_all[:, 0:chan]).astype(BF16)
+    value_row.start()
+    extra_send[...] = jnp.concatenate([small, norm_rec[:, 0:256], norm_rec[:, 256:512], pad6], axis=0)
+    extra_row = small_copy(extra_send, extra_land.at[0], 2, to_row)
+    extra_row.start()
     rs_row = small_copy(rs_in, rs_land.at[0], 3, to_row)
     rs_row.start()
-    acc[0:half, :] = dot(normed_t[0:half, :], p_all[:, chan:wide])
     acc[chunk_rows(2, r), :] = dot(normed_t[0:half, :], p_all[:, 0:chan])
-    row_copy.wait()
-    acc[chunk_rows(2, 1 - r), :] = row_land[0:half, 0:chan].astype(F32)
+    value_row.wait()
+    acc[chunk_rows(2, 1 - r), :] = swap_land[1].astype(F32)
     for n in values:
         start_level(n, 0)
-    gate_sums = acc[0:half, 0:256] + row_land[0:half, chan : chan + 256].astype(F32)
+    swap_send[0] = dot(normed_t[half:width, :], p_all[:, chan:wide]).astype(BF16)
+    misc_row.start()
+    extra_row.wait()
     extra = jnp.concatenate([small, norm_own[:, 0:256], norm_own[:, 256:512], pad6], axis=0)
-    extra = extra + row_land[half : half + 16, 0:256].astype(F32)
-    col_send[0:half, :] = gate_sums.astype(BF16)
-    col_send[half : half + 16, :] = extra.astype(BF16)
-    mid_copy = small_copy(col_send, col_land, 4, to_col)
-    mid_copy.start()
+    extra_sum[...] = extra + extra_land[0]
+    extra_col = small_copy(extra_sum, extra_land.at[1], 6, to_col)
+    extra_col.start()
+    shared = dot(normed_t[0:half, :], p_all[:, chan:wide])
+    split = half // 2
+    misc_row.wait()
+    shared_sum[...] = (shared[:, 0:256] + swap_land[0, :, 0:256].astype(F32)).astype(BF16)
+    theirs = pl.ds(pl.multiple_of((1 - c) * split, 16), split)
+    state_col = small_copy(shared_sum.at[theirs, :], col_land, 7, to_col)
+    state_col.start()
+    step_t = jnp.transpose(shared[:, 256:384] + swap_land[0, :, 256:384].astype(F32))[0:16]
     rs_row.wait()
     rs_out[...] = rs_in[...] + rs_land[0]
-    rs_col = small_copy(rs_out, rs_land.at[1], 5, to_col)
+    rs_col = small_copy(rs_out, rs_land.at[1], 8, to_col)
     rs_col.start()
     take_dn(0)
-    for i in reversed(range(DN_LATE)):
-        col_copy(1, i).start()
-
-    acc[0:half, 256:384] = jnp.concatenate(
-        [acc[0:half, 256:320], row_land[0:half, chan + 256 : chan + 320].astype(F32)], axis=1
-    )
-    acc[half : half + 16, 256:384] = jnp.zeros((16, 128), F32)
-    first = half + 16
-    acc[first : first + 8, :] = jnp.concatenate(
+    wide_copy(1, dn_parts[-1], len(dn_parts) - 1).start()
+
+    acc[0:split, 256:384] = jnp.zeros((split, 128), F32)
+    first = split
+    acc[first : first + 16, 256:384] = jnp.zeros((16, 128), F32)
+    acc[first + 16 : first + 24, :] = jnp.concatenate(
         [sum8(acc_v, n) for n in range(7)] + [jnp.zeros((1, chan), F32)], axis=0
     )
-    acc[first + 8 : first + 24, :] = jnp.broadcast_to(
+    acc[first + 24 : first + 40, :] = jnp.broadcast_to(
         jnp.sum(acc_h[...], axis=1, keepdims=True), (16, chan)
     )
-    if tail > first + 24:
-        acc[first + 24 : tail, :] = jnp.zeros((tail - first - 24, chan), F32)
-    mid_copy.wait()
-    acc[0 : half + 16, 0:256] = col_send[...].astype(F32) + col_land[...].astype(F32)
+    acc[first + 40 : first + 56, :] = step_t
+    if tail > first + 56:
+        acc[first + 56 : tail, :] = jnp.zeros((tail - first - 56, chan), F32)
+    extra_col.wait()
+    acc[first : first + 16, 0:256] = extra_sum[...] + extra_land[1]
+    state_col.wait()
+    acc[0:split, 0:256] = (
+        shared_sum[pl.ds(pl.multiple_of(c * split, 16), split), :].astype(F32)
+        + col_land[...].astype(F32)
+    )
     start_level(misc, 0)
-    early = early_levels(dp)
+    mine = pl.ds(pl.multiple_of(c * split, 16), split)
+    last_col = small_copy(out.at[pl.ds(0, split), pl.ds(0, 256)], state_out.at[mine, :], 9, to_col)
     done = []
 
     def save_chunk(n):
@@ -825,39 +929,44 @@
         copy.start()
         done.append(copy)
 
-    def end(n, level):
-        end_level(n, level)
+    for n in firsts[0::2]:
+        save_chunk(n)
+    for level in range(2 * bits):
+        if level == 0:
+            for n in firsts[1::2]:
+                end_level(n, 2 * bits - 1)
+                save_chunk(n)
         if level == 2 * bits - 1:
-            save_chunk(n)
-
-    if early >= 2 * bits:
-        for n in firsts:
-            save_chunk(n)
-
-    for level in range(2 * bits):
-        if early + level < 2 * bits:
-            for n in firsts:
-                end(n, early + level)
+            end_level(misc, level)
+            last_col.start()
+            save_chunk(misc)
+            state_out[mine, :] = out[0:split, 0:256]
         for n in values:
-            end(n, level)
-        end(misc, level)
+            end_level(n, level)
+            if level == 2 * bits - 1:
+                save_chunk(n)
+        if level < 2 * bits - 1:
+            end_level(misc, level)
     for copy in done:
         copy.wait()
+    last_col.wait()
     rs_col.wait()
     rs_out[...] = rs_out[...] + rs_land[1]
     for i in range(blocks):
         for n in range(2):
             save(n, i).wait()
-            col_copy(n, i).wait()
-
-
-def layer(seq_len, dp, hidden, hid_rec, cot, cot_rec, gains, w_own, w_rec, vtap, stap, head_par, wo_own, wo_rec, sel):
+    for n, parts in enumerate((proj_parts if first_part < blocks else proj_parts[:1], dn_parts)):
+        for index, part in enumerate(parts):
+            wide_copy(n, part, index).wait()
+
+
+def layer(seq_len, dp, hidden, cot, gate_w, value_w, state_w, out_w, *params):
     tokens, half = hidden.shape
-    chan = vtap.shape[1]
-    wide = w_own.shape[1] - chan
+    chan = params[1].shape[1]
+    wide = chan + 384
     bits = dp.bit_length() - 1
     size = big_rows(dp, 2 * half)
-    tail = misc_rows(dp, half + 48)
+    tail = misc_rows(dp, half // 2 + 64)
     total = tail + 3 * size
     blocks = tokens // STEP
     vmem = pl.BlockSpec(memory_space=pltpu.VMEM)
@@ -874,8 +983,8 @@
 
     return pl.pallas_call(
         functools.partial(layer_kernel, seq_len, dp, 4 * chan),
-        in_specs=[hbm] * 4 + [vmem] * 9,
-        out_specs=[hbm, hbm, hbm, hbm, hbm, vmem, vmem, vmem],
+        in_specs=[hbm] * 6 + [vmem] * len(params),
+        out_specs=[hbm, hbm, hbm, hbm, hbm, vmem, vmem, vmem, vmem],
         out_shape=[
             jax.ShapeDtypeStruct((total, chan), BF16),
             act(),
@@ -885,8 +994,20 @@
             jax.ShapeDtypeStruct((16, tokens), F32),
             jax.ShapeDtypeStruct((8, tokens), F32),
             jax.ShapeDtypeStruct((8, tokens), F32),
+            jax.ShapeDtypeStruct((half, 256), BF16),
         ],
         scratch_shapes=[
+            room(half, chan + wide),
+            room(half, chan + wide),
+            room(chan, half),
+            room(chan, half),
+            room(8, chan, dtype=F32),
+            room(8, 256, dtype=F32),
+            room(16, 128, dtype=F32),
+            room(8, 128, dtype=F32),
+            room(8, half, dtype=F32),
+            room(8, half, dtype=F32),
+            room(16, chan),
             room(tokens, half),
             room(tokens, half),
             room(tokens, half),
@@ -915,16 +1036,16 @@
             room(tokens, half),
             room(tokens, half),
             room(tokens, half),
-            room(16, STEP, dtype=F32),
-            room(3, 16, STEP, dtype=F32),
-            room(chan, half, dtype=F32),
+            room(blocks, 8, STEP, dtype=F32),
+            room(3, blocks, 8, STEP, dtype=F32),
             room(chan, half, dtype=F32),
             room(2, half, chan),
             room(2, half, chan),
-            room(half + 16, wide),
-            room(half + 16, wide),
-            room(half + 16, 256),
-            room(half + 16, 256),
+            room(16, 256, dtype=F32),
+            room(2, 16, 256, dtype=F32),
+            room(16, 256, dtype=F32),
+            room(half, 256),
+            room(half // 2, 256),
             room(2, 8, tokens, dtype=F32),
             room(56, chan, dtype=F32),
             room(40, 256, dtype=F32),
@@ -934,13 +1055,15 @@
             room(total, chan),
             room(total, chan),
             room(total, chan),
-            flags(4, blocks),
+            flags(2, blocks),
+            flags(2, 2, blocks),
+            flags(3, 6),
             flags(2, blocks),
             flags(2, blocks),
             flags(2, blocks),
-            flags(2, 2, blocks),
-            flags(2, 3),
-            flags(2, 6),
+            flags(2, 2, 3),
+            flags(2, 3, blocks),
+            flags(2, 10),
             flags(3 * AR_SPLIT + 1, 2 * bits),
             flags(3 * AR_SPLIT + 1, 2 * bits),
             flags(3 * AR_SPLIT + 1),
@@ -949,7 +1072,7 @@
             collective_id=0, has_side_effects=True, vmem_limit_bytes=67_000_000
         ),
         name="layer",
-    )(hidden, hid_rec, cot, cot_rec, gains, w_own, w_rec, vtap, stap, head_par, wo_own, wo_rec, sel)
+    )(hidden, cot, gate_w, value_w, state_w, out_w, *params)
 
 
 def finish_kernel(
@@ -960,13 +1083,13 @@
     value_a,
     value_b,
     misc,
+    state,
     hid,
     cot,
     dn_sum,
     dn_col,
     proj_own,
     proj_col,
-    sel,
     trow,
     recip_in,
     rs,
@@ -995,7 +1118,7 @@
     proj = proj_own[...].astype(F32) + proj_col[...].astype(F32)
     result[...] = (hid32 + cols[:, 0:1] * proj).astype(BF16)
     d_normed = dn_sum[...].astype(F32) + dn_col[...].astype(F32)
-    hidden_grad[...] = cot[...].astype(F32) + d_normed * gains[0:1, :] - cols[:, 8:9] * hid32
+    hidden_grad[...] = cot[...].astype(F32) + d_normed * gains[...].reshape(1, half) - cols[:, 8:9] * hid32
     @pl.when(pl.program_id(0) < half // 128)
     def _():
         g_output[...] = out_rows[...].astype(F32)
@@ -1006,13 +1129,10 @@
 
     @pl.when(pl.program_id(0) == 0)
     def _():
-        g_state[...] = misc[0:half, 0:256].astype(F32)
-        step_t = jnp.transpose(misc[0:half, 256:384].astype(F32))
+        g_state[...] = state[...].astype(F32)
+        small = misc[half // 2 : half // 2 + 64, :].astype(F32)
         heads = g_step.shape[0] // 2
-        own, rec = step_t[0:heads], step_t[64 : 64 + heads]
-        first = lax.axis_index("row") == 0
-        g_step[...] = jnp.concatenate([jnp.where(first, own, rec), jnp.where(first, rec, own)], axis=0)
-        small = misc[half : half + 48, :].astype(F32)
+        g_step[...] = small[40 : 40 + 2 * heads]
         g_kernel[...] = small[0:4, 0:256]
         g_offset[...] = small[4, 0:256]
         g_norm[0:256] = small[8, 0:256]
@@ -1023,11 +1143,12 @@
         head = jnp.transpose(small[24:40, 0:128])[0:8]
         g_decay[...] = head[0, 0:heads]
         g_bias[...] = head[0, 8 : 8 + heads]
-        skip = dot_nt(small[16:32].astype(BF16), sel[...])
+        sel = (iota((16, half), 0) == iota((16, half), 1) // (half // heads)).astype(F32).astype(BF16)
+        skip = dot_nt(small[16:32].astype(BF16), sel)
         g_skip[...] = skip[5, 0:heads]
 
 
-def finish(size, heads, out, hid, cot, dn_sum, dn_col, proj_own, proj_col, sel, trow, recip, rs, gains):
+def finish(size, heads, out, state, hid, cot, dn_sum, dn_col, proj_own, proj_col, trow, recip, rs, params):
     tokens, half = hid.shape
     chan = out.shape[1]
     size_f = tokens // 4
@@ -1076,17 +1197,17 @@
             part(tail + 2 * size),
             part(tail + 2 * size + half),
             whole((tail, chan)),
+            whole(state.shape),
             blk(half),
             blk(half),
             blk(half),
             blk(half),
             blk(half),
             blk(half),
-            whole(sel.shape),
             row(16),
             row(8),
             row(8),
-            whole((8, half)),
+            whole((half,)),
         ],
         out_specs=[blk(half), blk(half), streamed(*big), streamed(*big)]
         + [whole(shape) for shape in small]
@@ -1105,22 +1226,18 @@
         out,
         out,
         out,
+        state,
         hid,
         cot,
         dn_sum,
         dn_col,
         proj_own,
         proj_col,
-        sel,
         trow,
         recip,
         rs,
-        gains,
+        params,
     )
-
-
-def swap(x, axis):
-    return lax.ppermute(x, axis, SWAP)
 
 
 def body(
@@ -1144,80 +1261,45 @@
     tokens, half = hidden.shape
     width = 2 * half
     chan = gated_gain.shape[0]
-    inner_width = 4 * chan
     heads = decay_log.shape[0]
-    r = lax.axis_index("row")
     dp = lax.axis_size("dp")
     seq_len = min(LEN, tokens)
 
-    def cut(x, start, size, axis):
-        return lax.dynamic_slice_in_dim(x, start * size, size, axis)
-
-    def packed(side):
-        return jnp.concatenate(
-            [
-                cut(gate_proj, side, chan, 1),
-                cut(value_proj, side, chan, 1),
-                state_proj,
-                jnp.pad(cut(step_proj, side, heads, 1), ((0, 0), (0, 128 - heads))),
-            ],
-            axis=1,
-        )
-
-    w_own = packed(r)
-    w_rec = swap(packed(1 - r), "row")
-    hid_rec = swap(hidden, "row")
-    cot_rec = swap(cotangent, "row")
-    wo_own = cut(output_proj, r, chan, 0)
-    wo_part = cut(output_proj, 1 - r, chan, 0)
-    wo_rec = swap(wo_part, "row")
-    gain_f = gated_gain.astype(F32)
-    gain_rec = swap(input_gain, "row")
-    gains = jnp.concatenate([input_gain[None], gain_rec[None], jnp.zeros((6, half), F32)], axis=0)
-
-    skip_lane = jnp.repeat(skip_gain, chan // heads)
-    vtap = jnp.concatenate(
-        [value_filter, value_shift[None], skip_lane[None], gain_f[None], jnp.zeros((1, chan), F32)], axis=0
-    )
-    stap = jnp.concatenate([shared_kernel, shared_offset[None], jnp.zeros((3, 256), F32)], axis=0)
-    pad_h = (0, 8 - heads)
-    head_par = jnp.concatenate([jnp.pad(step_bias, pad_h), jnp.pad(-jnp.exp(decay_log), pad_h)])
-    head_par = jnp.broadcast_to(head_par[:, None], (16, 128))
-
-    lane_head = jnp.arange(chan) // (chan // heads)
-    sel = (jnp.arange(16)[:, None] == lane_head[None, :]).astype(BF16)
-    out, proj_own, proj_col, dn_sum, dn_col, trow, rs, recip = layer(
+    out, proj_own, proj_col, dn_sum, dn_col, trow, rs, recip, g_state = layer(
         seq_len,
         dp,
         hidden,
-        hid_rec,
         cotangent,
-        cot_rec,
-        gains,
-        w_own,
-        w_rec,
-        vtap,
-        stap,
-        head_par,
-        wo_own,
-        wo_rec,
-        sel,
+        gate_proj,
+        value_proj,
+        state_proj,
+        output_proj,
+        step_proj.T,
+        value_filter,
+        value_shift,
+        shared_kernel,
+        shared_offset,
+        decay_log,
+        step_bias,
+        skip_gain,
+        input_gain,
+        gated_gain,
     )
     outs = finish(
         big_rows(dp, width),
         heads,
         out,
+        g_state,
         hidden,
         cotangent,
         dn_sum,
         dn_col,
         proj_own,
         proj_col,
-        sel,
         trow,
         recip,
         rs,
-        gains,
+        input_gain,
     )
     return tuple(outs[0:4]) + (outs[4].T,) + tuple(outs[5:])
 

time: 146 us -> 136 us (0.932)
  local copies, waits for them, and re-layouts: 5.74 us -> 0 us
  other arithmetic: 3.08 us -> 0 us
  starting transfers between devices: 1.58 us -> 0 us
    dynamic_slice x3 -> x0, local copies, waits for them, and re-layouts: 2.79 us -> none  [cut(): return lax.dynamic_slice_in_dim(x, start * size, size, axis)]
    concatenate x4 -> x0, other arithmetic: 2.48 us -> none  [the longest x1 1.07 us: packed(): jnp.concatenate([cut(gate_proj, side, chan, 1), cut(value_proj, side, cha...]
    pallas_call x1, Pallas kernels: 125 us -> 126 us  [layer(): pl.pallas_call(functools.partial(layer_kernel, seq_len, dp, 4 * chan), in...]
    ppermute x5 -> x0, starting transfers between devices: 1.58 us -> none  [swap(): return lax.ppermute(x, axis, SWAP)]
  transfers between devices with their start and end apart: 5 -> 0, of which waited for: 1 -> 0; matrix products, arithmetic and copies ran while one was open for 5% -> 0% of each run, Pallas kernels for 0% -> 0%
where the time goes in v7:
time: 136 us
  Pallas kernels  135 us (99%)
    pallas_call x1, Pallas kernels, layer(): pl.pallas_call(functools.partial(layer_kernel, seq_len, dp, 4 * chan), in...  126 us
    pallas_call x1, Pallas kernels, finish(): pl.pallas_call(functools.partial(finish_kernel, 2 * half), grid=(grid,),...  9.22 us

profile of v7, /device:TPU:0, one launch (start us, length us, event | category | flops | bytes accessed | tf_op | source)
XLA Modules:
  0.0 136.3 jit_solution(1555490364917216380)
XLA Ops:
  0.7 126.3 %layer.1 = (bf16[2560,384]{1,0:T(8,128)(2,1)}, bf16[2048,384]{1,0:T(8,128)(2,1)}, bf16[2048,384]{1,0:T(8,128)(2,1)}, bf16[2048,384]{1,0:T(8,128)(2,1)}, bf16[204...) custom-call(bf16[2048,384]{1,0:T(8,128)(2,1)} %hid.1, ...), custom_call_target="tpu_custom_call" | custom-call | tf_op jit(solution)/shard_map/layer/pallas_call | solution.py:984
  126.9 9.2 %finish.1 = (bf16[2048,384]{1,0:T(8,128)(2,1)}, f32[2048,384]{1,0:T(8,128)}, f32[384,768]{1,0:T(8,128)}, f32[384,768]{1,0:T(8,128)}, f32[12,384]{1,0:T(8,128)}, ...) custom-call(bf16[2560,384]{1,0:T(8,128)(2,1)} %get-tuple-element.41., ...), custom_call_target="tpu_custom_call" | custom-call | flops 20000000 | bytes 20000000 | tf_op jit(solution)/shard_map/finish/pallas_call | solution.py:1190

commit v8 on v7

--- a/solution.py
+++ b/solution.py
@@ -9,6 +9,7 @@
 
 LEN = 2048
 EPSILON = 1e-05
+LOG2E = 1.4426950408889634
 SUB = 128
 STEP = 256
 F32 = jnp.float32
@@ -133,7 +134,7 @@
     sg = gate * sigmoid(gate)
     for sub in range(STEP // SUB):
         lo, hi = sub * SUB, (sub + 1) * SUB
-        cum_r = row_scan(logd[:, lo:hi], upper)
+        cum_r = row_scan(logd[:, lo:hi] * LOG2E, upper)
         rows_out[8:16, lo:hi] = cum_r
         cols = jnp.transpose(jnp.concatenate([cum_r, steps[:, lo:hi]], axis=0))
         b_in = act[lo:hi, 0:128]
@@ -148,7 +149,7 @@
             weights = []
             for col, h in ((c0, 2 * p), (c1, 2 * p + 1)):
                 gap = jnp.where(causal, col - cum_r[h : h + 1, :], -1e30)
-                weights.append((scores * jnp.exp(gap)).astype(BF16))
+                weights.append((scores * jnp.exp2(gap)).astype(BF16))
             lane = iota((SUB, 128), 1)
             cum_e = jnp.where(lane < 64, c0, c1)
             step_e = spread(cols, 8 + 2 * p, SUB)
@@ -159,11 +160,11 @@
             held_bf = held.astype(BF16)
             state_out[lo:hi, pl0:pl1] = held_bf
             carried = dot(c_bf, held_bf)
-            y = inside + carried * jnp.exp(cum_e)
+            y = inside + carried * jnp.exp2(cum_e)
             y_out[lo:hi, pl0:pl1] = y
             last = cum_e[SUB - 1 : SUB, :]
-            tail = (xh * jnp.exp(last - cum_e)).astype(BF16)
-            state[:, pl0:pl1] = held * jnp.exp(last) + dot(b_t, tail)
+            tail = (xh * jnp.exp2(last - cum_e)).astype(BF16)
+            state[:, pl0:pl1] = held * jnp.exp2(last) + dot(b_t, tail)
             y = y + vtap[5:6, pl0:pl1] * xs
             mixed_out[lo:hi, pl0:pl1] = (y * sg[lo:hi, pl0:pl1]).astype(BF16)
     mix = mixed_out[...].astype(F32)
@@ -320,7 +321,7 @@
             decays = []
             for col, h in ((c0, 2 * p), (c1, 2 * p + 1)):
                 gap = jnp.where(causal_t, cum_r[h : h + 1, :] - col, -1e30)
-                decays.append(jnp.exp(gap))
+                decays.append(jnp.exp2(gap))
             weights = [(scores_t * d).astype(BF16) for d in decays]
             lane = iota((SUB, 128), 1)
             cum_e = jnp.where(lane < 64, c0, c1)
@@ -335,14 +336,14 @@
             d_pair = dot_nt(xh_bf, stack)
             d_scores = d_scores + decays[0] * d_pair[:, 0:128] + decays[1] * d_pair[:, 128:256]
             last = cum_e[SUB - 1 : SUB, :]
-            tail_e = jnp.exp(last - cum_e)
+            tail_e = jnp.exp2(last - cum_e)
             g = grad[:, pl0:pl1]
             g_bf = g.astype(BF16)
             outer = dot(b_bf, g_bf) * tail_e
             u = inner + outer
             dxbuf[lo:hi, pl0:pl1] = step_e * u + vtap[5:6, pl0:pl1] * dys
             db = db + dot_nt((xh * tail_e).astype(BF16), g_bf)
-            dya = (dys * jnp.exp(cum_e)).astype(BF16)
+            dya = (dys * jnp.exp2(cum_e)).astype(BF16)
             held = state_in[lo:hi, pl0:pl1]
             dc = dc + dot_nt(dya, held)
             sel_p = sel[:, pl0:pl1]
@@ -351,7 +352,7 @@
             )
             e_sum = e_sum + plain_sums(sel_p, xh * outer)
             f_sum = f_sum + plain_sums(sel_p, xs * u)
-            decay_row = jnp.exp(last)
+            decay_row = jnp.exp2(last)
             gh_row = decay_row * jnp.sum(g * held.astype(F32), axis=0, keepdims=True)
             gh = gh + jnp.sum(sel_f[:, pl0:pl1] * gh_row, axis=1, keepdims=True)
             grad[:, pl0:pl1] = g * decay_row + dot(c_t, dya)
@@ -465,14 +466,13 @@
     input_gain,
     gated_gain,
     sums_out,
-    proj_out,
+    result_out,
+    hidden_out,
     proj_col,
-    dn_out,
     dn_col,
+    state_out,
     trow,
     rs_out,
-    recip_out,
-    state_out,
     w_own,
     w_rec,
     wo_own,
@@ -534,6 +534,7 @@
     load_sem,
     feed_sem,
     weight_sem,
+    fetch_sem,
     save_sem,
     po_sem,
     dn_sem,
@@ -600,8 +601,12 @@
     rec_weights.append(remote(gains, gains_land, weight_sem.at[1, 5], weight_sem.at[2, 5], to_row))
 
     def save(n, i):
-        src, dst = ((proj_s, proj_out), (dn_sum, dn_out))[n]
+        src, dst = ((pre_value, result_out), (p_gate, hidden_out))[n]
         return pltpu.make_async_copy(src.at[span(i), :], dst.at[span(i), :], save_sem.at[n, i])
+
+    def fetch(n, i):
+        src, dst = ((proj_col, mixed), (dn_col, dy_s))[n]
+        return pltpu.make_async_copy(src.at[span(i), :], dst.at[span(i), :], fetch_sem.at[n, i])
 
     def pair_copy(sem, i):
         return remote(pair_send.at[span(i), :], pair_land.at[span(i), :], sem.at[0, i], sem.at[1, i], to_row)
@@ -665,7 +670,6 @@
         sums[i, 4:8, :] = dots[4:8]
         for n in range(3):
             sums_copy(n, i).start()
-        save(0, i).start()
 
     def take_sums(i):
         for n in range(3):
@@ -764,7 +768,6 @@
         wide_copy(0, proj_parts[1], 1).start()
     else:
         wide_copy(0, proj_parts[0], 0).start()
-    recip_out[...] = rows[16:24, :]
 
     @pl.loop(0, blocks)
     def _(i):
@@ -790,7 +793,6 @@
         pair_copy(dn_sem, i).wait()
         part = pair_own[span(i), :].astype(F32) + pair_land[span(i), :].astype(F32)
         dn_sum[span(i), :] = part.astype(BF16)
-        save(1, i).start()
 
     def over_width(valid, i):
         here = span(i)
@@ -850,23 +852,22 @@
                     for n in firsts[kind::2]:
                         end_level(n, level)
 
+    def sum8(ref, n):
+        return jnp.sum(ref[8 * n : 8 * n + 8, :], axis=0, keepdims=True)
+
+    misc_row = small_copy(swap_send.at[0], swap_land.at[0], 4, to_row)
+    value_row = small_copy(swap_send.at[1], swap_land.at[1], 5, to_row)
+    swap_send[1] = dot(normed_t[half:width, :], p_all[:, 0:chan]).astype(BF16)
+    value_row.start()
     over_width(True, 0)
     pair_copy(dn_sem, 0).start()
     if blocks > 1:
         take_dn(1)
-
-    def sum8(ref, n):
-        return jnp.sum(ref[8 * n : 8 * n + 8, :], axis=0, keepdims=True)
-
     small = jnp.concatenate([sum8(acc_s, n) for n in range(5)] + [jnp.zeros((3, 256), F32)], axis=0)
     norm_own, norm_rec = [
         jnp.concatenate([sum8(acc_n, n), jnp.zeros((1, 512 - half), F32)], axis=1) for n in (0, 1)
     ]
     pad6 = jnp.zeros((6, 256), F32)
-    misc_row = small_copy(swap_send.at[0], swap_land.at[0], 4, to_row)
-    value_row = small_copy(swap_send.at[1], swap_land.at[1], 5, to_row)
-    swap_send[1] = dot(normed_t[half:width, :], p_all[:, 0:chan]).astype(BF16)
-    value_row.start()
     extra_send[...] = jnp.concatenate([small, norm_rec[:, 0:256], norm_rec[:, 256:512], pad6], axis=0)
     extra_row = small_copy(extra_send, extra_land.at[0], 2, to_row)
     extra_row.start()
@@ -919,6 +920,39 @@
         + col_land[...].astype(F32)
     )
     start_level(misc, 0)
+
+    parts_of = (proj_parts if first_part < blocks else proj_parts[:1], dn_parts)
+
+    def arrive(n, index):
+        part = parts_of[n][index]
+        wide_copy(n, part, index).wait()
+
+        @pl.loop(part[0], part[1])
+        def _(i):
+            fetch(n, i).start()
+
+    def write_result(part):
+        @pl.loop(part[0], part[1])
+        def _(i):
+            here = span(i)
+            fetch(0, i).wait()
+            scale = jnp.transpose(trow[0:8, here])[:, 0:1]
+            proj = proj_s[here, :].astype(F32) + mixed[here, :].astype(F32)
+            pre_value[here, :] = (hid_own[here, :].astype(F32) + scale * proj).astype(BF16)
+            save(0, i).start()
+
+    def write_hidden(part):
+        @pl.loop(part[0], part[1])
+        def _(i):
+            here = span(i)
+            fetch(1, i).wait()
+            recip = rows[16:24, here]
+            pull = jnp.transpose(rs_out[:, here] * recip * recip / width)[:, 0:1]
+            d_normed = dn_sum[here, :].astype(F32) + dy_s[here, :].astype(F32)
+            grad_in = cot_own[here, :].astype(F32) + d_normed * gains[0:1, :]
+            p_gate[here, :] = (grad_in - pull * hid_own[here, :].astype(F32)).astype(BF16)
+            save(1, i).start()
+
     mine = pl.ds(pl.multiple_of(c * split, 16), split)
     last_col = small_copy(out.at[pl.ds(0, split), pl.ds(0, 256)], state_out.at[mine, :], 9, to_col)
     done = []
@@ -932,6 +966,16 @@
     for n in firsts[0::2]:
         save_chunk(n)
     for level in range(2 * bits):
+        if level == min(3, 2 * bits - 1):
+            for index in range(len(parts_of[0])):
+                arrive(0, index)
+            write_result((0, blocks))
+            rs_col.wait()
+            rs_out[...] = rs_out[...] + rs_land[1]
+        if level == min(5, 2 * bits - 1):
+            for index in range(len(dn_parts) - 1):
+                arrive(1, index)
+                write_hidden(dn_parts[index])
         if level == 0:
             for n in firsts[1::2]:
                 end_level(n, 2 * bits - 1)
@@ -947,17 +991,14 @@
                 save_chunk(n)
         if level < 2 * bits - 1:
             end_level(misc, level)
+    arrive(1, len(dn_parts) - 1)
+    write_hidden(dn_parts[-1])
     for copy in done:
         copy.wait()
     last_col.wait()
-    rs_col.wait()
-    rs_out[...] = rs_out[...] + rs_land[1]
     for i in range(blocks):
         for n in range(2):
             save(n, i).wait()
-    for n, parts in enumerate((proj_parts if first_part < blocks else proj_parts[:1], dn_parts)):
-        for index, part in enumerate(parts):
-            wide_copy(n, part, index).wait()
 
 
 def layer(seq_len, dp, hidden, cot, gate_w, value_w, state_w, out_w, *params):
@@ -984,19 +1025,18 @@
     return pl.pallas_call(
         functools.partial(layer_kernel, seq_len, dp, 4 * chan),
         in_specs=[hbm] * 6 + [vmem] * len(params),
-        out_specs=[hbm, hbm, hbm, hbm, hbm, vmem, vmem, vmem, vmem],
+        out_specs=[hbm] * 5 + [vmem],
         out_shape=[
             jax.ShapeDtypeStruct((total, chan), BF16),
             act(),
             act(),
             act(),
             act(),
-            jax.ShapeDtypeStruct((16, tokens), F32),
-            jax.ShapeDtypeStruct((8, tokens), F32),
-            jax.ShapeDtypeStruct((8, tokens), F32),
             jax.ShapeDtypeStruct((half, 256), BF16),
         ],
         scratch_shapes=[
+            room(16, tokens, dtype=F32),
+            room(8, tokens, dtype=F32),
             room(half, chan + wide),
             room(half, chan + wide),
             room(chan, half),
@@ -1061,6 +1101,7 @@
             flags(2, blocks),
             flags(2, blocks),
             flags(2, blocks),
+            flags(2, blocks),
             flags(2, 2, 3),
             flags(2, 3, blocks),
             flags(2, 10),
@@ -1076,7 +1117,6 @@
 
 
 def finish_kernel(
-    width,
     out_rows,
     gate_a,
     gate_b,
@@ -1084,16 +1124,8 @@
     value_b,
     misc,
     state,
-    hid,
-    cot,
-    dn_sum,
-    dn_col,
-    proj_own,
-    proj_col,
-    trow,
-    recip_in,
-    rs,
-    gains,
+    result_in,
+    hidden_in,
     result,
     hidden_grad,
     g_gate,
@@ -1111,14 +1143,10 @@
     g_gated,
     g_output,
 ):
-    half = hid.shape[1]
-    hid32 = hid[...].astype(F32)
-    recip = recip_in[...]
-    cols = jnp.transpose(jnp.concatenate([trow[0:8, :], rs[...] * recip * recip / width], axis=0))
-    proj = proj_own[...].astype(F32) + proj_col[...].astype(F32)
-    result[...] = (hid32 + cols[:, 0:1] * proj).astype(BF16)
-    d_normed = dn_sum[...].astype(F32) + dn_col[...].astype(F32)
-    hidden_grad[...] = cot[...].astype(F32) + d_normed * gains[...].reshape(1, half) - cols[:, 8:9] * hid32
+    half = result.shape[1]
+    result[...] = result_in[...]
+    hidden_grad[...] = hidden_in[...].astype(F32)
+
     @pl.when(pl.program_id(0) < half // 128)
     def _():
         g_output[...] = out_rows[...].astype(F32)
@@ -1148,17 +1176,14 @@
         g_skip[...] = skip[5, 0:heads]
 
 
-def finish(size, heads, out, state, hid, cot, dn_sum, dn_col, proj_own, proj_col, trow, recip, rs, params):
-    tokens, half = hid.shape
+def finish(size, heads, out, state, result, hidden_grad):
+    tokens, half = result.shape
     chan = out.shape[1]
     size_f = tokens // 4
     grid = 4
 
     def blk(cols):
         return pl.BlockSpec((size_f, cols), lambda i: (i, 0))
-
-    def row(count):
-        return pl.BlockSpec((count, size_f), lambda i: (0, i))
 
     def whole(shape):
         return pl.BlockSpec(shape, lambda i: (0,) * len(shape))
@@ -1188,7 +1213,7 @@
     big = (half, 2 * chan)
     shapes = [big, big] + small + [(2 * chan, half)]
     return pl.pallas_call(
-        functools.partial(finish_kernel, 2 * half),
+        finish_kernel,
         grid=(grid,),
         in_specs=[
             pl.BlockSpec((256, half), lambda i: (tail // 256 + jnp.minimum(i, parts - 1), 0)),
@@ -1200,14 +1225,6 @@
             whole(state.shape),
             blk(half),
             blk(half),
-            blk(half),
-            blk(half),
-            blk(half),
-            blk(half),
-            row(16),
-            row(8),
-            row(8),
-            whole((half,)),
         ],
         out_specs=[blk(half), blk(half), streamed(*big), streamed(*big)]
         + [whole(shape) for shape in small]
@@ -1227,16 +1244,8 @@
         out,
         out,
         state,
-        hid,
-        cot,
-        dn_sum,
-        dn_col,
-        proj_own,
-        proj_col,
-        trow,
-        recip,
-        rs,
-        params,
+        result,
+        hidden_grad,
     )
 
 
@@ -1265,7 +1274,7 @@
     dp = lax.axis_size("dp")
     seq_len = min(LEN, tokens)
 
-    out, proj_own, proj_col, dn_sum, dn_col, trow, rs, recip, g_state = layer(
+    out, result, hidden_grad, _, _, g_state = layer(
         seq_len,
         dp,
         hidden,
@@ -1285,22 +1294,7 @@
         input_gain,
         gated_gain,
     )
-    outs = finish(
-        big_rows(dp, width),
-        heads,
-        out,
-        g_state,
-        hidden,
-        cotangent,
-        dn_sum,
-        dn_col,
-        proj_own,
-        proj_col,
-        trow,
-        recip,
-        rs,
-        input_gain,
-    )
+    outs = finish(big_rows(dp, width), heads, out, g_state, result, hidden_grad)
     return tuple(outs[0:4]) + (outs[4].T,) + tuple(outs[5:])
 
 

time: 136 us -> 133 us (0.978)
  Pallas kernels: 135 us -> 132 us
    pallas_call x1, Pallas kernels: 9.22 us -> 6.96 us  [finish(): pl.pallas_call(finish_kernel, grid=(grid,), in_specs=[pl.BlockSpec((256,...]
    pallas_call x1, Pallas kernels: 126 us -> 125 us  [layer(): pl.pallas_call(functools.partial(layer_kernel, seq_len, dp, 4 * chan), in...]
where the time goes in v8:
time: 133 us
  Pallas kernels  132 us (99%)
    pallas_call x1, Pallas kernels, layer(): pl.pallas_call(functools.partial(layer_kernel, seq_len, dp, 4 * chan), in...  125 us
    pallas_call x1, Pallas kernels, finish(): pl.pallas_call(finish_kernel, grid=(grid,), in_specs=[pl.BlockSpec((256,...  6.96 us

profile of v8, /device:TPU:0, one launch (start us, length us, event | category | flops | bytes accessed | tf_op | source)
XLA Modules:
  0.0 132.6 jit_solution(16283263895029250171)
XLA Ops:
  0.7 124.8 %layer.1 = (bf16[2560,384]{1,0:T(8,128)(2,1)}, bf16[2048,384]{1,0:T(8,128)(2,1)}, bf16[2048,384]{1,0:T(8,128)(2,1)}, bf16[2048,384]{1,0:T(8,128)(2,1)}, bf16[204...) custom-call(bf16[2048,384]{1,0:T(8,128)(2,1)} %hid_hbm.1, bf16[2048,384]{1,0:T(8,128)(2,1)} %cot_hbm.1, ...), custom_call_target="tpu_custom_call" | custom-call | tf_op jit(solution)/shard_map/layer/pallas_call | solution.py:1025
  125.5 7.0 %finish.1 = (bf16[2048,384]{1,0:T(8,128)(2,1)}, f32[2048,384]{1,0:T(8,128)}, f32[384,768]{1,0:T(8,128)}, f32[384,768]{1,0:T(8,128)}, f32[12,384]{1,0:T(8,128)}, ...) custom-call(bf16[2560,384]{1,0:T(8,128)(2,1)} %get-tuple-element.36., ...), custom_call_target="tpu_custom_call" | custom-call | flops 20000000 | bytes 20000000 | tf_op jit(solution)/shard_map/finish/pallas_call | solution.py:1215

commit v9 on v8

--- a/solution.py
+++ b/solution.py
@@ -729,7 +729,7 @@
 
     first_part = max(1, blocks // 4)
     proj_parts = [(0, first_part), (first_part, blocks)]
-    half_way = blocks // 2
+    half_way = max(2, 5 * blocks // 8) if blocks > 2 else 0
     dn_parts = [(half_way, blocks), (0, half_way)] if half_way else [(0, blocks)]
 
     def wide_copy(n, part, index):

time: 133 us -> 130 us (0.977)
  Pallas kernels: 132 us -> 129 us
    pallas_call x1, Pallas kernels: 125 us -> 122 us  [layer(): pl.pallas_call(functools.partial(layer_kernel, seq_len, dp, 4 * chan), in...]
where the time goes in v9:
time: 130 us
  Pallas kernels  129 us (99%)
    pallas_call x1, Pallas kernels, layer(): pl.pallas_call(functools.partial(layer_kernel, seq_len, dp, 4 * chan), in...  122 us
    pallas_call x1, Pallas kernels, finish(): pl.pallas_call(finish_kernel, grid=(grid,), in_specs=[pl.BlockSpec((256,...  6.96 us

profile of v9, /device:TPU:0, one launch (start us, length us, event | category | flops | bytes accessed | tf_op | source)
XLA Modules:
  0.0 129.6 jit_solution(4368759933506427131)
XLA Ops:
  0.7 121.9 %layer.1 = (bf16[2560,384]{1,0:T(8,128)(2,1)}, bf16[2048,384]{1,0:T(8,128)(2,1)}, bf16[2048,384]{1,0:T(8,128)(2,1)}, bf16[2048,384]{1,0:T(8,128)(2,1)}, bf16[204...) custom-call(bf16[2048,384]{1,0:T(8,128)(2,1)} %hid_hbm.1, bf16[2048,384]{1,0:T(8,128)(2,1)} %cot_hbm.1, ...), custom_call_target="tpu_custom_call" | custom-call | tf_op jit(solution)/shard_map/layer/pallas_call | solution.py:1025
  122.5 7.0 %finish.1 = (bf16[2048,384]{1,0:T(8,128)(2,1)}, f32[2048,384]{1,0:T(8,128)}, f32[384,768]{1,0:T(8,128)}, f32[384,768]{1,0:T(8,128)}, f32[12,384]{1,0:T(8,128)}, ...) custom-call(bf16[2560,384]{1,0:T(8,128)(2,1)} %get-tuple-element.36., ...), custom_call_target="tpu_custom_call" | custom-call | flops 20000000 | bytes 20000000 | tf_op jit(solution)/shard_map/finish/pallas_call | solution.py:1215
